TPU v7x, 32 devices: a whole 2x2x4 slice. The times are simulated.
32 devices in a mesh: wide: 8 (over z, x), narrow: 4 (over y, core).
Axes of the slice: x: 2, y: 2, z: 4, core: 2. Of those that a mesh axis runs over, the one named last changes fastest.
Arguments:
- tokens: bfloat16 [3, 10240, 768], P(None, 'wide'), may hold values from -6 to 6
- image_lengths: int32 [3, 8, 8], P(None, 'wide'), may hold values from 1 to 196, 1280 in all within a row
- heads_weight: bfloat16 [768, 3, 768], P('wide', None, 'narrow'), may hold values from -0.21875 to 0.21875
- heads_bias: float32 [2, 768], P(None, 'narrow'), may hold values from -3 to 3
- out_weight: bfloat16 [768, 768], P('narrow', 'wide'), may hold values from -1.75 to 1.75
- out_bias: float32 [768], replicated, may hold values from -3 to 3
- up_weight: bfloat16 [768, 3072], P('wide', 'narrow'), may hold values from -0.21875 to 0.21875
- up_bias: float32 [3072], P('narrow'), may hold values from -3 to 3
- down_weight: bfloat16 [3072, 768], P('narrow', 'wide'), may hold values from -0.109375 to 0.109375
- down_bias: float32 [768], replicated, may hold values from -3 to 3
- first_gain: float32 [768], replicated, may hold values from 0.1 to 1.9
- first_shift: float32 [768], replicated, may hold values from -3 to 3
- second_gain: float32 [768], replicated, may hold values from 0.1 to 1.9
- second_shift: float32 [768], replicated, may hold values from -3 to 3
- mixer_scale: float32 [768], replicated, may hold values from 0.5 to 2
- feed_scale: float32 [768], replicated, may hold values from 0.5 to 2
- cotangent: bfloat16 [3, 10240, 768], P(None, 'wide'), may hold values from -6 to 6
Outputs:
- layer_out: bfloat16 [3, 10240, 768], P(None, 'wide')
- token_grad: bfloat16 [3, 10240, 768], P(None, ('wide', 'narrow'))
- heads_weight_grad: float32 [768, 3, 768], P(None, None, 'narrow')
- heads_bias_grad: float32 [2, 768], P(None, 'narrow')
- out_weight_grad: float32 [768, 768], P('narrow')
- out_bias_grad: float32 [768], replicated
- up_weight_grad: float32 [768, 3072], P(None, 'narrow')
- up_bias_grad: float32 [3072], P('narrow')
- down_weight_grad: float32 [3072, 768], P('narrow')
- down_bias_grad: float32 [768], replicated
- first_gain_grad: float32 [768], replicated
- first_shift_grad: float32 [768], replicated
- second_gain_grad: float32 [768], replicated
- second_shift_grad: float32 [768], replicated
- mixer_scale_grad: float32 [768], replicated
- feed_scale_grad: float32 [768], replicated
Inputs may be any that keep to these rules, and one draw needn't show every extreme that they name: `image_lengths`: each row of 8 numbers gives the lengths of the images packed in order into one micro-batch of one index of wide; they sum to 1280, and the largest is 196.
All inputs are finite; a program needn't handle non-finite values.
Results may differ from a plain program's by a relative error of at most 0.02.
Values may be sent and summed in bfloat16 or wider, within the bound.
No kernel may reach another device: no remote copies, remote signals or barrier semaphores. Data moves between devices by JAX's collectives and lax.ppermute only.
A program may use at most 256 MiB of HBM per device.

v0:
```python
import math
from functools import partial

import jax
import jax.numpy as jnp
from jax import lax
from jax.experimental import pallas as pl
from jax.experimental.pallas import tpu as pltpu
from jax.sharding import PartitionSpec as P

HEAD_DIM = 64
MOST = 196
epsilon = 1e-06
bf16 = jnp.bfloat16
f32 = jnp.float32
LOG2E = math.log2(math.e)
VMEM_LIMIT = 60 * 1024 * 1024
FEED_CHUNKS = 2
QUERIES = 160


def round_up(value, step):
    return -(-value // step) * step


def nt(left, right):
    return lax.dot_general(left, right, (((1,), (1,)), ((), ())), preferred_element_type=f32)


def tn(left, right):
    return lax.dot_general(left, right, (((0,), (0,)), ((), ())), preferred_element_type=f32)


def nn(left, right):
    return jnp.dot(left, right, preferred_element_type=f32)


def query_chunk(own):
    return QUERIES if own % QUERIES == 0 else own


def key_span(own, win):
    return min(win, query_chunk(own) + 2 * round_up(MOST - 1, 16))


def key_start(off, at, own, win):
    first = jnp.clip(off + at - round_up(MOST - 1, 16), 0, win - key_span(own, win))
    return pl.multiple_of(first, 16)


def params():
    return pltpu.CompilerParams(
        dimension_semantics=("arbitrary",), vmem_limit_bytes=VMEM_LIMIT
    )


def cost(flops, transcendentals, moved):
    return pl.CostEstimate(flops=1024, transcendentals=0, bytes_accessed=1024)


def full(shape):
    return pl.BlockSpec(shape, lambda *a: (0,) * len(shape))


def per_micro(shape):
    return pl.BlockSpec((1,) + shape, lambda m, *a: (m,) + (0,) * len(shape))


def stack_heads(rows, heads):
    lane = lax.broadcasted_iota(jnp.int32, rows.shape, 1) // HEAD_DIM
    zero = jnp.zeros_like(rows)
    return jnp.concatenate([jnp.where(lane == h, rows, zero) for h in range(heads)], axis=0)


def unstack_heads(stacked, heads):
    rows = stacked.shape[0] // heads
    lane = lax.broadcasted_iota(jnp.int32, (rows, stacked.shape[1]), 1) // HEAD_DIM
    out = stacked[:rows]
    for h in range(1, heads):
        out = jnp.where(lane == h, stacked[h * rows : (h + 1) * rows], out)
    return out


def attend_kernel(own, heads, count, first, off_ref, *refs):
    x_ref, b_ref, bnd_ref = refs[:3]
    w_refs = refs[3 : 3 + count]
    rest = refs[3 + count + (0 if first else 1) :]
    mixed_ref = rest[0]
    off = pl.multiple_of(off_ref[0], 16)
    win = x_ref.shape[1]
    cols = heads * HEAD_DIM
    xw = x_ref[0]
    xo = x_ref[0, pl.ds(off, own), :]
    size, span = query_chunk(own), key_span(own, win)
    place = lax.broadcasted_iota(jnp.int32, (span, heads * size), 0)
    mixed = None if first else refs[3 + count][0]
    for i in range(count):
        q_ref, k_ref, v_ref, o_ref, l_ref = rest[1 + 5 * i : 6 + 5 * i]
        w = w_refs[i]
        both = nn(xw, w[:, : 2 * cols])
        k = both[:, :cols].astype(bf16)
        v = (both[:, cols:] + b_ref[i, 1:2]).astype(bf16)
        q = (nn(xo, w[:, 2 * cols : 3 * cols]) + b_ref[i, 0:1]).astype(bf16)
        q_ref[0] = q
        k_ref[0] = k
        v_ref[0] = v
        parts = []
        for c in range(own // size):
            key_at = key_start(off, c * size, own, win)
            kc, vc = k_ref[0, pl.ds(key_at, span), :], v_ref[0, pl.ds(key_at, span), :]
            qs = stack_heads(q[c * size : (c + 1) * size], heads)
            keep = (place >= bnd_ref[0, c, 0:1] - key_at) & (place < bnd_ref[0, c, 1:2] - key_at)
            scores = nt(kc, qs) * (HEAD_DIM**-0.5 * LOG2E)
            scores = jnp.where(keep, scores, -1e30)
            top = jnp.max(scores, axis=0, keepdims=True)
            weights = jnp.exp2(scores - top)
            total = jnp.sum(weights, axis=0, keepdims=True)
            out = tn(vc, weights.astype(bf16)) * (1.0 / total)
            parts.append(unstack_heads(out.T, heads).astype(bf16))
            l_ref[0, c] = top + jnp.log2(total)
        out = jnp.concatenate(parts, axis=0)
        o_ref[0] = out
        part = nt(out, w[:, 3 * cols :])
        mixed = part if mixed is None else mixed + part
    mixed_ref[0] = mixed


def attend(off, x_win, pieces, bias, bounds, own, mixed):
    micro, win, width = x_win.shape
    cols = pieces[0].shape[1] // 4
    heads = cols // HEAD_DIM
    size = query_chunk(own)
    stacked = heads * size
    count = len(pieces)
    first = mixed is None
    shapes = [jax.ShapeDtypeStruct((micro, own, width), f32)]
    specs = [per_micro((own, width))]
    for _ in pieces:
        for rows in (own, win, win, own):
            shapes.append(jax.ShapeDtypeStruct((micro, rows, cols), bf16))
            specs.append(per_micro((rows, cols)))
        shapes.append(jax.ShapeDtypeStruct((micro, own // size, 1, stacked), f32))
        specs.append(per_micro((own // size, 1, stacked)))
    args = [x_win, bias, bounds] + list(pieces)
    in_specs = [per_micro((win, width)), full(bias.shape), per_micro((own // size, 2, stacked))]
    in_specs += [full((width, 4 * cols))] * count
    if not first:
        args.append(mixed)
        in_specs.append(per_micro((own, width)))
    result = pl.pallas_call(
        partial(attend_kernel, own, heads, count, first),
        grid_spec=pltpu.PrefetchScalarGridSpec(
            num_scalar_prefetch=1, grid=(micro,), in_specs=in_specs, out_specs=specs
        ),
        out_shape=shapes,
        compiler_params=params(),
        cost_estimate=cost(
            count * micro * 2 * (win * width * cols * 3 + 8 * stacked * win * HEAD_DIM),
            count * micro * stacked * win,
            micro * win * width * 2 + count * 4 * width * cols * 2,
        ),
        name="attend",
    )(off, *args)
    return result[0], [tuple(result[1 + 5 * i : 6 + 5 * i]) for i in range(count)]


def attend_back_kernel(own, heads, count, first, halo, off_ref, *refs):
    x_ref, mg_ref, bnd_ref = refs[:3]
    w_refs = refs[3 : 3 + count]
    saved = refs[3 + count : 3 + 6 * count]
    at = 3 + 6 * count
    in_ref = None if first else refs[at]
    rest = refs[at + (0 if first else 1) :]
    dn_ref = rest[0]
    halo_refs = rest[1 + 2 * count : 1 + 2 * count + (2 if halo else 0)]
    *acc_refs, dkv_ref = rest[1 + 2 * count + len(halo_refs) :]
    off = pl.multiple_of(off_ref[0], 16)
    win = x_ref.shape[1]
    cols = heads * HEAD_DIM
    scale = HEAD_DIM**-0.5
    step = pl.program_id(0)
    mg = mg_ref[0]
    xt = x_ref[0].T
    xot = x_ref[0, pl.ds(off, own), :].T
    mgt = mg.T
    size, span = query_chunk(own), key_span(own, win)
    place = lax.broadcasted_iota(jnp.int32, (span, heads * size), 0)
    dn = None if first else in_ref[0]
    dn_own = None
    for i in range(count):
        w = w_refs[i]
        q_ref, k_ref, v_ref, o_ref, l_ref = saved[5 * i : 5 * i + 5]
        dw_ref, db_ref = rest[1 + 2 * i : 3 + 2 * i]
        acc_ref = acc_refs[i]
        o = o_ref[0]
        g = nn(mg, w[:, 3 * cols :]).astype(bf16)
        dkv_ref[...] = jnp.zeros_like(dkv_ref)
        parts = []
        for c in range(own // size):
            key_at = key_start(off, c * size, own, win)
            keys = pl.ds(key_at, span)
            kc, vc = k_ref[0, keys, :], v_ref[0, keys, :]
            qs = stack_heads(q_ref[0, c * size : (c + 1) * size, :], heads)
            gs = stack_heads(g[c * size : (c + 1) * size], heads)
            keep = (place >= bnd_ref[0, c, 0:1] - key_at) & (place < bnd_ref[0, c, 1:2] - key_at)
            scores = nt(kc, qs) * (scale * LOG2E) - l_ref[0, c]
            weights = jnp.exp2(jnp.where(keep, scores, -1e30))
            weighed = weights * nt(vc, gs)
            delta = jnp.sum(weighed, axis=0, keepdims=True)
            slope = (weighed - weights * delta).astype(bf16)
            parts.append((unstack_heads(tn(kc, slope).T, heads) * scale).astype(bf16))
            dkv_ref[0, keys, :] += nn(slope, qs)
            dkv_ref[1, keys, :] += nn(weights.astype(bf16), gs)
        dq = jnp.concatenate(parts, axis=0)
        dkv = jnp.concatenate([dkv_ref[0] * scale, dkv_ref[1]], axis=1).astype(bf16)
        part = nt(dkv, w[:, : 2 * cols])
        dn = part if dn is None else dn + part
        part = nt(dq, w[:, 2 * cols : 3 * cols])
        dn_own = part if dn_own is None else dn_own + part
        left = nn(xt, dkv)
        right = jnp.concatenate([nn(xot, dq), nn(mgt, o)], axis=1)
        sums = jnp.concatenate(
            [
                jnp.sum(dkv.astype(f32), axis=0, keepdims=True),
                jnp.sum(jnp.concatenate([dq, dq], axis=1).astype(f32), axis=0, keepdims=True),
            ],
            axis=1,
        )

        @pl.when(step == 0)
        def _():
            acc_ref[:, : 2 * cols] = left
            acc_ref[:, 2 * cols :] = right
            db_ref[...] = sums

        @pl.when(step > 0)
        def _():
            acc_ref[:, : 2 * cols] += left
            acc_ref[:, 2 * cols :] += right
            db_ref[...] += sums

        @pl.when(step == pl.num_programs(0) - 1)
        def _():
            dw_ref[...] = acc_ref[...].astype(bf16)

    dn_ref[0] = dn
    dn_ref[0, pl.ds(off, own), :] += dn_own
    if halo:
        before = pl.multiple_of(jnp.maximum(off - halo, 0), 16)
        after = pl.multiple_of(jnp.minimum(off + own, win - halo), 16)
        halo_refs[0][0] = dn_ref[0, pl.ds(before, halo), :].astype(bf16)
        halo_refs[1][0] = dn_ref[0, pl.ds(after, halo), :].astype(bf16)


def attend_back(off, x_win, mixed_grad, pieces, saved, bounds, grad_in, halo):
    micro, win, width = x_win.shape
    own = mixed_grad.shape[1]
    cols = pieces[0].shape[1] // 4
    heads = cols // HEAD_DIM
    size = query_chunk(own)
    stacked = heads * size
    count = len(pieces)
    first = grad_in is None
    args = [x_win, mixed_grad, bounds] + list(pieces)
    in_specs = [per_micro((win, width)), per_micro((own, width)), per_micro((own // size, 2, stacked))]
    in_specs += [full((width, 4 * cols))] * count
    for one in saved:
        args += list(one)
        in_specs += [per_micro((rows, cols)) for rows in (own, win, win, own)]
        in_specs.append(per_micro((own // size, 1, stacked)))
    if not first:
        args.append(grad_in)
        in_specs.append(per_micro((win, width)))
    shapes = [jax.ShapeDtypeStruct((micro, win, width), f32)]
    specs = [per_micro((win, width))]
    for _ in pieces:
        shapes += [
            jax.ShapeDtypeStruct((width, 4 * cols), bf16),
            jax.ShapeDtypeStruct((1, 4 * cols), f32),
        ]
        specs += [full((width, 4 * cols)), full((1, 4 * cols))]
    for _ in range(2 if halo else 0):
        shapes.append(jax.ShapeDtypeStruct((micro, halo, width), bf16))
        specs.append(per_micro((halo, width)))
    result = pl.pallas_call(
        partial(attend_back_kernel, own, heads, count, first, halo),
        grid_spec=pltpu.PrefetchScalarGridSpec(
            num_scalar_prefetch=1,
            grid=(micro,),
            in_specs=in_specs,
            out_specs=specs,
            scratch_shapes=[pltpu.VMEM((width, 4 * cols), f32)] * count
            + [pltpu.VMEM((2, win, cols), f32)],
        ),
        out_shape=shapes,
        compiler_params=params(),
        cost_estimate=cost(
            count * micro * (40 * stacked * win * HEAD_DIM + 12 * win * width * cols),
            count * micro * stacked * win,
            micro * (10 * win) * width + count * 4 * width * cols * 4,
        ),
        name="attend_back",
    )(off, *args)
    return result[0], result[1 : 1 + 2 * count : 2], result[2 : 2 + 2 * count : 2], result[1 + 2 * count :]


def feed_kernel(chunks, count, first, *refs):
    x_ref, g_ref = refs[:2]
    w_refs = refs[2 : 2 + count]
    b_refs = refs[2 + count : 2 + 2 * count]
    at = 2 + 2 * count
    if not first:
        fi_ref, ni_ref = refs[at : at + 2]
        at = at + 2
    f_ref, n_ref = refs[at : at + 2]
    outs = refs[at + 2 : at + 2 + 2 * count]
    act_ref, ug_ref, xt_ref, gt_ref = refs[at + 2 + 2 * count :]
    rows = x_ref.shape[0]
    step = rows // chunks
    xt_ref[...] = x_ref[...].T
    gt_ref[...] = g_ref[...].T
    for i in range(count):
        w_ref, b_ref = w_refs[i], b_refs[i]
        dw_ref, db_ref = outs[2 * i : 2 * i + 2]
        hidden = b_ref.shape[1]
        total = jnp.zeros((1, hidden), f32)
        for c in range(chunks):
            rows_at = pl.ds(c * step, step)
            upper = nn(x_ref[rows_at, :], w_ref[:, :hidden]) + b_ref[...]
            phi = 0.5 + 0.5 * lax.erf(upper * math.sqrt(0.5))
            active = (upper * phi).astype(bf16)
            bell = jnp.exp2(upper * upper * (-0.5 * LOG2E)) * (1.0 / math.sqrt(2.0 * math.pi))
            slope = phi + upper * bell
            grad = (nn(g_ref[rows_at, :], w_ref[:, hidden:]) * slope).astype(bf16)
            act_ref[rows_at, :] = active
            ug_ref[rows_at, :] = grad
            total = total + jnp.sum(grad.astype(f32), axis=0, keepdims=True)
            feed = nt(active, w_ref[:, hidden:])
            back = nt(grad, w_ref[:, :hidden])
            if i > 0:
                feed = feed + f_ref[rows_at, :]
                back = back + n_ref[rows_at, :]
            elif not first:
                feed = feed + fi_ref[rows_at, :]
                back = back + ni_ref[rows_at, :]
            f_ref[rows_at, :] = feed
            n_ref[rows_at, :] = back
        db_ref[...] = total
        dw_ref[:, :hidden] = nn(xt_ref[...], ug_ref[...]).astype(bf16)
        dw_ref[:, hidden:] = nn(gt_ref[...], act_ref[...]).astype(bf16)


def feed_part(x2, grad, pieces, biases, before):
    rows, width = x2.shape
    hidden = biases[0].shape[1]
    count = len(pieces)
    first = before is None
    args = [x2, grad] + list(pieces) + list(biases)
    aliases = {}
    if not first:
        aliases = {len(args): 0, len(args) + 1: 1}
        args += list(before)
    whole = pl.BlockSpec(memory_space=pltpu.VMEM)
    shapes = [jax.ShapeDtypeStruct((rows, width), f32)] * 2
    for _ in pieces:
        shapes += [
            jax.ShapeDtypeStruct((width, 2 * hidden), bf16),
            jax.ShapeDtypeStruct((1, hidden), f32),
        ]
    result = pl.pallas_call(
        partial(feed_kernel, FEED_CHUNKS, count, first),
        in_specs=[whole] * len(args),
        out_specs=[whole] * len(shapes),
        out_shape=shapes,
        scratch_shapes=[
            pltpu.VMEM((rows, hidden), bf16),
            pltpu.VMEM((rows, hidden), bf16),
            pltpu.VMEM((width, rows), bf16),
            pltpu.VMEM((width, rows), bf16),
        ],
        input_output_aliases=aliases,
        compiler_params=pltpu.CompilerParams(vmem_limit_bytes=VMEM_LIMIT),
        cost_estimate=cost(
            count * 12 * rows * width * hidden,
            count * 2 * rows * hidden,
            16 * rows * width + count * 8 * width * hidden,
        ),
        name="feed_part",
    )(*args)
    return tuple(result[:2]), list(result[2::2]), list(result[3::2])


def norm_parts(values_in):
    center = jnp.mean(values_in, axis=-1, keepdims=True)
    shifted = values_in - center
    inverse = lax.rsqrt(jnp.mean(shifted * shifted, axis=-1, keepdims=True) + epsilon)
    return (shifted * inverse, inverse)


def norm_back(grad_in, unit_rows, inverse, gain_row):
    scaled = grad_in * gain_row
    return inverse * (
        scaled
        - jnp.mean(scaled, axis=-1, keepdims=True)
        - unit_rows * jnp.mean(scaled * unit_rows, axis=-1, keepdims=True)
    )


VECTORS = (
    "out_bias", "down_bias", "first_gain", "first_shift", "second_gain", "second_shift",
    "mixer_scale", "feed_scale",
)


def row(vec_ref, name):
    at = VECTORS.index(name)
    return vec_ref[at : at + 1]


def own_rows(shape):
    return pl.BlockSpec((1,) + shape, lambda m, place: (m, place[0]) + (0,) * (len(shape) - 1))


def rows_call(kernel, name, place, args, specs, shapes, out_specs):
    micro = args[0].shape[0]
    return pl.pallas_call(
        kernel,
        grid_spec=pltpu.PrefetchScalarGridSpec(
            num_scalar_prefetch=1, grid=(micro,), in_specs=specs, out_specs=out_specs
        ),
        out_shape=shapes,
        compiler_params=params(),
        cost_estimate=cost(0, 0, 0),
        name=name,
    )(place, *args)


def first_norm_kernel(place_ref, x_ref, c_ref, vec_ref, n_ref, g_ref):
    start = pl.multiple_of(place_ref[1], 16)
    win = n_ref.shape[1]
    unit = norm_parts(x_ref[0, pl.ds(start, win), :].astype(f32))[0]
    n_ref[0] = (unit * row(vec_ref, "first_gain") + row(vec_ref, "first_shift")).astype(bf16)
    g_ref[0] = (row(vec_ref, "feed_scale") * c_ref[0].astype(f32)).astype(bf16)


def second_norm_kernel(place_ref, mixed_ref, x_ref, vec_ref, m_ref, n_ref):
    branch = mixed_ref[0] + row(vec_ref, "out_bias")
    middle = x_ref[0].astype(f32) + row(vec_ref, "mixer_scale") * branch
    m_ref[0] = middle
    unit = norm_parts(middle)[0]
    n_ref[0] = (unit * row(vec_ref, "second_gain") + row(vec_ref, "second_shift")).astype(bf16)


def column_sums(sum_ref, rows_in):
    total = jnp.concatenate([jnp.sum(r, axis=0, keepdims=True) for r in rows_in], axis=0)

    @pl.when(pl.program_id(0) == 0)
    def _():
        sum_ref[...] = total

    @pl.when(pl.program_id(0) > 0)
    def _():
        sum_ref[...] += total


def second_back_kernel(
    place_ref, feed_ref, back_ref, m_ref, mixed_ref, c_ref, vec_ref, l_ref, mg_ref, low_ref, sum_ref
):
    middle, back, grad = m_ref[0], back_ref[0], c_ref[0].astype(f32)
    feed_scale = row(vec_ref, "feed_scale")
    branch = feed_ref[0] + row(vec_ref, "down_bias")
    l_ref[0] = (middle + feed_scale * branch).astype(bf16)
    unit, inverse = norm_parts(middle)
    middle_grad = grad + norm_back(back, unit, inverse, row(vec_ref, "second_gain"))
    mg_ref[0] = middle_grad
    low_ref[0] = (row(vec_ref, "mixer_scale") * middle_grad).astype(bf16)
    mixer = mixed_ref[0] + row(vec_ref, "out_bias")
    zero = jnp.zeros_like(grad[:8])
    column_sums(
        sum_ref,
        [middle_grad, grad, zero, zero, back * unit, back, middle_grad * mixer, grad * branch],
    )


def first_back_kernel(
    place_ref, win_ref, left_ref, right_ref, mg_ref, x_ref, vec_ref, t_ref, sum_ref
):
    own, halo = mg_ref.shape[1], left_ref.shape[1]
    off = pl.multiple_of(place_ref[2], 16)
    gap = jnp.zeros((own - halo, left_ref.shape[2]), f32)
    grad = win_ref[0, pl.ds(off, own), :]
    grad = grad + jnp.concatenate([left_ref[0].astype(f32), gap], axis=0)
    grad = grad + jnp.concatenate([gap, right_ref[0].astype(f32)], axis=0)
    unit, inverse = norm_parts(x_ref[0].astype(f32))
    t_ref[0] = (
        mg_ref[0] + norm_back(grad, unit, inverse, row(vec_ref, "first_gain"))
    ).astype(bf16)
    zero = jnp.zeros_like(grad[:8])
    column_sums(sum_ref, [zero, zero, grad * unit, grad, zero, zero, zero, zero])


def swap(values_in, axis, bit):
    size = lax.axis_size(axis)
    return lax.ppermute(values_in, axis, [(i, i ^ bit) for i in range(size)])


def shift(values_in, axis, step):
    size = lax.axis_size(axis)
    pairs = [(i, i + step) for i in range(size) if 0 <= i + step < size]
    return lax.ppermute(values_in, axis, pairs)


def wide_bits(size):
    bits = []
    bit = size // 2
    while bit:
        bits.append(bit)
        bit //= 2
    return bits


def bit_of(axis, bit):
    return (lax.axis_index(axis) & bit) != 0


def join(mine, other, is_high, axis):
    low = jnp.where(is_high, other, mine)
    high = jnp.where(is_high, mine, other)
    return jnp.stack([low, high], axis=axis)


def tie(*values_in):
    return lax.optimization_barrier(values_in)


def far_groups():
    bits = wide_bits(lax.axis_size("wide"))[:-1]
    return [bits[i : i + 2] for i in range(0, len(bits), 2)]


def offsets(bits):
    return [
        sum(bit for i, bit in enumerate(reversed(bits)) if (k >> i) & 1)
        for k in range(2 ** len(bits))
    ]


def exchange(values_in, bits):
    return [values_in] + [swap(values_in, "wide", o) for o in offsets(bits)[1:]]


def arrange(parts, bits, axis):
    if not bits:
        return jnp.expand_dims(parts[0], axis)
    half = len(parts) // 2
    low = arrange(parts[:half], bits[1:], axis)
    high = arrange(parts[half:], bits[1:], axis)
    is_high = bit_of("wide", bits[0])
    return jnp.concatenate(
        [jnp.where(is_high, high, low), jnp.where(is_high, low, high)], axis=axis
    )


def arrange_blocks(parts, bits):
    return arrange(parts, bits, 1).reshape((-1,) + parts[0].shape[1:])


def last_bit():
    return wide_bits(lax.axis_size("wide"))[-1]


def gather_narrow(piece):
    far = swap(piece, "narrow", 2)
    return [piece, swap(piece, "narrow", 1), far, swap(far, "narrow", 1)]


def add_low(*parts):
    total = parts[0].astype(f32)
    for part in parts[1:]:
        total = total + part.astype(f32)
    return total.astype(bf16)


def cut(values_in, axis, bits):
    count = 2 ** len(bits)
    size = values_in.shape[0] // count
    at = lax.axis_index(axis)
    places = []
    for o in offsets(bits):
        other = at ^ o
        place = 0
        for bit in bits:
            place = 2 * place + ((other & bit) != 0).astype(jnp.int32)
        places.append(place)
    return [lax.dynamic_slice_in_dim(values_in, p * size, size, 0) for p in places]


def send_cut(parts, bits):
    return [swap(part, "wide", o) for part, o in zip(parts[1:], offsets(bits)[1:])]


def reduce_far(part):
    for bits in far_groups():
        parts = cut(part, "wide", bits)
        part = add_low(parts[0], *send_cut(parts, bits))
    return part


def spread_far(part):
    for bits in reversed(far_groups()):
        part = arrange(exchange(part, bits), bits, 0).reshape((-1,) + part.shape[1:])
    return part


def reduce_last(part):
    parts = cut(part, "wide", [last_bit()])
    return add_low(parts[0], *send_cut(parts, [last_bit()]))


def spread_last(part):
    bits = [last_bit()]
    return arrange(exchange(part, bits), bits, 0).reshape((-1,) + part.shape[1:])


def tree_sum(parts):
    while len(parts) > 1:
        parts = [parts[i] + parts[i + 1] for i in range(0, len(parts), 2)]
    return parts[0]


def reduce_everywhere(values_in):
    for bits in far_groups() + [[last_bit()]]:
        values_in = tree_sum(exchange(values_in, bits))
    return tree_sum([values_in] + [swap(values_in, "narrow", o) for o in (1, 2, 3)])


def body(
    tokens, image_lengths, heads_weight, heads_bias, out_weight, out_bias, up_weight, up_bias,
    down_weight, down_bias, first_gain, first_shift, second_gain, second_shift, mixer_scale,
    feed_scale, cotangent,
):
    micro, row_count, width = tokens.shape
    narrow_size = lax.axis_size("narrow")
    narrow_at = lax.axis_index("narrow")
    own = row_count // narrow_size
    cols = heads_weight.shape[2]
    heads = cols // HEAD_DIM
    rows = micro * own
    halo = round_up(MOST - 1, 16)
    window = min(row_count, round_up(own + 2 * halo, 128))
    lead = round_up((window - own) // 2, 16)
    start = jnp.clip(narrow_at * own - lead, 0, row_count - window)
    off = narrow_at * own - start
    offset = off.reshape(1).astype(jnp.int32)

    hidden = up_weight.shape[1]
    groups = far_groups()

    bias_pieces = gather_narrow(
        jnp.concatenate([heads_bias.reshape(-1), up_bias]).reshape(1, -1)
    )
    qv_biases = [heads_bias[None]]
    qv_biases += [b[:, : 2 * cols].reshape(1, 2, cols) for b in bias_pieces[1:]]
    up_biases = [up_bias.reshape(1, hidden)] + [b[:, 2 * cols :] for b in bias_pieces[1:]]
    heads_blocks = jnp.concatenate(
        [heads_weight[:, 1], heads_weight[:, 2], heads_weight[:, 0], out_weight.T], axis=1
    )[None]
    for bits in groups:
        heads_blocks = arrange_blocks(exchange(heads_blocks, bits), bits)
    feed_blocks = jnp.concatenate([up_weight, down_weight.T], axis=1)[None]
    heads_blocks, feed_blocks = tie(heads_blocks, feed_blocks)
    for bits in groups[:-1]:
        feed_blocks = arrange_blocks(exchange(feed_blocks, bits), bits)
    feed_parts = exchange(feed_blocks, groups[-1])
    last = [last_bit()]
    heads_all = arrange_blocks(exchange(heads_blocks, last), last)
    heads_own = heads_all.reshape(width, -1)

    ends = jnp.cumsum(image_lengths[:, 0], axis=1)
    places = narrow_at * own + jnp.arange(own, dtype=jnp.int32)
    passed = ends[:, :, None] <= places[None, None, :]
    first_key = jnp.max(jnp.where(passed, ends[:, :, None], 0), axis=1) - start
    last_key = jnp.min(jnp.where(passed, row_count, ends[:, :, None]), axis=1) - start
    bounds = jnp.stack([first_key, last_key], axis=1).astype(jnp.int32)
    size = query_chunk(own)
    bounds = bounds.reshape(micro, 2, own // size, size).transpose(0, 2, 1, 3)
    bounds = jnp.tile(bounds, (1, 1, 1, heads))

    place = jnp.stack([narrow_at, start, off]).astype(jnp.int32)
    vectors = jnp.stack(
        [out_bias, down_bias, first_gain, first_shift, second_gain, second_shift, mixer_scale,
         feed_scale]
    )
    own_spec, part_spec, vec_spec = own_rows((own, width)), per_micro((own, width)), full((8, width))
    low_rows = jax.ShapeDtypeStruct((micro, own, width), bf16)
    high_rows = jax.ShapeDtypeStruct((micro, own, width), f32)
    sum_rows = jax.ShapeDtypeStruct((8, width), f32)
    window_normed, feed_grad = rows_call(
        first_norm_kernel, "first_norm", place, [tokens, cotangent, vectors],
        [per_micro((row_count, width)), own_spec, vec_spec],
        [jax.ShapeDtypeStruct((micro, window, width), bf16), low_rows],
        [per_micro((window, width)), part_spec],
    )
    feed_grad = feed_grad.reshape(rows, width)

    def halves(blocks):
        half = blocks.shape[0] // 2
        return blocks[:half], blocks[half:]

    def attend_on(piece, at, before):
        return attend(offset, window_normed, [piece], qv_biases[at], bounds, own, before)

    heads_low, heads_high = halves(heads_all)
    window_normed, heads_low, *biases = tie(window_normed, heads_low, *qv_biases, *up_biases)
    qv_biases, up_biases = biases[:narrow_size], biases[narrow_size:]
    heads_near = swap(heads_own, "narrow", 1)
    far_low = swap(heads_low, "narrow", 2)
    mixed, saved0 = attend_on(heads_own, 0, None)
    mixed, far_low, *feed_parts = tie(mixed, far_low, *feed_parts)
    feed_low, feed_high = halves(arrange_blocks(feed_parts, groups[-1]))
    mixed, feed_low, feed_high, heads_high = tie(mixed, feed_low, feed_high, heads_high)
    far_high = swap(heads_high, "narrow", 2)
    low_other = exchange(feed_low, last)[1]
    mixed, saved1 = attend_on(heads_near, 1, mixed)
    mixed, far_high, low_other = tie(mixed, far_high, low_other)
    heads_far = jnp.concatenate([far_low, far_high], axis=0).reshape(width, -1)
    mixed, heads_far, feed_low, feed_high = tie(mixed, heads_far, feed_low, feed_high)
    heads_cross = swap(heads_far, "narrow", 1)
    high_other = exchange(feed_high, last)[1]
    feed_far_low = swap(feed_low, "narrow", 2)
    mixed, saved2 = attend_on(heads_far, 2, mixed)
    mixed, high_other, feed_far_low = tie(mixed, high_other, feed_far_low)

    def whole_feed(low, high, low_sent, high_sent):
        mine = jnp.concatenate([low, high], axis=0)
        other = jnp.concatenate([low_sent, high_sent], axis=0)
        return arrange_blocks([mine, other], last).reshape(width, -1)

    feed_own = whole_feed(feed_low, feed_high, low_other, high_other)
    mixed, feed_own, feed_high = tie(mixed, feed_own, feed_high)
    feed_near = swap(feed_own, "narrow", 1)
    feed_far_high = swap(feed_high, "narrow", 2)
    mixed, saved3 = attend_on(heads_cross, 3, mixed)
    mixed, feed_far_high = tie(mixed, feed_far_high)
    middle, second_normed = rows_call(
        second_norm_kernel, "second_norm", place, [mixed, tokens, vectors],
        [part_spec, own_spec, vec_spec], [high_rows, low_rows], [part_spec, part_spec],
    )
    second_normed = second_normed.reshape(rows, width)

    def feed_on(pieces, biases, before):
        return feed_part(second_normed, feed_grad, pieces, biases, before)

    second_normed, feed_far_low = tie(second_normed, feed_far_low)
    far_low_other = exchange(feed_far_low, last)[1]
    sums, (part0,), bias0 = feed_on([feed_own], up_biases[:1], None)
    *sums, far_low_other, feed_far_high = tie(*sums, far_low_other, feed_far_high)
    far_high_other = exchange(feed_far_high, last)[1]
    sums, (part1,), bias1 = feed_on([feed_near], up_biases[1:2], sums)
    *sums, far_high_other = tie(*sums, far_high_other)
    feed_far = whole_feed(feed_far_low, feed_far_high, far_low_other, far_high_other)
    *sums, feed_far, part1 = tie(*sums, feed_far, part1)
    feed_cross = swap(feed_far, "narrow", 1)
    given = swap(part1, "narrow", 1)
    sums, (part2,), bias2 = feed_on([feed_far], up_biases[2:3], sums)
    *sums, given = tie(*sums, given)
    near_keep, near_give = cut(add_low(part0, given), "wide", last)
    up_give, down_give = near_give[:, :hidden], near_give[:, hidden:]
    *sums, near_keep, up_give, down_give = tie(*sums, near_keep, up_give, down_give)
    up_sent = swap(up_give, "wide", last[0])
    sums, (part3,), bias3 = feed_on([feed_cross], up_biases[3:], sums)
    feed, second_normed_grad, up_sent, part3, down_give = tie(*sums, up_sent, part3, down_give)
    down_sent = swap(down_give, "wide", last[0])
    given = swap(part3, "narrow", 1)
    up_bias_parts = bias0 + bias1 + bias2 + bias3

    layer_own, middle_grad, mixed_grad, back_sums = rows_call(
        second_back_kernel, "second_back", place,
        [feed.reshape(micro, own, width), second_normed_grad.reshape(micro, own, width), middle,
         mixed, cotangent, vectors],
        [part_spec, part_spec, part_spec, part_spec, own_spec, vec_spec],
        [low_rows, high_rows, low_rows, sum_rows],
        [part_spec, part_spec, part_spec, vec_spec],
    )
    layer_far = swap(layer_own, "narrow", 2)
    layer_parts = [
        layer_own, swap(layer_own, "narrow", 1), layer_far, swap(layer_far, "narrow", 1)
    ]

    def back_on(pieces, saved, grad_in, halo):
        return attend_back(
            offset, window_normed, mixed_grad, pieces, saved, bounds, grad_in, halo
        )

    mixed_grad, down_sent, given = tie(mixed_grad, down_sent, given)
    near = add_low(near_keep, jnp.concatenate([up_sent, down_sent], axis=1))
    far_cut = cut(add_low(part2, given), "wide", last)
    mixed_grad, near, *far_cut = tie(mixed_grad, near, *far_cut)
    far_sent = send_cut(far_cut, last)
    window_grad, (heads3,), sums3, _ = back_on([heads_cross], saved3, None, 0)
    given3 = swap(heads3, "narrow", 1)
    window_grad, *far_sent = tie(window_grad, *far_sent)
    far = add_low(far_cut[0], *far_sent)
    window_grad, far = tie(window_grad, far)
    far_given = swap(far, "narrow", 2)
    window_grad, (heads2,), sums2, _ = back_on([heads_far], saved2, window_grad, 0)
    window_grad, far_given, given3 = tie(window_grad, far_given, given3)
    mine = add_low(near, far_given)
    for bits in groups[:-1]:
        parts = cut(mine, "wide", bits)
        mine = add_low(parts[0], *send_cut(parts, bits))
    mine_cut = cut(mine, "wide", groups[-1])
    heads_sum = add_low(heads2, given3)
    window_grad, heads_sum, *mine_cut = tie(window_grad, heads_sum, *mine_cut)
    mine_sent = send_cut(mine_cut, groups[-1])
    heads_given = swap(heads_sum, "narrow", 2)
    window_grad, (heads1,), sums1, _ = back_on([heads_near], saved1, window_grad, 0)
    given1 = swap(heads1, "narrow", 1)
    window_grad, heads_given, *mine_sent = tie(window_grad, heads_given, *mine_sent)
    mine = add_low(mine_cut[0], *mine_sent)
    window_grad, mine = tie(window_grad, mine)
    mine_all = exchange(mine, groups[-1])
    window_grad, (heads0,), sums0, halos = back_on([heads_own], saved0, window_grad, halo)
    window_grad, *mine_all = tie(window_grad, *mine_all)
    window_grad, *layer_parts = tie(window_grad, *layer_parts)
    y_high, core_high = bit_of("narrow", 2), bit_of("narrow", 1)
    layer_near = join(layer_parts[0], layer_parts[1], core_high, 1)
    layer_far = join(layer_parts[2], layer_parts[3], core_high, 1)
    layer_out = join(layer_near, layer_far, y_high, 1).reshape(micro, row_count, width)
    mine = arrange(mine_all, groups[-1], 0).reshape((-1,) + mine.shape[1:])
    for bits in reversed(groups[:-1]):
        mine = arrange(exchange(mine, bits), bits, 0).reshape((-1,) + mine.shape[1:])
    feed_total = spread_last(mine)
    heads_total = spread_last(
        spread_far(reduce_far(reduce_last(add_low(heads0, given1, heads_given))))
    )
    head_bias_parts = [
        jnp.concatenate([s[0, 2 * cols : 3 * cols], s[0, cols : 2 * cols]])
        for s in [*sums0, *sums1, *sums2, *sums3]
    ]

    from_left = shift(halos[1], "narrow", 1)
    from_right = shift(halos[0], "narrow", -1)
    token_grad, first_sums = rows_call(
        first_back_kernel, "first_back", place,
        [window_grad, from_left, from_right, middle_grad, tokens, vectors],
        [per_micro((window, width)), per_micro((halo, width)), per_micro((halo, width)), part_spec,
         own_spec, vec_spec],
        [low_rows, sum_rows], [part_spec, vec_spec],
    )
    outer = jnp.stack([mixer_scale, feed_scale] + [jnp.ones_like(out_bias)] * 6)
    sums = (back_sums + first_sums) * outer
    group_sums = jnp.stack(
        [jnp.concatenate([head_bias_parts[r], up_bias_parts[r][0]]) for r in range(narrow_size)]
    )
    group_sums = jnp.stack([group_sums[r ^ narrow_at] for r in range(narrow_size)])
    packed = jnp.concatenate([sums.reshape(-1), group_sums.reshape(-1)]).reshape(-1, 128)
    packed = reduce_everywhere(packed).reshape(-1)
    sums = packed[: 8 * width].reshape(8, width)
    group_sums = packed[8 * width :].reshape(narrow_size, -1)
    mine = lax.dynamic_slice_in_dim(group_sums, narrow_at, 1, 0)[0]

    heads_grad = jnp.stack(
        [heads_total[:, 2 * cols : 3 * cols], heads_total[:, :cols], heads_total[:, cols : 2 * cols]],
        axis=1,
    ).astype(f32)
    out_grad = heads_total[:, 3 * cols :].T.astype(f32)
    return (
        layer_out, token_grad, heads_grad, mine[: 2 * cols].reshape(2, cols), out_grad, sums[0],
        feed_total[:, :hidden].astype(f32), mine[2 * cols :],
        feed_total[:, hidden:].T.astype(f32), sums[1], sums[2],
        sums[3], sums[4], sums[5], sums[6], sums[7],
    )


def solution(mesh):
    return jax.shard_map(
        body,
        mesh=mesh,
        in_specs=(
            P(None, "wide", None),
            P(None, "wide", None),
            P("wide", None, "narrow"),
            P(None, "narrow"),
            P("narrow", "wide"),
            P(),
            P("wide", "narrow"),
            P("narrow"),
            P("narrow", "wide"),
            P(),
            P(),
            P(),
            P(),
            P(),
            P(),
            P(),
            P(None, "wide", None),
        ),
        out_specs=(
            P(None, "wide", None),
            P(None, ("wide", "narrow"), None),
            P(None, None, "narrow"),
            P(None, "narrow"),
            P("narrow", None),
            P(),
            P(None, "narrow"),
            P("narrow"),
            P("narrow", None),
            P(),
            P(),
            P(),
            P(),
            P(),
            P(),
            P(),
        ),
        check_vma=False,
    )
```

profile of v0, /device:TPU:0, one launch (start us, length us, event | category | flops | bytes accessed | tf_op | source)
XLA Modules:
  0.0 459.2 jit_solution(15820666476429060937)
XLA Ops:
  2.5 5.1 %collective-permute-start = (bf16[1,96,768]{2,1,0:T(8,128)(2,1)S(1)}, bf16[1,96,768]{2,1,0:T(8,128)(2,1)S(1)}, u32[]{:S(2)}, u32[]{:S(2)}) collective-permute-start(bf16[1,96,768]{2,1,0:T(8,128)(2,1)S(1)} %maximum_bitcast_fusion.2), channel_id=1, source_target_pairs={{0,24},{4,28},{8,16},{12,20},{16,8},{20,12},{24,0},{28,4},{1,25},{... | collective-permute-start | bytes 442376 | tf_op jit(solution)/shard_map/ppermute | solution.py:504
  10.1 2.4 collective-permute-done
  12.5 7.7 %collective-permute-done.1 = bf16[1,96,768]{2,1,0:T(8,128)(2,1)S(1)} collective-permute-done((bf16[1,96,768]{2,1,0:T(8,128)(2,1)S(1)}, bf16[1,96,768]{2,1,0:T(8,128)(2,1)S(1)}, u32[]{:S(2)}, u32[]{:S(2)}) %collective-permute-start.1) | collective-permute-done | bytes 147488 | tf_op jit(solution)/shard_map/ppermute | solution.py:504
  25.1 8.1 %first_norm.1 = (bf16[3,768,768]{2,1,0:T(8,128)(2,1)}, bf16[3,320,768]{2,1,0:T(8,128)(2,1)}) custom-call(s32[3]{0:T(128)} %pad_add_fusion.place_ref, bf16[3,1280,768]{2,1,0:T(8,128)(2,1)} %x_ref.5, bf16[3,1280,768]{2,1,0:T(8,128)(2,1)} %c_ref.3, f32[8,768]{1,0:T(8,128)} %stack.117.vec_ref), custom_call_target="tpu_custom_call" | custom-call | flops 1024 | bytes 1024 | tf_op jit(solution)/shard_map/first_norm/pallas_call | solution.py:426
  40.3 2.6 collective-permute-start.11
  45.8 11.3 %attend.4 = (f32[3,320,768]{2,1,0:T(8,128)}, bf16[3,320,192]{2,1,0:T(8,128)(2,1)}, bf16[3,768,192]{2,1,0:T(8,128)(2,1)}, bf16[3,768,192]{2,1,0:T(8,128)(2,1)}, b...) custom-call(s32[1]{0:T(128)} %bitcast.off_ref, bf16[3,768,768]{2,1,0:T(8,128)(2,1)} %get-tuple-element.182.refs_0_, ...), custom_call_target="tpu_custom_call" | custom-call | flops 1024 | bytes 1024 | tf_op jit(solution)/shard_map/attend/pallas_call | solution.py:150
  57.1 5.3 %collective-permute-done.10 = bf16[1,96,1536]{2,1,0:T(8,128)(2,1)S(1)} collective-permute-done((bf16[1,96,1536]{2,1,0:T(8,128)(2,1)S(1)}, bf16[1,96,1536]{2,1,0:T(8,128)(2,1)S(1)}, u32[]{:S(2)}, u32[]{:S(2)}) %collective-permute-start.10) | collective-permute-done | bytes 294944 | tf_op jit(solution)/shard_map/ppermute | solution.py:504
  69.8 11.7 %attend.5 = (f32[3,320,768]{2,1,0:T(8,128)}, bf16[3,320,192]{2,1,0:T(8,128)(2,1)}, bf16[3,768,192]{2,1,0:T(8,128)(2,1)}, bf16[3,768,192]{2,1,0:T(8,128)(2,1)}, b...) custom-call(s32[1]{0:T(128)} %bitcast.off_ref, bf16[3,768,768]{2,1,0:T(8,128)(2,1)} %get-tuple-element.182.refs_0_, ...), custom_call_target="tpu_custom_call" | custom-call | flops 1024 | bytes 1024 | tf_op jit(solution)/shard_map/attend/pallas_call | solution.py:150
  85.0 11.7 %attend.6 = (f32[3,320,768]{2,1,0:T(8,128)}, bf16[3,320,192]{2,1,0:T(8,128)(2,1)}, bf16[3,768,192]{2,1,0:T(8,128)(2,1)}, bf16[3,768,192]{2,1,0:T(8,128)(2,1)}, b...) custom-call(s32[1]{0:T(128)} %bitcast.off_ref, bf16[3,768,768]{2,1,0:T(8,128)(2,1)} %get-tuple-element.182.refs_0_, ...), custom_call_target="tpu_custom_call" | custom-call | flops 1024 | bytes 1024 | tf_op jit(solution)/shard_map/attend/pallas_call | solution.py:150
  100.7 22.4 %attend.7 = (f32[3,320,768]{2,1,0:T(8,128)}, bf16[3,320,192]{2,1,0:T(8,128)(2,1)}, bf16[3,768,192]{2,1,0:T(8,128)(2,1)}, bf16[3,768,192]{2,1,0:T(8,128)(2,1)}, b...) custom-call(s32[1]{0:T(128)} %bitcast.off_ref, bf16[3,768,768]{2,1,0:T(8,128)(2,1)} %get-tuple-element.182.refs_0_, ...), custom_call_target="tpu_custom_call" | custom-call | flops 1024 | bytes 1024 | tf_op jit(solution)/shard_map/attend/pallas_call | solution.py:150
  124.0 5.9 %second_norm.1 = (f32[3,320,768]{2,1,0:T(8,128)}, bf16[3,320,768]{2,1,0:T(8,128)(2,1)}) custom-call(s32[3]{0:T(128)} %pad_add_fusion.place_ref, f32[3,320,768]{2,1,0:T(8,128)} %get-tuple-element.214.mixed_ref, bf16[3,1280,768]{2,1,0:T(8,128)(2,1)} %x_ref.5, f32[8,768]{1,0:T(8,128)} %stack.117.vec_ref), custom_call_target="tpu_custom_call" | custom-call | flops 1024 | bytes 1024 | tf_op jit(solution)/shard_map/second_norm/pallas_call | solution.py:426
  130.6 11.5 %feed_part.4 = (f32[960,768]{1,0:T(8,128)}, f32[960,768]{1,0:T(8,128)}, bf16[768,1536]{1,0:T(8,128)(2,1)}, f32[1,768]{1,0:T(1,128)}) custom-call(bf16[960,768]{1,0:T(8,128)(2,1)} %bitcast.145, bf16[960,768]{1,0:T(8,128)(2,1)} %bitcast.141, bf16[768,1536]{1,0:T(8,128)(2,1)} %bitcast.156, f32[1,768]{1,0:T(1,128)} %reshape.810.refs_3_), custom_call_target="tpu_custom_call" | custom-call | flops 1024 | bytes 1024 | tf_op jit(solution)/shard_map/feed_part/pallas_call | solution.py:370
  142.2 2.8 collective-permute-done.19
  145.7 13.2 %feed_part.5 = (f32[960,768]{1,0:T(8,128)}, f32[960,768]{1,0:T(8,128)}, bf16[768,1536]{1,0:T(8,128)(2,1)}, f32[1,768]{1,0:T(1,128)}) custom-call(bf16[960,768]{1,0:T(8,128)(2,1)} %bitcast.146, bf16[960,768]{1,0:T(8,128)(2,1)} %bitcast.142, bf16[768,1536]{1,0:T(8,128)(2,1)} %collective-permute-done.18.refs_2_, ...), custom_call_target="tpu_custom_call", output_to_operand_aliasing={{0}: (4, {}), {1}: (5, {})} | custom-call | flops 1024 | bytes 1024 | tf_op jit(solution)/shard_map/feed_part/pallas_call | solution.py:370
  162.8 13.2 %feed_part.6 = (f32[960,768]{1,0:T(8,128)}, f32[960,768]{1,0:T(8,128)}, bf16[768,1536]{1,0:T(8,128)(2,1)}, f32[1,768]{1,0:T(1,128)}) custom-call(bf16[960,768]{1,0:T(8,128)(2,1)} %bitcast.147, bf16[960,768]{1,0:T(8,128)(2,1)} %bitcast.143, bf16[768,1536]{1,0:T(8,128)(2,1)} %bitcast.159, ...), custom_call_target="tpu_custom_call", output_to_operand_aliasing={{0}: (4, {}), {1}: (5, {})} | custom-call | flops 1024 | bytes 1024 | tf_op jit(solution)/shard_map/feed_part/pallas_call | solution.py:370
  176.0 3.0 add_convert_fusion.1
  181.1 13.4 %feed_part.7 = (f32[960,768]{1,0:T(8,128)}, f32[960,768]{1,0:T(8,128)}, bf16[768,1536]{1,0:T(8,128)(2,1)}, f32[1,768]{1,0:T(1,128)}) custom-call(bf16[960,768]{1,0:T(8,128)(2,1)} %bitcast.148, bf16[960,768]{1,0:T(8,128)(2,1)} %bitcast.144, bf16[768,1536]{1,0:T(8,128)(2,1)} %collective-permute-done.21.refs_2_, ...), custom_call_target="tpu_custom_call", output_to_operand_aliasing={{0}: (4, {}), {1}: (5, {})} | custom-call | flops 1024 | bytes 1024 | tf_op jit(solution)/shard_map/feed_part/pallas_call | solution.py:370
  195.9 10.6 %second_back.1 = (bf16[3,320,768]{2,1,0:T(8,128)(2,1)}, f32[3,320,768]{2,1,0:T(8,128)}, bf16[3,320,768]{2,1,0:T(8,128)(2,1)}, f32[8,768]{1,0:T(8,128)}) custom-call(s32[3]{0:T(128)} %pad_add_fusion.place_ref, f32[3,320,768]{2,1,0:T(8,128)} %bitcast.139, f32[3,320,768]{2,1,0:T(8,128)} %bitcast.140, f32[3,320,768]{2,1,0:T(8,128)} %get-tuple-element.257.m_ref, ...), custom_call_target="tpu_custom_call" | custom-call | flops 1024 | bytes 1024 | tf_op jit(solution)/shard_map/second_back/pallas_call | solution.py:426
  206.6 4.5 collective-permute-done.24
  211.1 2.3 add_convert_fusion
  217.0 21.3 %attend_back.4 = (f32[3,768,768]{2,1,0:T(8,128)}, bf16[768,768]{1,0:T(8,128)(2,1)}, f32[1,768]{1,0:T(1,128)}) custom-call(s32[1]{0:T(128)} %bitcast.off_ref, bf16[3,768,768]{2,1,0:T(8,128)(2,1)} %get-tuple-element.182.refs_0_, bf16[3,320,768]{2,1,0:T(8,128)(2,1)} %get-tuple-element.267.refs_1_, s32[3,2,2,480]{3,2,1,0:T(2,128)} %tile.10.refs_2_, ...), custom_call_target="tpu_custom_call" | custom-call | flops 1024 | bytes 1024 | tf_op jit(solution)/shard_map/attend_back/pallas_call | solution.py:285
  238.3 5.6 %collective-permute-done.26 = bf16[384,1536]{1,0:T(8,128)(2,1)} collective-permute-done((bf16[384,1536]{1,0:T(8,128)(2,1)}, bf16[384,1536]{1,0:T(8,128)(2,1)}, u32[]{:S(2)}, u32[]{:S(2)}) %collective-permute-start.26) | collective-permute-done | bytes 1179680 | tf_op jit(solution)/shard_map/ppermute | solution.py:504
  243.9 2.6 add_convert_fusion.5
  248.5 21.9 %attend_back.5 = (f32[3,768,768]{2,1,0:T(8,128)}, bf16[768,768]{1,0:T(8,128)(2,1)}, f32[1,768]{1,0:T(1,128)}) custom-call(s32[1]{0:T(128)} %bitcast.off_ref, bf16[3,768,768]{2,1,0:T(8,128)(2,1)} %get-tuple-element.182.refs_0_, bf16[3,320,768]{2,1,0:T(8,128)(2,1)} %get-tuple-element.267.refs_1_, s32[3,2,2,480]{3,2,1,0:T(2,128)} %tile.10.refs_2_, ...), custom_call_target="tpu_custom_call" | custom-call | flops 1024 | bytes 1024 | tf_op jit(solution)/shard_map/attend_back/pallas_call | solution.py:285
  270.4 5.1 %collective-permute-done.27 = bf16[384,1536]{1,0:T(8,128)(2,1)S(1)} collective-permute-done((bf16[384,1536]{1,0:T(8,128)(2,1)}, bf16[384,1536]{1,0:T(8,128)(2,1)S(1)}, u32[]{:S(2)}, u32[]{:S(2)}) %collective-permute-start.27) | collective-permute-done | bytes 1179680 | tf_op jit(solution)/shard_map/ppermute | solution.py:504
  282.9 7.3 %collective-permute-start.30 = (bf16[96,1536]{1,0:T(8,128)(2,1)}, bf16[96,1536]{1,0:T(8,128)(2,1)S(1)}, u32[]{:S(2)}, u32[]{:S(2)}) collective-permute-start(bf16[96,1536]{1,0:T(8,128)(2,1)} %get-tuple-element.305), channel_id=1, source_target_pairs={{0,8},{4,12},{8,0},{12,4},{16,24},{20,28},{24,16},{28,20},{1,9},{5... | collective-permute-start | bytes 884744 | tf_op jit(solution)/shard_map/ppermute | solution.py:504
  290.1 2.4 collective-permute-start.32
  294.1 22.5 %attend_back.6 = (f32[3,768,768]{2,1,0:T(8,128)}, bf16[768,768]{1,0:T(8,128)(2,1)}, f32[1,768]{1,0:T(1,128)}) custom-call(s32[1]{0:T(128)} %bitcast.off_ref, bf16[3,768,768]{2,1,0:T(8,128)(2,1)} %get-tuple-element.182.refs_0_, bf16[3,320,768]{2,1,0:T(8,128)(2,1)} %get-tuple-element.267.refs_1_, s32[3,2,2,480]{3,2,1,0:T(2,128)} %tile.10.refs_2_, ...), custom_call_target="tpu_custom_call" | custom-call | flops 1024 | bytes 1024 | tf_op jit(solution)/shard_map/attend_back/pallas_call | solution.py:285
  320.0 10.4 %collective-permute-done.29 = bf16[768,768]{1,0:T(8,128)(2,1)} collective-permute-done((bf16[768,768]{1,0:T(8,128)(2,1)S(1)}, bf16[768,768]{1,0:T(8,128)(2,1)}, u32[]{:S(2)}, u32[]{:S(2)}) %collective-permute-start.29) | collective-permute-done | bytes 1179680 | tf_op jit(solution)/shard_map/ppermute | solution.py:504
  331.6 7.5 %collective-permute-start.33 = (bf16[96,1536]{1,0:T(8,128)(2,1)S(1)}, bf16[96,1536]{1,0:T(8,128)(2,1)S(1)}, u32[]{:S(2)}, u32[]{:S(2)}) collective-permute-start(bf16[96,1536]{1,0:T(8,128)(2,1)S(1)} %add_convert_fusion.8), channel_id=1, source_target_pairs={{0,8},{4,12},{8,0},{12,4},{16,24},{20,28},{24,16},{28,20},{1,9},{5... | collective-permute-start | bytes 884744 | tf_op jit(solution)/shard_map/ppermute | solution.py:504
  339.1 22.4 %attend_back.7 = (f32[3,768,768]{2,1,0:T(8,128)}, bf16[768,768]{1,0:T(8,128)(2,1)}, f32[1,768]{1,0:T(1,128)}, bf16[3,208,768]{2,1,0:T(8,128)(2,1)}, bf16[3,208,768]{2,1,0:T(8,128)(2,1)}) custom-call(s32[1]{0:T(128)} %bitcast.off_ref, bf16[3,768,768]{2,1,0:T(8,128)(2,1)} %get-tuple-element.182.refs_0_, bf16[3,320,768]{2,1,0:T(8,128)(2,1)} %get-tuple-element.267.refs_1_, ...), custom_call_target="tpu_custom_call" | custom-call | flops 1024 | bytes 1024 | tf_op jit(solution)/shard_map/attend_back/pallas_call | solution.py:285
  362.5 2.5 collective-permute-start.35
  365.0 2.4 add_convert_fusion.2
  369.5 2.3 collective-permute-start.39
  375.7 2.0 select_bitcast_fusion.3
  380.0 8.5 %collective-permute-done.42 = bf16[384,768]{1,0:T(8,128)(2,1)S(1)} collective-permute-done((bf16[384,768]{1,0:T(8,128)(2,1)S(1)}, bf16[384,768]{1,0:T(8,128)(2,1)S(1)}, u32[]{:S(2)}, u32[]{:S(2)}) %collective-permute-start.42) | collective-permute-done | bytes 589856 | tf_op jit(solution)/shard_map/ppermute | solution.py:504
  388.7 3.4 collective-permute-start.43
  394.7 2.1 collective-permute-done.43
  398.5 6.3 %collective-permute-done.44 = bf16[96,768]{1,0:T(8,128)(2,1)S(1)} collective-permute-done((bf16[96,768]{1,0:T(8,128)(2,1)S(1)}, bf16[96,768]{1,0:T(8,128)(2,1)S(1)}, u32[]{:S(2)}, u32[]{:S(2)}) %collective-permute-start.44) | collective-permute-done | bytes 147488 | tf_op jit(solution)/shard_map/ppermute | solution.py:504
  404.9 2.2 collective-permute-start.48
  407.6 3.0 copy.60
  410.6 2.6 collective-permute-start.46
  413.4 8.3 %first_back.1 = (bf16[3,320,768]{2,1,0:T(8,128)(2,1)}, f32[8,768]{1,0:T(8,128)}) custom-call(s32[3]{0:T(128)} %pad_add_fusion.place_ref, f32[3,768,768]{2,1,0:T(8,128)} %get-tuple-element.322.win_ref, bf16[3,208,768]{2,1,0:T(8,128)(2,1)} %collective-permute-done.39.left_ref, bf16[3,208,768]{2,1,0:T(8,128)(2,1)} %collective-permute-done.40.right_ref, ...), custom_call_target="tpu_custom_call" | custom-call | flops 1024 | bytes 1024 | tf_op jit(solution)/shard_map/first_back/pallas_call | solution.py:426
  422.6 1.7 collective-permute-start.50
  427.1 2.6 collective-permute-done.51
  433.2 2.3 collective-permute-done.53
  444.4 1.8 copy.63
  447.8 6.5 %collective-permute-done.49 = bf16[384,768]{1,0:T(8,128)(2,1)} collective-permute-done((bf16[384,768]{1,0:T(8,128)(2,1)}, bf16[384,768]{1,0:T(8,128)(2,1)}, u32[]{:S(2)}, u32[]{:S(2)}) %collective-permute-start.49) | collective-permute-done | bytes 589856 | tf_op jit(solution)/shard_map/ppermute | solution.py:504
  (298 shorter events, 99.1 us)
Async XLA Ops:
  2.5 9.9 %collective-permute-start = (bf16[1,96,768]{2,1,0:T(8,128)(2,1)S(1)}, bf16[1,96,768]{2,1,0:T(8,128)(2,1)S(1)}, u32[]{:S(2)}, u32[]{:S(2)}) collective-permute-start(bf16[1,96,768]{2,1,0:T(8,128)(2,1)S(1)} %maximum_bitcast_fusion.2), channel_id=1, source_target_pairs={{0,24},{4,28},{8,16},{12,20},{16,8},{20,12},{24,0},{28,4},{1,25},{... | collective-permute-start | bytes 442376 | tf_op jit(solution)/shard_map/ppermute | solution.py:504
  7.7 12.5 %collective-permute-start.1 = (bf16[1,96,768]{2,1,0:T(8,128)(2,1)S(1)}, bf16[1,96,768]{2,1,0:T(8,128)(2,1)S(1)}, u32[]{:S(2)}, u32[]{:S(2)}) collective-permute-start(bf16[1,96,768]{2,1,0:T(8,128)(2,1)S(1)} %maximum_bitcast_fusion.2), channel_id=1, source_target_pairs={{0,16},{4,20},{8,24},{12,28},{16,0},{20,4},{24,8},{28,12},{1,17},{... | collective-permute-start | bytes 442376 | tf_op jit(solution)/shard_map/ppermute | solution.py:504
  7.7 12.5 %collective-permute-start.2 = (bf16[1,96,768]{2,1,0:T(8,128)(2,1)S(1)}, bf16[1,96,768]{2,1,0:T(8,128)(2,1)S(1)}, u32[]{:S(2)}, u32[]{:S(2)}) collective-permute-start(bf16[1,96,768]{2,1,0:T(8,128)(2,1)S(1)} %maximum_bitcast_fusion.2), channel_id=1, source_target_pairs={{0,8},{4,12},{8,0},{12,4},{16,24},{20,28},{24,16},{28,20},{1,9},{5... | collective-permute-start | bytes 442376 | tf_op jit(solution)/shard_map/ppermute | solution.py:504
  20.6 17.8 %collective-permute-start.3 = (bf16[4,96,768]{2,1,0:T(8,128)(2,1)S(1)}, bf16[4,96,768]{2,1,0:T(8,128)(2,1)S(1)}, u32[]{:S(2)}, u32[]{:S(2)}) collective-permute-start(bf16[4,96,768]{2,1,0:T(8,128)(2,1)S(1)} %maximum_bitcast_fusion), channel_id=1, source_target_pairs={{0,4},{4,0},{8,12},{12,8},{16,20},{20,16},{24,28},{28,24},{1,5},{5... | collective-permute-start | bytes 1769480 | tf_op jit(solution)/shard_map/ppermute | solution.py:504
  22.1 11.9 %collective-permute-start.5 = (f32[1,1152]{1,0:T(1,128)S(1)}, f32[1,1152]{1,0:T(1,128)S(1)}, u32[]{:S(2)}, u32[]{:S(2)}) collective-permute-start(f32[1,1152]{1,0:T(1,128)S(1)} %reshape.806), channel_id=1, source_target_pairs={{0,2},{1,3},{2,0},{3,1},{4,6},{5,7},{6,4},{7,5},{8,10},{9,11},{10,... | collective-permute-start | bytes 13832 | tf_op jit(solution)/shard_map/ppermute | solution.py:504
  23.7 10.9 %collective-permute-start.4 = (f32[1,1152]{1,0:T(1,128)S(1)}, f32[1,1152]{1,0:T(1,128)S(1)}, u32[]{:S(2)}, u32[]{:S(2)}) collective-permute-start(f32[1,1152]{1,0:T(1,128)S(1)} %reshape.806), channel_id=1, source_target_pairs={{0,1},{1,0},{2,3},{3,2},{4,5},{5,4},{6,7},{7,6},{8,9},{9,8},{10,11... | collective-permute-start | bytes 13832 | tf_op jit(solution)/shard_map/ppermute | solution.py:504
  39.6 24.3 %collective-permute-start.8 = (bf16[4,96,768]{2,1,0:T(8,128)(2,1)}, bf16[4,96,768]{2,1,0:T(8,128)(2,1)}, u32[]{:S(2)}, u32[]{:S(2)}) collective-permute-start(bf16[4,96,768]{2,1,0:T(8,128)(2,1)} %bitcast.22), channel_id=1, source_target_pairs={{0,2},{1,3},{2,0},{3,1},{4,6},{5,7},{6,4},{7,5},{8,10},{9,11},{10,... | collective-permute-start | bytes 1769480 | tf_op jit(solution)/shard_map/ppermute | solution.py:504
  40.2 22.2 %collective-permute-start.10 = (bf16[1,96,1536]{2,1,0:T(8,128)(2,1)S(1)}, bf16[1,96,1536]{2,1,0:T(8,128)(2,1)S(1)}, u32[]{:S(2)}, u32[]{:S(2)}) collective-permute-start(bf16[1,96,1536]{2,1,0:T(8,128)(2,1)S(1)} %maximum_bitcast_fusion.1), channel_id=1, source_target_pairs={{0,16},{4,20},{8,24},{12,28},{16,0},{20,4},{24,8},{28,12},{1,17},{... | collective-permute-start | bytes 884744 | tf_op jit(solution)/shard_map/ppermute | solution.py:504
  40.3 22.2 %collective-permute-start.11 = (bf16[1,96,1536]{2,1,0:T(8,128)(2,1)S(1)}, bf16[1,96,1536]{2,1,0:T(8,128)(2,1)}, u32[]{:S(2)}, u32[]{:S(2)}) collective-permute-start(bf16[1,96,1536]{2,1,0:T(8,128)(2,1)S(1)} %maximum_bitcast_fusion.1), channel_id=1, source_target_pairs={{0,24},{4,28},{8,16},{12,20},{16,8},{20,12},{24,0},{28,4},{1,25},{... | collective-permute-start | bytes 884744 | tf_op jit(solution)/shard_map/ppermute | solution.py:504
  42.8 21.0 %collective-permute-start.9 = (bf16[1,96,1536]{2,1,0:T(8,128)(2,1)S(1)}, bf16[1,96,1536]{2,1,0:T(8,128)(2,1)}, u32[]{:S(2)}, u32[]{:S(2)}) collective-permute-start(bf16[1,96,1536]{2,1,0:T(8,128)(2,1)S(1)} %maximum_bitcast_fusion.1), channel_id=1, source_target_pairs={{0,8},{4,12},{8,0},{12,4},{16,24},{20,28},{24,16},{28,20},{1,9},{5... | collective-permute-start | bytes 884744 | tf_op jit(solution)/shard_map/ppermute | solution.py:504
  44.8 24.1 %collective-permute-start.7 = (bf16[768,768]{1,0:T(8,128)(2,1)S(1)}, bf16[768,768]{1,0:T(8,128)(2,1)S(1)}, u32[]{:S(2)}, u32[]{:S(2)}) collective-permute-start(bf16[768,768]{1,0:T(8,128)(2,1)S(1)} %bitcast.149), channel_id=1, source_target_pairs={{0,1},{1,0},{2,3},{3,2},{4,5},{5,4},{6,7},{7,6},{8,9},{9,8},{10,11... | collective-permute-start | bytes 3538952 | tf_op jit(solution)/shard_map/ppermute | solution.py:504
  66.8 14.8 %collective-permute-start.12 = (bf16[4,96,768]{2,1,0:T(8,128)(2,1)}, bf16[4,96,768]{2,1,0:T(8,128)(2,1)}, u32[]{:S(2)}, u32[]{:S(2)}) collective-permute-start(bf16[4,96,768]{2,1,0:T(8,128)(2,1)} %bitcast.26), channel_id=1, source_target_pairs={{0,2},{1,3},{2,0},{3,1},{4,6},{5,7},{6,4},{7,5},{8,10},{9,11},{10,... | collective-permute-start | bytes 1769480 | tf_op jit(solution)/shard_map/ppermute | solution.py:504
  68.3 13.5 %collective-permute-start.13 = (bf16[2,96,1536]{2,1,0:T(8,128)(2,1)S(1)}, bf16[2,96,1536]{2,1,0:T(8,128)(2,1)S(1)}, u32[]{:S(2)}, u32[]{:S(2)}) collective-permute-start(bf16[2,96,1536]{2,1,0:T(8,128)(2,1)S(1)} %get-tuple-element.207), channel_id=1, source_target_pairs={{0,4},{4,0},{8,12},{12,8},{16,20},{20,16},{24,28},{28,24},{1,5},{5... | collective-permute-start | bytes 1769480 | tf_op jit(solution)/shard_map/ppermute | solution.py:504
  83.1 13.5 %collective-permute-start.15 = (bf16[2,96,1536]{2,1,0:T(8,128)(2,1)}, bf16[2,96,1536]{2,1,0:T(8,128)(2,1)S(1)}, u32[]{:S(2)}, u32[]{:S(2)}) collective-permute-start(bf16[2,96,1536]{2,1,0:T(8,128)(2,1)} %get-tuple-element.213), channel_id=1, source_target_pairs={{0,4},{4,0},{8,12},{12,8},{16,20},{20,16},{24,28},{28,24},{1,5},{5... | collective-permute-start | bytes 1769480 | tf_op jit(solution)/shard_map/ppermute | solution.py:504
  84.5 13.0 %collective-permute-start.16 = (bf16[2,96,1536]{2,1,0:T(8,128)(2,1)S(1)}, bf16[2,96,1536]{2,1,0:T(8,128)(2,1)S(1)}, u32[]{:S(2)}, u32[]{:S(2)}) collective-permute-start(bf16[2,96,1536]{2,1,0:T(8,128)(2,1)S(1)} %get-tuple-element.207), channel_id=1, source_target_pairs={{0,2},{1,3},{2,0},{3,1},{4,6},{5,7},{6,4},{7,5},{8,10},{9,11},{10,... | collective-permute-start | bytes 1769480 | tf_op jit(solution)/shard_map/ppermute | solution.py:504
  85.0 15.7 %collective-permute-start.14 = (bf16[768,768]{1,0:T(8,128)(2,1)S(1)}, bf16[768,768]{1,0:T(8,128)(2,1)}, u32[]{:S(2)}, u32[]{:S(2)}) collective-permute-start(bf16[768,768]{1,0:T(8,128)(2,1)S(1)} %bitcast.152), channel_id=1, source_target_pairs={{0,1},{1,0},{2,3},{3,2},{4,5},{5,4},{6,7},{7,6},{8,9},{9,8},{10,11... | collective-permute-start | bytes 3538952 | tf_op jit(solution)/shard_map/ppermute | solution.py:504
  99.3 46.4 %collective-permute-start.18 = (bf16[768,1536]{1,0:T(8,128)(2,1)S(1)}, bf16[768,1536]{1,0:T(8,128)(2,1)}, u32[]{:S(2)}, u32[]{:S(2)}) collective-permute-start(bf16[768,1536]{1,0:T(8,128)(2,1)S(1)} %bitcast.155), channel_id=1, source_target_pairs={{0,1},{1,0},{2,3},{3,2},{4,5},{5,4},{6,7},{7,6},{8,9},{9,8},{10,11... | collective-permute-start | bytes 7077896 | tf_op jit(solution)/shard_map/ppermute | solution.py:504
  99.4 23.7 %collective-permute-start.17 = (bf16[2,96,1536]{2,1,0:T(8,128)(2,1)}, bf16[2,96,1536]{2,1,0:T(8,128)(2,1)S(1)}, u32[]{:S(2)}, u32[]{:S(2)}) collective-permute-start(bf16[2,96,1536]{2,1,0:T(8,128)(2,1)} %get-tuple-element.213), channel_id=1, source_target_pairs={{0,2},{1,3},{2,0},{3,1},{4,6},{5,7},{6,4},{7,5},{8,10},{9,11},{10,... | collective-permute-start | bytes 1769480 | tf_op jit(solution)/shard_map/ppermute | solution.py:504
  129.9 15.1 %collective-permute-start.19 = (bf16[2,96,1536]{2,1,0:T(8,128)(2,1)S(1)}, bf16[2,96,1536]{2,1,0:T(8,128)(2,1)S(1)}, u32[]{:S(2)}, u32[]{:S(2)}) collective-permute-start(bf16[2,96,1536]{2,1,0:T(8,128)(2,1)S(1)} %copy-done.10), channel_id=1, source_target_pairs={{0,4},{4,0},{8,12},{12,8},{16,20},{20,16},{24,28},{28,24},{1,5},{5... | collective-permute-start | bytes 1769480 | tf_op jit(solution)/shard_map/ppermute | solution.py:504
  145.0 14.3 %collective-permute-start.20 = (bf16[2,96,1536]{2,1,0:T(8,128)(2,1)S(1)}, bf16[2,96,1536]{2,1,0:T(8,128)(2,1)}, u32[]{:S(2)}, u32[]{:S(2)}) collective-permute-start(bf16[2,96,1536]{2,1,0:T(8,128)(2,1)S(1)} %copy-done.12), channel_id=1, source_target_pairs={{0,4},{4,0},{8,12},{12,8},{16,20},{20,16},{24,28},{28,24},{1,5},{5... | collective-permute-start | bytes 1769480 | tf_op jit(solution)/shard_map/ppermute | solution.py:504
  161.4 14.6 %collective-permute-start.22 = (bf16[768,1536]{1,0:T(8,128)(2,1)}, bf16[768,1536]{1,0:T(8,128)(2,1)}, u32[]{:S(2)}, u32[]{:S(2)}) collective-permute-start(bf16[768,1536]{1,0:T(8,128)(2,1)} %get-tuple-element.243), channel_id=1, source_target_pairs={{0,1},{1,0},{2,3},{3,2},{4,5},{5,4},{6,7},{7,6},{8,9},{9,8},{10,11... | collective-permute-start | bytes 7077896 | tf_op jit(solution)/shard_map/ppermute | solution.py:504
  161.4 19.7 %collective-permute-start.21 = (bf16[768,1536]{1,0:T(8,128)(2,1)S(1)}, bf16[768,1536]{1,0:T(8,128)(2,1)}, u32[]{:S(2)}, u32[]{:S(2)}) collective-permute-start(bf16[768,1536]{1,0:T(8,128)(2,1)S(1)} %bitcast.158), channel_id=1, source_target_pairs={{0,1},{1,0},{2,3},{3,2},{4,5},{5,4},{6,7},{7,6},{8,9},{9,8},{10,11... | collective-permute-start | bytes 7077896 | tf_op jit(solution)/shard_map/ppermute | solution.py:504
  180.1 14.9 %collective-permute-start.23 = (bf16[384,768]{1,0:T(8,128)(2,1)}, bf16[384,768]{1,0:T(8,128)(2,1)}, u32[]{:S(2)}, u32[]{:S(2)}) collective-permute-start(bf16[384,768]{1,0:T(8,128)(2,1)} %get-tuple-element.252), channel_id=1, source_target_pairs={{0,4},{4,0},{8,12},{12,8},{16,20},{20,16},{24,28},{28,24},{1,5},{5... | collective-permute-start | bytes 1769480 | tf_op jit(solution)/shard_map/ppermute | solution.py:504
  195.0 16.1 %collective-permute-start.25 = (bf16[768,1536]{1,0:T(8,128)(2,1)}, bf16[768,1536]{1,0:T(8,128)(2,1)}, u32[]{:S(2)}, u32[]{:S(2)}) collective-permute-start(bf16[768,1536]{1,0:T(8,128)(2,1)} %get-tuple-element.260), channel_id=1, source_target_pairs={{0,1},{1,0},{2,3},{3,2},{4,5},{5,4},{6,7},{7,6},{8,9},{9,8},{10,11... | collective-permute-start | bytes 7077896 | tf_op jit(solution)/shard_map/ppermute | solution.py:504
  195.0 16.1 %collective-permute-start.24 = (bf16[384,768]{1,0:T(8,128)(2,1)}, bf16[384,768]{1,0:T(8,128)(2,1)}, u32[]{:S(2)}, u32[]{:S(2)}) collective-permute-start(bf16[384,768]{1,0:T(8,128)(2,1)} %get-tuple-element.259), channel_id=1, source_target_pairs={{0,4},{4,0},{8,12},{12,8},{16,20},{20,16},{24,28},{28,24},{1,5},{5... | collective-permute-start | bytes 1769480 | tf_op jit(solution)/shard_map/ppermute | solution.py:504
  216.0 27.9 %collective-permute-start.26 = (bf16[384,1536]{1,0:T(8,128)(2,1)}, bf16[384,1536]{1,0:T(8,128)(2,1)}, u32[]{:S(2)}, u32[]{:S(2)}) collective-permute-start(bf16[384,1536]{1,0:T(8,128)(2,1)} %get-tuple-element.289), channel_id=1, source_target_pairs={{0,4},{4,0},{8,12},{12,8},{16,20},{20,16},{24,28},{28,24},{1,5},{5... | collective-permute-start | bytes 3538952 | tf_op jit(solution)/shard_map/ppermute | solution.py:504
  238.3 32.1 %collective-permute-start.28 = (bf16[768,768]{1,0:T(8,128)(2,1)}, bf16[768,768]{1,0:T(8,128)(2,1)S(1)}, u32[]{:S(2)}, u32[]{:S(2)}) collective-permute-start(bf16[768,768]{1,0:T(8,128)(2,1)} %get-tuple-element.296), channel_id=1, source_target_pairs={{0,1},{1,0},{2,3},{3,2},{4,5},{5,4},{6,7},{7,6},{8,9},{9,8},{10,11... | collective-permute-start | bytes 3538952 | tf_op jit(solution)/shard_map/ppermute | solution.py:504
  246.5 29.0 %collective-permute-start.27 = (bf16[384,1536]{1,0:T(8,128)(2,1)}, bf16[384,1536]{1,0:T(8,128)(2,1)S(1)}, u32[]{:S(2)}, u32[]{:S(2)}) collective-permute-start(bf16[384,1536]{1,0:T(8,128)(2,1)} %add_convert_fusion.5), channel_id=1, source_target_pairs={{0,2},{1,3},{2,0},{3,1},{4,6},{5,7},{6,4},{7,5},{8,10},{9,11},{10,... | collective-permute-start | bytes 3538952 | tf_op jit(solution)/shard_map/ppermute | solution.py:504
  248.0 68.6 %collective-permute-start.37 = (bf16[3,320,768]{2,1,0:T(8,128)(2,1)}, bf16[3,320,768]{2,1,0:T(8,128)(2,1)}, u32[]{:S(2)}, u32[]{:S(2)}) collective-permute-start(bf16[3,320,768]{2,1,0:T(8,128)(2,1)} %get-tuple-element.321), channel_id=1, source_target_pairs={{0,2},{1,3},{2,0},{3,1},{4,6},{5,7},{6,4},{7,5},{8,10},{9,11},{10,... | collective-permute-start | bytes 4423688 | tf_op jit(solution)/shard_map/ppermute | solution.py:504
  277.8 52.5 %collective-permute-start.29 = (bf16[768,768]{1,0:T(8,128)(2,1)S(1)}, bf16[768,768]{1,0:T(8,128)(2,1)}, u32[]{:S(2)}, u32[]{:S(2)}) collective-permute-start(bf16[768,768]{1,0:T(8,128)(2,1)S(1)} %add_convert_fusion.4), channel_id=1, source_target_pairs={{0,2},{1,3},{2,0},{3,1},{4,6},{5,7},{6,4},{7,5},{8,10},{9,11},{10,... | collective-permute-start | bytes 3538952 | tf_op jit(solution)/shard_map/ppermute | solution.py:504
  282.9 36.5 %collective-permute-start.30 = (bf16[96,1536]{1,0:T(8,128)(2,1)}, bf16[96,1536]{1,0:T(8,128)(2,1)S(1)}, u32[]{:S(2)}, u32[]{:S(2)}) collective-permute-start(bf16[96,1536]{1,0:T(8,128)(2,1)} %get-tuple-element.305), channel_id=1, source_target_pairs={{0,8},{4,12},{8,0},{12,4},{16,24},{20,28},{24,16},{28,20},{1,9},{5... | collective-permute-start | bytes 884744 | tf_op jit(solution)/shard_map/ppermute | solution.py:504
  290.1 29.8 %collective-permute-start.31 = (bf16[96,1536]{1,0:T(8,128)(2,1)}, bf16[96,1536]{1,0:T(8,128)(2,1)S(1)}, u32[]{:S(2)}, u32[]{:S(2)}) collective-permute-start(bf16[96,1536]{1,0:T(8,128)(2,1)} %get-tuple-element.306), channel_id=1, source_target_pairs={{0,16},{4,20},{8,24},{12,28},{16,0},{20,4},{24,8},{28,12},{1,17},{... | collective-permute-start | bytes 884744 | tf_op jit(solution)/shard_map/ppermute | solution.py:504
  290.1 29.9 %collective-permute-start.32 = (bf16[96,1536]{1,0:T(8,128)(2,1)}, bf16[96,1536]{1,0:T(8,128)(2,1)}, u32[]{:S(2)}, u32[]{:S(2)}) collective-permute-start(bf16[96,1536]{1,0:T(8,128)(2,1)} %get-tuple-element.307), channel_id=1, source_target_pairs={{0,24},{4,28},{8,16},{12,20},{16,8},{20,12},{24,0},{28,4},{1,25},{... | collective-permute-start | bytes 884744 | tf_op jit(solution)/shard_map/ppermute | solution.py:504
  316.5 46.0 %collective-permute-start.41 = (bf16[768,768]{1,0:T(8,128)(2,1)}, bf16[768,768]{1,0:T(8,128)(2,1)}, u32[]{:S(2)}, u32[]{:S(2)}) collective-permute-start(bf16[768,768]{1,0:T(8,128)(2,1)} %get-tuple-element.328), channel_id=1, source_target_pairs={{0,1},{1,0},{2,3},{3,2},{4,5},{5,4},{6,7},{7,6},{8,9},{9,8},{10,11... | collective-permute-start | bytes 3538952 | tf_op jit(solution)/shard_map/ppermute | solution.py:504
  319.4 55.2 %collective-permute-start.36 = (bf16[3,320,768]{2,1,0:T(8,128)(2,1)S(1)}, bf16[3,320,768]{2,1,0:T(8,128)(2,1)}, u32[]{:S(2)}, u32[]{:S(2)}) collective-permute-start(bf16[3,320,768]{2,1,0:T(8,128)(2,1)S(1)} %copy-done.6), channel_id=1, source_target_pairs={{0,1},{1,0},{2,3},{3,2},{4,5},{5,4},{6,7},{7,6},{8,9},{9,8},{10,11... | collective-permute-start | bytes 4423688 | tf_op jit(solution)/shard_map/ppermute | solution.py:504
  319.9 54.7 %collective-permute-start.38 = (bf16[3,320,768]{2,1,0:T(8,128)(2,1)}, bf16[3,320,768]{2,1,0:T(8,128)(2,1)}, u32[]{:S(2)}, u32[]{:S(2)}) collective-permute-start(bf16[3,320,768]{2,1,0:T(8,128)(2,1)} %collective-permute-done.37), channel_id=1, source_target_pairs={{0,1},{1,0},{2,3},{3,2},{4,5},{5,4},{6,7},{7,6},{8,9},{9,8},{10,11... | collective-permute-start | bytes 4423688 | tf_op jit(solution)/shard_map/ppermute | solution.py:504
  331.6 37.9 %collective-permute-start.33 = (bf16[96,1536]{1,0:T(8,128)(2,1)S(1)}, bf16[96,1536]{1,0:T(8,128)(2,1)S(1)}, u32[]{:S(2)}, u32[]{:S(2)}) collective-permute-start(bf16[96,1536]{1,0:T(8,128)(2,1)S(1)} %add_convert_fusion.8), channel_id=1, source_target_pairs={{0,8},{4,12},{8,0},{12,4},{16,24},{20,28},{24,16},{28,20},{1,9},{5... | collective-permute-start | bytes 884744 | tf_op jit(solution)/shard_map/ppermute | solution.py:504
  339.1 32.6 %collective-permute-start.34 = (bf16[96,1536]{1,0:T(8,128)(2,1)S(1)}, bf16[96,1536]{1,0:T(8,128)(2,1)S(1)}, u32[]{:S(2)}, u32[]{:S(2)}) collective-permute-start(bf16[96,1536]{1,0:T(8,128)(2,1)S(1)} %add_convert_fusion.8), channel_id=1, source_target_pairs={{0,16},{4,20},{8,24},{12,28},{16,0},{20,4},{24,8},{28,12},{1,17},{... | collective-permute-start | bytes 884744 | tf_op jit(solution)/shard_map/ppermute | solution.py:504
  362.5 10.5 %collective-permute-start.35 = (bf16[96,1536]{1,0:T(8,128)(2,1)S(1)}, bf16[96,1536]{1,0:T(8,128)(2,1)}, u32[]{:S(2)}, u32[]{:S(2)}) collective-permute-start(bf16[96,1536]{1,0:T(8,128)(2,1)S(1)} %add_convert_fusion.8), channel_id=1, source_target_pairs={{0,24},{4,28},{8,16},{12,20},{16,8},{20,12},{24,0},{28,4},{1,25},{... | collective-permute-start | bytes 884744 | tf_op jit(solution)/shard_map/ppermute | solution.py:504
  369.5 43.9 %collective-permute-start.39 = (bf16[3,208,768]{2,1,0:T(8,128)(2,1)}, bf16[3,208,768]{2,1,0:T(8,128)(2,1)}, u32[]{:S(2)}, u32[]{:S(2)}) collective-permute-start(bf16[3,208,768]{2,1,0:T(8,128)(2,1)} %get-tuple-element.323), channel_id=1, source_target_pairs={{0,1},{1,2},{2,3},{4,5},{5,6},{6,7},{8,9},{9,10},{10,11},{12,13},{... | collective-permute-start | bytes 2875400 | tf_op jit(solution)/shard_map/ppermute | solution.py:510
  371.7 41.7 %collective-permute-start.40 = (bf16[3,208,768]{2,1,0:T(8,128)(2,1)}, bf16[3,208,768]{2,1,0:T(8,128)(2,1)}, u32[]{:S(2)}, u32[]{:S(2)}) collective-permute-start(bf16[3,208,768]{2,1,0:T(8,128)(2,1)} %get-tuple-element.324), channel_id=1, source_target_pairs={{1,0},{2,1},{3,2},{5,4},{6,5},{7,6},{9,8},{10,9},{11,10},{13,12},{... | collective-permute-start | bytes 2875400 | tf_op jit(solution)/shard_map/ppermute | solution.py:510
  373.0 15.5 %collective-permute-start.42 = (bf16[384,768]{1,0:T(8,128)(2,1)S(1)}, bf16[384,768]{1,0:T(8,128)(2,1)S(1)}, u32[]{:S(2)}, u32[]{:S(2)}) collective-permute-start(bf16[384,768]{1,0:T(8,128)(2,1)S(1)} %constant_dynamic-slice_fusion.9), channel_id=1, source_target_pairs={{0,4},{4,0},{8,12},{12,8},{16,20},{20,16},{24,28},{28,24},{1,5},{5... | collective-permute-start | bytes 1769480 | tf_op jit(solution)/shard_map/ppermute | solution.py:504
  392.1 12.7 %collective-permute-start.44 = (bf16[96,768]{1,0:T(8,128)(2,1)S(1)}, bf16[96,768]{1,0:T(8,128)(2,1)S(1)}, u32[]{:S(2)}, u32[]{:S(2)}) collective-permute-start(bf16[96,768]{1,0:T(8,128)(2,1)S(1)} %get-tuple-element.438), channel_id=1, source_target_pairs={{0,16},{4,20},{8,24},{12,28},{16,0},{20,4},{24,8},{28,12},{1,17},{... | collective-permute-start | bytes 442376 | tf_op jit(solution)/shard_map/ppermute | solution.py:504
  393.2 11.5 %collective-permute-start.45 = (bf16[96,768]{1,0:T(8,128)(2,1)S(1)}, bf16[96,768]{1,0:T(8,128)(2,1)S(1)}, u32[]{:S(2)}, u32[]{:S(2)}) collective-permute-start(bf16[96,768]{1,0:T(8,128)(2,1)S(1)} %get-tuple-element.437), channel_id=1, source_target_pairs={{0,24},{4,28},{8,16},{12,20},{16,8},{20,12},{24,0},{28,4},{1,25},{... | collective-permute-start | bytes 442376 | tf_op jit(solution)/shard_map/ppermute | solution.py:504
  396.8 45.6 %collective-permute-start.57 = (bf16[384,1536]{1,0:T(8,128)(2,1)S(1)}, bf16[384,1536]{1,0:T(8,128)(2,1)S(1)}, u32[]{:S(2)}, u32[]{:S(2)}) collective-permute-start(bf16[384,1536]{1,0:T(8,128)(2,1)S(1)} %bitcast.162), channel_id=1, source_target_pairs={{0,4},{4,0},{8,12},{12,8},{16,20},{20,16},{24,28},{28,24},{1,5},{5... | collective-permute-start | bytes 3538952 | tf_op jit(solution)/shard_map/ppermute | solution.py:504
  410.6 15.0 %collective-permute-start.46 = (bf16[96,768]{1,0:T(8,128)(2,1)S(1)}, bf16[96,768]{1,0:T(8,128)(2,1)S(1)}, u32[]{:S(2)}, u32[]{:S(2)}) collective-permute-start(bf16[96,768]{1,0:T(8,128)(2,1)S(1)} %add_convert_fusion.9), channel_id=1, source_target_pairs={{0,24},{4,28},{8,16},{12,20},{16,8},{20,12},{24,0},{28,4},{1,25},{... | collective-permute-start | bytes 442376 | tf_op jit(solution)/shard_map/ppermute | solution.py:504
  413.2 13.9 %collective-permute-start.47 = (bf16[96,768]{1,0:T(8,128)(2,1)S(1)}, bf16[96,768]{1,0:T(8,128)(2,1)S(1)}, u32[]{:S(2)}, u32[]{:S(2)}) collective-permute-start(bf16[96,768]{1,0:T(8,128)(2,1)S(1)} %add_convert_fusion.9), channel_id=1, source_target_pairs={{0,16},{4,20},{8,24},{12,28},{16,0},{20,4},{24,8},{28,12},{1,17},{... | collective-permute-start | bytes 442376 | tf_op jit(solution)/shard_map/ppermute | solution.py:504
  438.4 15.9 %collective-permute-start.49 = (bf16[384,768]{1,0:T(8,128)(2,1)}, bf16[384,768]{1,0:T(8,128)(2,1)}, u32[]{:S(2)}, u32[]{:S(2)}) collective-permute-start(bf16[384,768]{1,0:T(8,128)(2,1)} %bitcast.51), channel_id=1, source_target_pairs={{0,4},{4,0},{8,12},{12,8},{16,20},{20,16},{24,28},{28,24},{1,5},{5... | collective-permute-start | bytes 1769480 | tf_op jit(solution)/shard_map/ppermute | solution.py:504
  (49 other events, 391.0 us)
where the time goes:
time: 466 us; the launch traced here: 459 us
  Pallas kernels  229 us (49%)
  waiting for transfers between devices  77.6 us (17%)
  starting transfers between devices  75.1 us (16%)
  other arithmetic  40.6 us (9%)
  local copies, waits for them, and re-layouts  34.6 us (7%)
    pallas_call x4, Pallas kernels, attend_back(): pl.pallas_call(partial(attend_back_kernel, own, heads, count, first, halo...  88 us
    ppermute x56, waiting for transfers between devices, swap(): return lax.ppermute(values_in, axis, [(i, i ^ bit) for i in range(size)])  77.6 us
    ppermute x56, starting transfers between devices, swap(): return lax.ppermute(values_in, axis, [(i, i ^ bit) for i in range(size)])  71.5 us
    pallas_call x4, Pallas kernels, attend(): pl.pallas_call(partial(attend_kernel, own, heads, count, first), grid_spe...  57.1 us
    pallas_call x4, Pallas kernels, feed_part(): pl.pallas_call(partial(feed_kernel, FEED_CHUNKS, count, first), in_specs=...  51.3 us
    pallas_call x4, Pallas kernels, rows_call(): pl.pallas_call(kernel, grid_spec=pltpu.PrefetchScalarGridSpec(num_scalar_...  33 us
    convert_element_type x10, other arithmetic, add_low(): return total.astype(bf16)  13.8 us
  transfers between devices with their start and end apart: 58, of which 21 were waited for; matrix products, arithmetic and copies ran while one was open for 12% of the time, Pallas kernels for 50%

commit v1 on v0

--- a/solution.py
+++ b/solution.py
@@ -599,24 +599,6 @@
     return [swap(part, "wide", o) for part, o in zip(parts[1:], offsets(bits)[1:])]
 
 
-def reduce_far(part):
-    for bits in far_groups():
-        parts = cut(part, "wide", bits)
-        part = add_low(parts[0], *send_cut(parts, bits))
-    return part
-
-
-def spread_far(part):
-    for bits in reversed(far_groups()):
-        part = arrange(exchange(part, bits), bits, 0).reshape((-1,) + part.shape[1:])
-    return part
-
-
-def reduce_last(part):
-    parts = cut(part, "wide", [last_bit()])
-    return add_low(parts[0], *send_cut(parts, [last_bit()]))
-
-
 def spread_last(part):
     bits = [last_bit()]
     return arrange(exchange(part, bits), bits, 0).reshape((-1,) + part.shape[1:])
@@ -628,9 +610,13 @@
     return parts[0]
 
 
-def reduce_everywhere(values_in):
+def reduce_wide(values_in):
     for bits in far_groups() + [[last_bit()]]:
         values_in = tree_sum(exchange(values_in, bits))
+    return values_in
+
+
+def reduce_narrow(values_in):
     return tree_sum([values_in] + [swap(values_in, "narrow", o) for o in (1, 2, 3)])
 
 
@@ -782,11 +768,6 @@
         [low_rows, high_rows, low_rows, sum_rows],
         [part_spec, part_spec, part_spec, vec_spec],
     )
-    layer_far = swap(layer_own, "narrow", 2)
-    layer_parts = [
-        layer_own, swap(layer_own, "narrow", 1), layer_far, swap(layer_far, "narrow", 1)
-    ]
-
     def back_on(pieces, saved, grad_in, halo):
         return attend_back(
             offset, window_normed, mixed_grad, pieces, saved, bounds, grad_in, halo
@@ -795,16 +776,22 @@
     mixed_grad, down_sent, given = tie(mixed_grad, down_sent, given)
     near = add_low(near_keep, jnp.concatenate([up_sent, down_sent], axis=1))
     far_cut = cut(add_low(part2, given), "wide", last)
-    mixed_grad, near, *far_cut = tie(mixed_grad, near, *far_cut)
+    mixed_grad, near, layer_own, *far_cut = tie(mixed_grad, near, layer_own, *far_cut)
+    layer_far = swap(layer_own, "narrow", 2)
     far_sent = send_cut(far_cut, last)
     window_grad, (heads3,), sums3, _ = back_on([heads_cross], saved3, None, 0)
     given3 = swap(heads3, "narrow", 1)
-    window_grad, *far_sent = tie(window_grad, *far_sent)
+    window_grad, layer_far, *far_sent = tie(window_grad, layer_far, *far_sent)
     far = add_low(far_cut[0], *far_sent)
-    window_grad, far = tie(window_grad, far)
+    window_grad, far, layer_far = tie(window_grad, far, layer_far)
+    layer_parts = [
+        layer_own, swap(layer_own, "narrow", 1), layer_far, swap(layer_far, "narrow", 1)
+    ]
     far_given = swap(far, "narrow", 2)
     window_grad, (heads2,), sums2, _ = back_on([heads_far], saved2, window_grad, 0)
-    window_grad, far_given, given3 = tie(window_grad, far_given, given3)
+    window_grad, far_given, given3, *layer_parts = tie(
+        window_grad, far_given, given3, *layer_parts
+    )
     mine = add_low(near, far_given)
     for bits in groups[:-1]:
         parts = cut(mine, "wide", bits)
@@ -822,25 +809,36 @@
     mine_all = exchange(mine, groups[-1])
     window_grad, (heads0,), sums0, halos = back_on([heads_own], saved0, window_grad, halo)
     window_grad, *mine_all = tie(window_grad, *mine_all)
-    window_grad, *layer_parts = tie(window_grad, *layer_parts)
+    heads_cut = cut(add_low(heads0, given1, heads_given), "wide", last)
+    tied = tie(window_grad, *halos, *heads_cut, *mine_all, *layer_parts)
+    window_grad, *halos = tied[:3]
+    heads_cut, layer_parts = tied[3:5], tied[-4:]
+    heads_sent = send_cut(heads_cut, last)
+    from_left = shift(halos[1], "narrow", 1)
+    from_right = shift(halos[0], "narrow", -1)
+    mine = arrange(tied[5:-4], groups[-1], 0).reshape((-1,) + mine.shape[1:])
+    for bits in reversed(groups[:-1]):
+        mine = arrange(exchange(mine, bits), bits, 0).reshape((-1,) + mine.shape[1:])
+    mine, *heads_sent = tie(mine, *heads_sent)
+    mine_sent = exchange(mine, last)[1]
+    heads_part = add_low(heads_cut[0], *heads_sent)
+    for bits in groups[:-1]:
+        parts = cut(heads_part, "wide", bits)
+        heads_part = add_low(parts[0], *send_cut(parts, bits))
+    heads_cut = cut(heads_part, "wide", groups[-1])
+    window_grad, from_left, from_right, *heads_cut = tie(
+        window_grad, from_left, from_right, *heads_cut
+    )
+    heads_sent = send_cut(heads_cut, groups[-1])
     y_high, core_high = bit_of("narrow", 2), bit_of("narrow", 1)
     layer_near = join(layer_parts[0], layer_parts[1], core_high, 1)
     layer_far = join(layer_parts[2], layer_parts[3], core_high, 1)
     layer_out = join(layer_near, layer_far, y_high, 1).reshape(micro, row_count, width)
-    mine = arrange(mine_all, groups[-1], 0).reshape((-1,) + mine.shape[1:])
-    for bits in reversed(groups[:-1]):
-        mine = arrange(exchange(mine, bits), bits, 0).reshape((-1,) + mine.shape[1:])
-    feed_total = spread_last(mine)
-    heads_total = spread_last(
-        spread_far(reduce_far(reduce_last(add_low(heads0, given1, heads_given))))
-    )
     head_bias_parts = [
         jnp.concatenate([s[0, 2 * cols : 3 * cols], s[0, cols : 2 * cols]])
         for s in [*sums0, *sums1, *sums2, *sums3]
     ]
 
-    from_left = shift(halos[1], "narrow", 1)
-    from_right = shift(halos[0], "narrow", -1)
     token_grad, first_sums = rows_call(
         first_back_kernel, "first_back", place,
         [window_grad, from_left, from_right, middle_grad, tokens, vectors],
@@ -855,7 +853,20 @@
     )
     group_sums = jnp.stack([group_sums[r ^ narrow_at] for r in range(narrow_size)])
     packed = jnp.concatenate([sums.reshape(-1), group_sums.reshape(-1)]).reshape(-1, 128)
-    packed = reduce_everywhere(packed).reshape(-1)
+    packed, mine_sent, *heads_sent = tie(packed, mine_sent, *heads_sent)
+    heads_part = add_low(heads_cut[0], *heads_sent)
+    packed, heads_part, mine_sent = tie(packed, heads_part, mine_sent)
+    heads_all = exchange(heads_part, groups[-1])
+    packed = reduce_narrow(packed)
+    feed_total = arrange([mine, mine_sent], last, 0).reshape(width, -1)
+    packed, *heads_all = tie(packed, *heads_all)
+    packed = reduce_wide(packed)
+    heads_total = arrange(heads_all, groups[-1], 0).reshape((-1,) + heads_part.shape[1:])
+    for bits in reversed(groups[:-1]):
+        heads_total = arrange(exchange(heads_total, bits), bits, 0)
+        heads_total = heads_total.reshape((-1,) + heads_part.shape[1:])
+    heads_total = spread_last(heads_total)
+    packed = packed.reshape(-1)
     sums = packed[: 8 * width].reshape(8, width)
     group_sums = packed[8 * width :].reshape(narrow_size, -1)
     mine = lax.dynamic_slice_in_dim(group_sums, narrow_at, 1, 0)[0]

time: 466 us -> 458 us (0.983)
  waiting for transfers between devices: 77.6 us -> 69.2 us
  other arithmetic: 40.6 us -> 48.4 us
  starting transfers between devices: 75.1 us -> 67.6 us
    ppermute x56, waiting for transfers between devices: 77.6 us -> 69.2 us  [swap(): return lax.ppermute(values_in, axis, [(i, i ^ bit) for i in range(size)])]
    ppermute x56, starting transfers between devices: 71.5 us -> 64 us  [swap(): return lax.ppermute(values_in, axis, [(i, i ^ bit) for i in range(size)])]
  transfers between devices with their start and end apart: 58 -> 58, of which waited for: 21 -> 18; matrix products, arithmetic and copies ran while one was open for 12% -> 14% of each run, Pallas kernels for 50% -> 51%
where the time goes in v1:
time: 458 us; the launch traced here: 452 us
  Pallas kernels  229 us (50%)
  waiting for transfers between devices  69.2 us (15%)
  starting transfers between devices  67.6 us (15%)
  other arithmetic  48.4 us (11%)
  local copies, waits for them, and re-layouts  36 us (8%)
    pallas_call x4, Pallas kernels, attend_back(): pl.pallas_call(partial(attend_back_kernel, own, heads, count, first, halo...  87.9 us
    ppermute x56, waiting for transfers between devices, swap(): return lax.ppermute(values_in, axis, [(i, i ^ bit) for i in range(size)])  69.2 us
    ppermute x56, starting transfers between devices, swap(): return lax.ppermute(values_in, axis, [(i, i ^ bit) for i in range(size)])  64 us
    pallas_call x4, Pallas kernels, attend(): pl.pallas_call(partial(attend_kernel, own, heads, count, first), grid_spe...  57.1 us
    pallas_call x4, Pallas kernels, feed_part(): pl.pallas_call(partial(feed_kernel, FEED_CHUNKS, count, first), in_specs=...  51.3 us
    pallas_call x4, Pallas kernels, rows_call(): pl.pallas_call(kernel, grid_spec=pltpu.PrefetchScalarGridSpec(num_scalar_...  33 us
    convert_element_type x10, other arithmetic, add_low(): return total.astype(bf16)  15.9 us
  transfers between devices with their start and end apart: 58, of which 18 were waited for; matrix products, arithmetic and copies ran while one was open for 14% of the time, Pallas kernels for 51%

profile of v1, /device:TPU:0, one launch (start us, length us, event | category | flops | bytes accessed | tf_op | source)
XLA Modules:
  0.0 452.2 jit_solution(9240296931358046608)
XLA Ops:
  2.5 5.1 %collective-permute-start = (bf16[1,96,768]{2,1,0:T(8,128)(2,1)S(1)}, bf16[1,96,768]{2,1,0:T(8,128)(2,1)S(1)}, u32[]{:S(2)}, u32[]{:S(2)}) collective-permute-start(bf16[1,96,768]{2,1,0:T(8,128)(2,1)S(1)} %maximum_bitcast_fusion.2), channel_id=1, source_target_pairs={{0,24},{4,28},{8,16},{12,20},{16,8},{20,12},{24,0},{28,4},{1,25},{... | collective-permute-start | bytes 442376 | tf_op jit(solution)/shard_map/ppermute | solution.py:504
  10.1 2.4 collective-permute-done
  12.5 7.7 %collective-permute-done.1 = bf16[1,96,768]{2,1,0:T(8,128)(2,1)S(1)} collective-permute-done((bf16[1,96,768]{2,1,0:T(8,128)(2,1)S(1)}, bf16[1,96,768]{2,1,0:T(8,128)(2,1)S(1)}, u32[]{:S(2)}, u32[]{:S(2)}) %collective-permute-start.1) | collective-permute-done | bytes 147488 | tf_op jit(solution)/shard_map/ppermute | solution.py:504
  25.2 8.1 %first_norm.1 = (bf16[3,768,768]{2,1,0:T(8,128)(2,1)}, bf16[3,320,768]{2,1,0:T(8,128)(2,1)}) custom-call(s32[3]{0:T(128)} %pad_add_fusion.place_ref, bf16[3,1280,768]{2,1,0:T(8,128)(2,1)} %x_ref.5, bf16[3,1280,768]{2,1,0:T(8,128)(2,1)} %c_ref.3, f32[8,768]{1,0:T(8,128)} %stack.117.vec_ref), custom_call_target="tpu_custom_call" | custom-call | flops 1024 | bytes 1024 | tf_op jit(solution)/shard_map/first_norm/pallas_call | solution.py:426
  40.2 2.6 collective-permute-start.11
  45.8 11.3 %attend.4 = (f32[3,320,768]{2,1,0:T(8,128)}, bf16[3,320,192]{2,1,0:T(8,128)(2,1)}, bf16[3,768,192]{2,1,0:T(8,128)(2,1)}, bf16[3,768,192]{2,1,0:T(8,128)(2,1)}, b...) custom-call(s32[1]{0:T(128)} %bitcast.off_ref, bf16[3,768,768]{2,1,0:T(8,128)(2,1)} %get-tuple-element.219.refs_0_, ...), custom_call_target="tpu_custom_call" | custom-call | flops 1024 | bytes 1024 | tf_op jit(solution)/shard_map/attend/pallas_call | solution.py:150
  57.2 5.3 %collective-permute-done.10 = bf16[1,96,1536]{2,1,0:T(8,128)(2,1)S(1)} collective-permute-done((bf16[1,96,1536]{2,1,0:T(8,128)(2,1)S(1)}, bf16[1,96,1536]{2,1,0:T(8,128)(2,1)S(1)}, u32[]{:S(2)}, u32[]{:S(2)}) %collective-permute-start.10) | collective-permute-done | bytes 294944 | tf_op jit(solution)/shard_map/ppermute | solution.py:504
  70.1 11.7 %attend.5 = (f32[3,320,768]{2,1,0:T(8,128)}, bf16[3,320,192]{2,1,0:T(8,128)(2,1)}, bf16[3,768,192]{2,1,0:T(8,128)(2,1)}, bf16[3,768,192]{2,1,0:T(8,128)(2,1)}, b...) custom-call(s32[1]{0:T(128)} %bitcast.off_ref, bf16[3,768,768]{2,1,0:T(8,128)(2,1)} %get-tuple-element.219.refs_0_, ...), custom_call_target="tpu_custom_call" | custom-call | flops 1024 | bytes 1024 | tf_op jit(solution)/shard_map/attend/pallas_call | solution.py:150
  85.2 11.7 %attend.6 = (f32[3,320,768]{2,1,0:T(8,128)}, bf16[3,320,192]{2,1,0:T(8,128)(2,1)}, bf16[3,768,192]{2,1,0:T(8,128)(2,1)}, bf16[3,768,192]{2,1,0:T(8,128)(2,1)}, b...) custom-call(s32[1]{0:T(128)} %bitcast.off_ref, bf16[3,768,768]{2,1,0:T(8,128)(2,1)} %get-tuple-element.219.refs_0_, ...), custom_call_target="tpu_custom_call" | custom-call | flops 1024 | bytes 1024 | tf_op jit(solution)/shard_map/attend/pallas_call | solution.py:150
  100.9 22.4 %attend.7 = (f32[3,320,768]{2,1,0:T(8,128)}, bf16[3,320,192]{2,1,0:T(8,128)(2,1)}, bf16[3,768,192]{2,1,0:T(8,128)(2,1)}, bf16[3,768,192]{2,1,0:T(8,128)(2,1)}, b...) custom-call(s32[1]{0:T(128)} %bitcast.off_ref, bf16[3,768,768]{2,1,0:T(8,128)(2,1)} %get-tuple-element.219.refs_0_, ...), custom_call_target="tpu_custom_call" | custom-call | flops 1024 | bytes 1024 | tf_op jit(solution)/shard_map/attend/pallas_call | solution.py:150
  123.3 6.0 %second_norm.1 = (f32[3,320,768]{2,1,0:T(8,128)}, bf16[3,320,768]{2,1,0:T(8,128)(2,1)}) custom-call(s32[3]{0:T(128)} %pad_add_fusion.place_ref, f32[3,320,768]{2,1,0:T(8,128)} %get-tuple-element.251.mixed_ref, bf16[3,1280,768]{2,1,0:T(8,128)(2,1)} %x_ref.5, f32[8,768]{1,0:T(8,128)} %stack.117.vec_ref), custom_call_target="tpu_custom_call" | custom-call | flops 1024 | bytes 1024 | tf_op jit(solution)/shard_map/second_norm/pallas_call | solution.py:426
  130.1 11.5 %feed_part.4 = (f32[960,768]{1,0:T(8,128)}, f32[960,768]{1,0:T(8,128)}, bf16[768,1536]{1,0:T(8,128)(2,1)}, f32[1,768]{1,0:T(1,128)}) custom-call(bf16[960,768]{1,0:T(8,128)(2,1)} %bitcast.141, bf16[960,768]{1,0:T(8,128)(2,1)} %bitcast.137, bf16[768,1536]{1,0:T(8,128)(2,1)} %bitcast.152, f32[1,768]{1,0:T(1,128)} %reshape.808.refs_3_), custom_call_target="tpu_custom_call" | custom-call | flops 1024 | bytes 1024 | tf_op jit(solution)/shard_map/feed_part/pallas_call | solution.py:370
  141.5 2.8 collective-permute-done.19
  145.1 13.2 %feed_part.5 = (f32[960,768]{1,0:T(8,128)}, f32[960,768]{1,0:T(8,128)}, bf16[768,1536]{1,0:T(8,128)(2,1)}, f32[1,768]{1,0:T(1,128)}) custom-call(bf16[960,768]{1,0:T(8,128)(2,1)} %bitcast.142, bf16[960,768]{1,0:T(8,128)(2,1)} %bitcast.138, bf16[768,1536]{1,0:T(8,128)(2,1)} %collective-permute-done.18.refs_2_, ...), custom_call_target="tpu_custom_call", output_to_operand_aliasing={{0}: (4, {}), {1}: (5, {})} | custom-call | flops 1024 | bytes 1024 | tf_op jit(solution)/shard_map/feed_part/pallas_call | solution.py:370
  162.5 13.2 %feed_part.6 = (f32[960,768]{1,0:T(8,128)}, f32[960,768]{1,0:T(8,128)}, bf16[768,1536]{1,0:T(8,128)(2,1)}, f32[1,768]{1,0:T(1,128)}) custom-call(bf16[960,768]{1,0:T(8,128)(2,1)} %bitcast.143, bf16[960,768]{1,0:T(8,128)(2,1)} %bitcast.139, bf16[768,1536]{1,0:T(8,128)(2,1)} %bitcast.155, ...), custom_call_target="tpu_custom_call", output_to_operand_aliasing={{0}: (4, {}), {1}: (5, {})} | custom-call | flops 1024 | bytes 1024 | tf_op jit(solution)/shard_map/feed_part/pallas_call | solution.py:370
  175.7 3.0 add_convert_fusion.1
  180.7 13.4 %feed_part.7 = (f32[960,768]{1,0:T(8,128)}, f32[960,768]{1,0:T(8,128)}, bf16[768,1536]{1,0:T(8,128)(2,1)}, f32[1,768]{1,0:T(1,128)}) custom-call(bf16[960,768]{1,0:T(8,128)(2,1)} %bitcast.144, bf16[960,768]{1,0:T(8,128)(2,1)} %bitcast.140, bf16[768,1536]{1,0:T(8,128)(2,1)} %collective-permute-done.21.refs_2_, ...), custom_call_target="tpu_custom_call", output_to_operand_aliasing={{0}: (4, {}), {1}: (5, {})} | custom-call | flops 1024 | bytes 1024 | tf_op jit(solution)/shard_map/feed_part/pallas_call | solution.py:370
  195.5 10.6 %second_back.1 = (bf16[3,320,768]{2,1,0:T(8,128)(2,1)}, f32[3,320,768]{2,1,0:T(8,128)}, bf16[3,320,768]{2,1,0:T(8,128)(2,1)}, f32[8,768]{1,0:T(8,128)}) custom-call(s32[3]{0:T(128)} %pad_add_fusion.place_ref, f32[3,320,768]{2,1,0:T(8,128)} %bitcast.135, f32[3,320,768]{2,1,0:T(8,128)} %bitcast.136, f32[3,320,768]{2,1,0:T(8,128)} %get-tuple-element.294.m_ref, ...), custom_call_target="tpu_custom_call" | custom-call | flops 1024 | bytes 1024 | tf_op jit(solution)/shard_map/second_back/pallas_call | solution.py:426
  206.1 4.7 %collective-permute-done.24 = bf16[384,768]{1,0:T(8,128)(2,1)} collective-permute-done((bf16[384,768]{1,0:T(8,128)(2,1)}, bf16[384,768]{1,0:T(8,128)(2,1)}, u32[]{:S(2)}, u32[]{:S(2)}) %collective-permute-start.24) | collective-permute-done | bytes 589856 | tf_op jit(solution)/shard_map/ppermute | solution.py:504
  210.8 2.3 add_convert_fusion
  217.9 21.2 %attend_back.4 = (f32[3,768,768]{2,1,0:T(8,128)}, bf16[768,768]{1,0:T(8,128)(2,1)}, f32[1,768]{1,0:T(1,128)}) custom-call(s32[1]{0:T(128)} %bitcast.off_ref, bf16[3,768,768]{2,1,0:T(8,128)(2,1)} %get-tuple-element.219.refs_0_, bf16[3,320,768]{2,1,0:T(8,128)(2,1)} %get-tuple-element.305.refs_1_, s32[3,2,2,480]{3,2,1,0:T(2,128)} %tile.10.refs_2_, ...), custom_call_target="tpu_custom_call" | custom-call | flops 1024 | bytes 1024 | tf_op jit(solution)/shard_map/attend_back/pallas_call | solution.py:285
  239.1 5.6 %collective-permute-done.27 = bf16[384,1536]{1,0:T(8,128)(2,1)S(1)} collective-permute-done((bf16[384,1536]{1,0:T(8,128)(2,1)}, bf16[384,1536]{1,0:T(8,128)(2,1)S(1)}, u32[]{:S(2)}, u32[]{:S(2)}) %collective-permute-start.27) | collective-permute-done | bytes 1179680 | tf_op jit(solution)/shard_map/ppermute | solution.py:504
  244.8 5.2 %collective-permute-done.26 = bf16[3,320,768]{2,1,0:T(8,128)(2,1)} collective-permute-done((bf16[3,320,768]{2,1,0:T(8,128)(2,1)}, bf16[3,320,768]{2,1,0:T(8,128)(2,1)}, u32[]{:S(2)}, u32[]{:S(2)}) %collective-permute-start.26) | collective-permute-done | bytes 1474592 | tf_op jit(solution)/shard_map/ppermute | solution.py:504
  253.3 22.0 %attend_back.5 = (f32[3,768,768]{2,1,0:T(8,128)}, bf16[768,768]{1,0:T(8,128)(2,1)}, f32[1,768]{1,0:T(1,128)}) custom-call(s32[1]{0:T(128)} %bitcast.off_ref, bf16[3,768,768]{2,1,0:T(8,128)(2,1)} %get-tuple-element.219.refs_0_, bf16[3,320,768]{2,1,0:T(8,128)(2,1)} %get-tuple-element.305.refs_1_, s32[3,2,2,480]{3,2,1,0:T(2,128)} %tile.10.refs_2_, ...), custom_call_target="tpu_custom_call" | custom-call | flops 1024 | bytes 1024 | tf_op jit(solution)/shard_map/attend_back/pallas_call | solution.py:285
  275.3 4.7 %collective-permute-done.28 = bf16[384,1536]{1,0:T(8,128)(2,1)} collective-permute-done((bf16[384,1536]{1,0:T(8,128)(2,1)}, bf16[384,1536]{1,0:T(8,128)(2,1)}, u32[]{:S(2)}, u32[]{:S(2)}) %collective-permute-start.28) | collective-permute-done | bytes 1179680 | tf_op jit(solution)/shard_map/ppermute | solution.py:504
  280.0 1.6 add_convert_fusion.3
  293.3 7.2 %collective-permute-start.33 = (bf16[96,1536]{1,0:T(8,128)(2,1)}, bf16[96,1536]{1,0:T(8,128)(2,1)}, u32[]{:S(2)}, u32[]{:S(2)}) collective-permute-start(bf16[96,1536]{1,0:T(8,128)(2,1)} %get-tuple-element.346), channel_id=1, source_target_pairs={{0,8},{4,12},{8,0},{12,4},{16,24},{20,28},{24,16},{28,20},{1,9},{5... | collective-permute-start | bytes 884744 | tf_op jit(solution)/shard_map/ppermute | solution.py:504
  300.5 2.4 collective-permute-start.35
  305.7 22.3 %attend_back.6 = (f32[3,768,768]{2,1,0:T(8,128)}, bf16[768,768]{1,0:T(8,128)(2,1)}, f32[1,768]{1,0:T(1,128)}) custom-call(s32[1]{0:T(128)} %bitcast.off_ref, bf16[3,768,768]{2,1,0:T(8,128)(2,1)} %get-tuple-element.219.refs_0_, bf16[3,320,768]{2,1,0:T(8,128)(2,1)} %get-tuple-element.305.refs_1_, s32[3,2,2,480]{3,2,1,0:T(2,128)} %tile.10.refs_2_, ...), custom_call_target="tpu_custom_call" | custom-call | flops 1024 | bytes 1024 | tf_op jit(solution)/shard_map/attend_back/pallas_call | solution.py:285
  334.1 2.4 collective-permute-start.38
  336.5 22.4 %attend_back.7 = (f32[3,768,768]{2,1,0:T(8,128)}, bf16[768,768]{1,0:T(8,128)(2,1)}, f32[1,768]{1,0:T(1,128)}, bf16[3,208,768]{2,1,0:T(8,128)(2,1)}, bf16[3,208,768]{2,1,0:T(8,128)(2,1)}) custom-call(s32[1]{0:T(128)} %bitcast.off_ref, bf16[3,768,768]{2,1,0:T(8,128)(2,1)} %get-tuple-element.219.refs_0_, bf16[3,320,768]{2,1,0:T(8,128)(2,1)} %get-tuple-element.305.refs_1_, ...), custom_call_target="tpu_custom_call" | custom-call | flops 1024 | bytes 1024 | tf_op jit(solution)/shard_map/attend_back/pallas_call | solution.py:285
  360.0 2.4 add_convert_fusion.2
  366.0 2.4 collective-permute-start.40
  372.6 2.0 select_bitcast_fusion.1
  374.6 5.0 %collective-permute-done.42 = bf16[384,768]{1,0:T(8,128)(2,1)S(1)} collective-permute-done((bf16[384,768]{1,0:T(8,128)(2,1)S(1)}, bf16[384,768]{1,0:T(8,128)(2,1)S(1)}, u32[]{:S(2)}, u32[]{:S(2)}) %collective-permute-start.42) | collective-permute-done | bytes 589856 | tf_op jit(solution)/shard_map/ppermute | solution.py:504
  382.2 3.0 copy.60
  385.7 1.8 collective-permute-start.45
  387.5 2.4 collective-permute-start.46
  389.8 8.3 %first_back.1 = (bf16[3,320,768]{2,1,0:T(8,128)(2,1)}, f32[8,768]{1,0:T(8,128)}) custom-call(s32[3]{0:T(128)} %pad_add_fusion.place_ref, f32[3,768,768]{2,1,0:T(8,128)} %get-tuple-element.385.win_ref, bf16[3,208,768]{2,1,0:T(8,128)(2,1)} %collective-permute-done.40.left_ref, bf16[3,208,768]{2,1,0:T(8,128)(2,1)} %collective-permute-done.41.right_ref, ...), custom_call_target="tpu_custom_call" | custom-call | flops 1024 | bytes 1024 | tf_op jit(solution)/shard_map/first_back/pallas_call | solution.py:426
  399.6 6.8 %collective-permute-done.43 = bf16[384,1536]{1,0:T(8,128)(2,1)S(1)} collective-permute-done((bf16[384,1536]{1,0:T(8,128)(2,1)S(1)}, bf16[384,1536]{1,0:T(8,128)(2,1)S(1)}, u32[]{:S(2)}, u32[]{:S(2)}) %collective-permute-start.43) | collective-permute-done | bytes 1179680 | tf_op jit(solution)/shard_map/ppermute | solution.py:504
  409.3 1.8 collective-permute-start.51
  412.3 2.4 collective-permute-start.52
  415.6 1.9 collective-permute-done.50
  417.4 6.1 %collective-permute-done.51 = bf16[96,768]{1,0:T(8,128)(2,1)} collective-permute-done((bf16[96,768]{1,0:T(8,128)(2,1)}, bf16[96,768]{1,0:T(8,128)(2,1)}, u32[]{:S(2)}, u32[]{:S(2)}) %collective-permute-start.51) | collective-permute-done | bytes 147488 | tf_op jit(solution)/shard_map/ppermute | solution.py:504
  423.6 2.7 collective-permute-start.54
  426.3 2.3 collective-permute-start.56
  436.6 1.8 copy.63
  438.3 7.3 %collective-permute-done.57 = f32[84,128]{1,0:T(8,128)} collective-permute-done((f32[84,128]{1,0:T(8,128)}, f32[84,128]{1,0:T(8,128)}, u32[]{:S(2)}, u32[]{:S(2)}) %collective-permute-start.57) | collective-permute-done | bytes 43040 | tf_op jit(solution)/shard_map/ppermute | solution.py:504
  (282 shorter events, 104.2 us)
Async XLA Ops:
  7.7 12.5 %collective-permute-start.1 = (bf16[1,96,768]{2,1,0:T(8,128)(2,1)S(1)}, bf16[1,96,768]{2,1,0:T(8,128)(2,1)S(1)}, u32[]{:S(2)}, u32[]{:S(2)}) collective-permute-start(bf16[1,96,768]{2,1,0:T(8,128)(2,1)S(1)} %maximum_bitcast_fusion.2), channel_id=1, source_target_pairs={{0,16},{4,20},{8,24},{12,28},{16,0},{20,4},{24,8},{28,12},{1,17},{... | collective-permute-start | bytes 442376 | tf_op jit(solution)/shard_map/ppermute | solution.py:504
  7.7 12.5 %collective-permute-start.2 = (bf16[1,96,768]{2,1,0:T(8,128)(2,1)S(1)}, bf16[1,96,768]{2,1,0:T(8,128)(2,1)S(1)}, u32[]{:S(2)}, u32[]{:S(2)}) collective-permute-start(bf16[1,96,768]{2,1,0:T(8,128)(2,1)S(1)} %maximum_bitcast_fusion.2), channel_id=1, source_target_pairs={{0,8},{4,12},{8,0},{12,4},{16,24},{20,28},{24,16},{28,20},{1,9},{5... | collective-permute-start | bytes 442376 | tf_op jit(solution)/shard_map/ppermute | solution.py:504
  20.6 17.8 %collective-permute-start.3 = (bf16[4,96,768]{2,1,0:T(8,128)(2,1)S(1)}, bf16[4,96,768]{2,1,0:T(8,128)(2,1)S(1)}, u32[]{:S(2)}, u32[]{:S(2)}) collective-permute-start(bf16[4,96,768]{2,1,0:T(8,128)(2,1)S(1)} %maximum_bitcast_fusion), channel_id=1, source_target_pairs={{0,4},{4,0},{8,12},{12,8},{16,20},{20,16},{24,28},{28,24},{1,5},{5... | collective-permute-start | bytes 1769480 | tf_op jit(solution)/shard_map/ppermute | solution.py:504
  22.1 11.9 %collective-permute-start.5 = (f32[1,1152]{1,0:T(1,128)S(1)}, f32[1,1152]{1,0:T(1,128)S(1)}, u32[]{:S(2)}, u32[]{:S(2)}) collective-permute-start(f32[1,1152]{1,0:T(1,128)S(1)} %reshape.804), channel_id=1, source_target_pairs={{0,2},{1,3},{2,0},{3,1},{4,6},{5,7},{6,4},{7,5},{8,10},{9,11},{10,... | collective-permute-start | bytes 13832 | tf_op jit(solution)/shard_map/ppermute | solution.py:504
  39.6 24.3 %collective-permute-start.8 = (bf16[4,96,768]{2,1,0:T(8,128)(2,1)}, bf16[4,96,768]{2,1,0:T(8,128)(2,1)S(1)}, u32[]{:S(2)}, u32[]{:S(2)}) collective-permute-start(bf16[4,96,768]{2,1,0:T(8,128)(2,1)} %bitcast.22), channel_id=1, source_target_pairs={{0,2},{1,3},{2,0},{3,1},{4,6},{5,7},{6,4},{7,5},{8,10},{9,11},{10,... | collective-permute-start | bytes 1769480 | tf_op jit(solution)/shard_map/ppermute | solution.py:504
  40.2 22.2 %collective-permute-start.10 = (bf16[1,96,1536]{2,1,0:T(8,128)(2,1)S(1)}, bf16[1,96,1536]{2,1,0:T(8,128)(2,1)S(1)}, u32[]{:S(2)}, u32[]{:S(2)}) collective-permute-start(bf16[1,96,1536]{2,1,0:T(8,128)(2,1)S(1)} %maximum_bitcast_fusion.1), channel_id=1, source_target_pairs={{0,16},{4,20},{8,24},{12,28},{16,0},{20,4},{24,8},{28,12},{1,17},{... | collective-permute-start | bytes 884744 | tf_op jit(solution)/shard_map/ppermute | solution.py:504
  40.2 22.2 %collective-permute-start.11 = (bf16[1,96,1536]{2,1,0:T(8,128)(2,1)S(1)}, bf16[1,96,1536]{2,1,0:T(8,128)(2,1)}, u32[]{:S(2)}, u32[]{:S(2)}) collective-permute-start(bf16[1,96,1536]{2,1,0:T(8,128)(2,1)S(1)} %maximum_bitcast_fusion.1), channel_id=1, source_target_pairs={{0,24},{4,28},{8,16},{12,20},{16,8},{20,12},{24,0},{28,4},{1,25},{... | collective-permute-start | bytes 884744 | tf_op jit(solution)/shard_map/ppermute | solution.py:504
  42.8 21.0 %collective-permute-start.9 = (bf16[1,96,1536]{2,1,0:T(8,128)(2,1)S(1)}, bf16[1,96,1536]{2,1,0:T(8,128)(2,1)}, u32[]{:S(2)}, u32[]{:S(2)}) collective-permute-start(bf16[1,96,1536]{2,1,0:T(8,128)(2,1)S(1)} %maximum_bitcast_fusion.1), channel_id=1, source_target_pairs={{0,8},{4,12},{8,0},{12,4},{16,24},{20,28},{24,16},{28,20},{1,9},{5... | collective-permute-start | bytes 884744 | tf_op jit(solution)/shard_map/ppermute | solution.py:504
  44.8 24.2 %collective-permute-start.7 = (bf16[768,768]{1,0:T(8,128)(2,1)S(1)}, bf16[768,768]{1,0:T(8,128)(2,1)S(1)}, u32[]{:S(2)}, u32[]{:S(2)}) collective-permute-start(bf16[768,768]{1,0:T(8,128)(2,1)S(1)} %bitcast.145), channel_id=1, source_target_pairs={{0,1},{1,0},{2,3},{3,2},{4,5},{5,4},{6,7},{7,6},{8,9},{9,8},{10,11... | collective-permute-start | bytes 3538952 | tf_op jit(solution)/shard_map/ppermute | solution.py:504
  67.0 14.8 %collective-permute-start.12 = (bf16[4,96,768]{2,1,0:T(8,128)(2,1)}, bf16[4,96,768]{2,1,0:T(8,128)(2,1)}, u32[]{:S(2)}, u32[]{:S(2)}) collective-permute-start(bf16[4,96,768]{2,1,0:T(8,128)(2,1)} %bitcast.26), channel_id=1, source_target_pairs={{0,2},{1,3},{2,0},{3,1},{4,6},{5,7},{6,4},{7,5},{8,10},{9,11},{10,... | collective-permute-start | bytes 1769480 | tf_op jit(solution)/shard_map/ppermute | solution.py:504
  68.5 13.5 %collective-permute-start.13 = (bf16[2,96,1536]{2,1,0:T(8,128)(2,1)S(1)}, bf16[2,96,1536]{2,1,0:T(8,128)(2,1)S(1)}, u32[]{:S(2)}, u32[]{:S(2)}) collective-permute-start(bf16[2,96,1536]{2,1,0:T(8,128)(2,1)S(1)} %get-tuple-element.244), channel_id=1, source_target_pairs={{0,4},{4,0},{8,12},{12,8},{16,20},{20,16},{24,28},{28,24},{1,5},{5... | collective-permute-start | bytes 1769480 | tf_op jit(solution)/shard_map/ppermute | solution.py:504
  83.4 13.6 %collective-permute-start.15 = (bf16[2,96,1536]{2,1,0:T(8,128)(2,1)}, bf16[2,96,1536]{2,1,0:T(8,128)(2,1)S(1)}, u32[]{:S(2)}, u32[]{:S(2)}) collective-permute-start(bf16[2,96,1536]{2,1,0:T(8,128)(2,1)} %get-tuple-element.250), channel_id=1, source_target_pairs={{0,4},{4,0},{8,12},{12,8},{16,20},{20,16},{24,28},{28,24},{1,5},{5... | collective-permute-start | bytes 1769480 | tf_op jit(solution)/shard_map/ppermute | solution.py:504
  84.7 13.0 %collective-permute-start.16 = (bf16[2,96,1536]{2,1,0:T(8,128)(2,1)S(1)}, bf16[2,96,1536]{2,1,0:T(8,128)(2,1)S(1)}, u32[]{:S(2)}, u32[]{:S(2)}) collective-permute-start(bf16[2,96,1536]{2,1,0:T(8,128)(2,1)S(1)} %get-tuple-element.244), channel_id=1, source_target_pairs={{0,2},{1,3},{2,0},{3,1},{4,6},{5,7},{6,4},{7,5},{8,10},{9,11},{10,... | collective-permute-start | bytes 1769480 | tf_op jit(solution)/shard_map/ppermute | solution.py:504
  85.2 15.7 %collective-permute-start.14 = (bf16[768,768]{1,0:T(8,128)(2,1)S(1)}, bf16[768,768]{1,0:T(8,128)(2,1)}, u32[]{:S(2)}, u32[]{:S(2)}) collective-permute-start(bf16[768,768]{1,0:T(8,128)(2,1)S(1)} %bitcast.148), channel_id=1, source_target_pairs={{0,1},{1,0},{2,3},{3,2},{4,5},{5,4},{6,7},{7,6},{8,9},{9,8},{10,11... | collective-permute-start | bytes 3538952 | tf_op jit(solution)/shard_map/ppermute | solution.py:504
  99.6 45.5 %collective-permute-start.18 = (bf16[768,1536]{1,0:T(8,128)(2,1)S(1)}, bf16[768,1536]{1,0:T(8,128)(2,1)}, u32[]{:S(2)}, u32[]{:S(2)}) collective-permute-start(bf16[768,1536]{1,0:T(8,128)(2,1)S(1)} %bitcast.151), channel_id=1, source_target_pairs={{0,1},{1,0},{2,3},{3,2},{4,5},{5,4},{6,7},{7,6},{8,9},{9,8},{10,11... | collective-permute-start | bytes 7077896 | tf_op jit(solution)/shard_map/ppermute | solution.py:504
  99.7 23.6 %collective-permute-start.17 = (bf16[2,96,1536]{2,1,0:T(8,128)(2,1)}, bf16[2,96,1536]{2,1,0:T(8,128)(2,1)}, u32[]{:S(2)}, u32[]{:S(2)}) collective-permute-start(bf16[2,96,1536]{2,1,0:T(8,128)(2,1)} %get-tuple-element.250), channel_id=1, source_target_pairs={{0,2},{1,3},{2,0},{3,1},{4,6},{5,7},{6,4},{7,5},{8,10},{9,11},{10,... | collective-permute-start | bytes 1769480 | tf_op jit(solution)/shard_map/ppermute | solution.py:504
  129.3 15.1 %collective-permute-start.19 = (bf16[2,96,1536]{2,1,0:T(8,128)(2,1)S(1)}, bf16[2,96,1536]{2,1,0:T(8,128)(2,1)S(1)}, u32[]{:S(2)}, u32[]{:S(2)}) collective-permute-start(bf16[2,96,1536]{2,1,0:T(8,128)(2,1)S(1)} %copy-done.8), channel_id=1, source_target_pairs={{0,4},{4,0},{8,12},{12,8},{16,20},{20,16},{24,28},{28,24},{1,5},{5... | collective-permute-start | bytes 1769480 | tf_op jit(solution)/shard_map/ppermute | solution.py:504
  144.3 14.5 %collective-permute-start.20 = (bf16[2,96,1536]{2,1,0:T(8,128)(2,1)}, bf16[2,96,1536]{2,1,0:T(8,128)(2,1)}, u32[]{:S(2)}, u32[]{:S(2)}) collective-permute-start(bf16[2,96,1536]{2,1,0:T(8,128)(2,1)} %collective-permute-done.17), channel_id=1, source_target_pairs={{0,4},{4,0},{8,12},{12,8},{16,20},{20,16},{24,28},{28,24},{1,5},{5... | collective-permute-start | bytes 1769480 | tf_op jit(solution)/shard_map/ppermute | solution.py:504
  161.1 14.6 %collective-permute-start.22 = (bf16[768,1536]{1,0:T(8,128)(2,1)}, bf16[768,1536]{1,0:T(8,128)(2,1)}, u32[]{:S(2)}, u32[]{:S(2)}) collective-permute-start(bf16[768,1536]{1,0:T(8,128)(2,1)} %get-tuple-element.280), channel_id=1, source_target_pairs={{0,1},{1,0},{2,3},{3,2},{4,5},{5,4},{6,7},{7,6},{8,9},{9,8},{10,11... | collective-permute-start | bytes 7077896 | tf_op jit(solution)/shard_map/ppermute | solution.py:504
  161.2 19.5 %collective-permute-start.21 = (bf16[768,1536]{1,0:T(8,128)(2,1)S(1)}, bf16[768,1536]{1,0:T(8,128)(2,1)}, u32[]{:S(2)}, u32[]{:S(2)}) collective-permute-start(bf16[768,1536]{1,0:T(8,128)(2,1)S(1)} %bitcast.154), channel_id=1, source_target_pairs={{0,1},{1,0},{2,3},{3,2},{4,5},{5,4},{6,7},{7,6},{8,9},{9,8},{10,11... | collective-permute-start | bytes 7077896 | tf_op jit(solution)/shard_map/ppermute | solution.py:504
  179.9 14.9 %collective-permute-start.23 = (bf16[384,768]{1,0:T(8,128)(2,1)}, bf16[384,768]{1,0:T(8,128)(2,1)}, u32[]{:S(2)}, u32[]{:S(2)}) collective-permute-start(bf16[384,768]{1,0:T(8,128)(2,1)} %get-tuple-element.289), channel_id=1, source_target_pairs={{0,4},{4,0},{8,12},{12,8},{16,20},{20,16},{24,28},{28,24},{1,5},{5... | collective-permute-start | bytes 1769480 | tf_op jit(solution)/shard_map/ppermute | solution.py:504
  194.7 16.1 %collective-permute-start.25 = (bf16[768,1536]{1,0:T(8,128)(2,1)}, bf16[768,1536]{1,0:T(8,128)(2,1)}, u32[]{:S(2)}, u32[]{:S(2)}) collective-permute-start(bf16[768,1536]{1,0:T(8,128)(2,1)} %get-tuple-element.297), channel_id=1, source_target_pairs={{0,1},{1,0},{2,3},{3,2},{4,5},{5,4},{6,7},{7,6},{8,9},{9,8},{10,11... | collective-permute-start | bytes 7077896 | tf_op jit(solution)/shard_map/ppermute | solution.py:504
  194.7 16.1 %collective-permute-start.24 = (bf16[384,768]{1,0:T(8,128)(2,1)}, bf16[384,768]{1,0:T(8,128)(2,1)}, u32[]{:S(2)}, u32[]{:S(2)}) collective-permute-start(bf16[384,768]{1,0:T(8,128)(2,1)} %get-tuple-element.296), channel_id=1, source_target_pairs={{0,4},{4,0},{8,12},{12,8},{16,20},{20,16},{24,28},{28,24},{1,5},{5... | collective-permute-start | bytes 1769480 | tf_op jit(solution)/shard_map/ppermute | solution.py:504
  215.8 34.2 %collective-permute-start.26 = (bf16[3,320,768]{2,1,0:T(8,128)(2,1)}, bf16[3,320,768]{2,1,0:T(8,128)(2,1)}, u32[]{:S(2)}, u32[]{:S(2)}) collective-permute-start(bf16[3,320,768]{2,1,0:T(8,128)(2,1)} %get-tuple-element.374), channel_id=1, source_target_pairs={{0,2},{1,3},{2,0},{3,1},{4,6},{5,7},{6,4},{7,5},{8,10},{9,11},{10,... | collective-permute-start | bytes 4423688 | tf_op jit(solution)/shard_map/ppermute | solution.py:504
  217.3 27.5 %collective-permute-start.27 = (bf16[384,1536]{1,0:T(8,128)(2,1)}, bf16[384,1536]{1,0:T(8,128)(2,1)S(1)}, u32[]{:S(2)}, u32[]{:S(2)}) collective-permute-start(bf16[384,1536]{1,0:T(8,128)(2,1)} %get-tuple-element.328), channel_id=1, source_target_pairs={{0,4},{4,0},{8,12},{12,8},{16,20},{20,16},{24,28},{28,24},{1,5},{5... | collective-permute-start | bytes 3538952 | tf_op jit(solution)/shard_map/ppermute | solution.py:504
  217.9 57.3 %collective-permute-start.30 = (bf16[3,320,768]{2,1,0:T(8,128)(2,1)}, bf16[3,320,768]{2,1,0:T(8,128)(2,1)}, u32[]{:S(2)}, u32[]{:S(2)}) collective-permute-start(bf16[3,320,768]{2,1,0:T(8,128)(2,1)} %get-tuple-element.374), channel_id=1, source_target_pairs={{0,1},{1,0},{2,3},{3,2},{4,5},{5,4},{6,7},{7,6},{8,9},{9,8},{10,11... | collective-permute-start | bytes 4423688 | tf_op jit(solution)/shard_map/ppermute | solution.py:504
  251.3 28.7 %collective-permute-start.31 = (bf16[3,320,768]{2,1,0:T(8,128)(2,1)}, bf16[3,320,768]{2,1,0:T(8,128)(2,1)S(1)}, u32[]{:S(2)}, u32[]{:S(2)}) collective-permute-start(bf16[3,320,768]{2,1,0:T(8,128)(2,1)} %collective-permute-done.26), channel_id=1, source_target_pairs={{0,1},{1,0},{2,3},{3,2},{4,5},{5,4},{6,7},{7,6},{8,9},{9,8},{10,11... | collective-permute-start | bytes 4423688 | tf_op jit(solution)/shard_map/ppermute | solution.py:504
  251.3 24.0 %collective-permute-start.29 = (bf16[768,768]{1,0:T(8,128)(2,1)}, bf16[768,768]{1,0:T(8,128)(2,1)}, u32[]{:S(2)}, u32[]{:S(2)}) collective-permute-start(bf16[768,768]{1,0:T(8,128)(2,1)} %get-tuple-element.336), channel_id=1, source_target_pairs={{0,1},{1,0},{2,3},{3,2},{4,5},{5,4},{6,7},{7,6},{8,9},{9,8},{10,11... | collective-permute-start | bytes 3538952 | tf_op jit(solution)/shard_map/ppermute | solution.py:504
  251.8 28.2 %collective-permute-start.28 = (bf16[384,1536]{1,0:T(8,128)(2,1)}, bf16[384,1536]{1,0:T(8,128)(2,1)}, u32[]{:S(2)}, u32[]{:S(2)}) collective-permute-start(bf16[384,1536]{1,0:T(8,128)(2,1)} %add_convert_fusion.5), channel_id=1, source_target_pairs={{0,2},{1,3},{2,0},{3,1},{4,6},{5,7},{6,4},{7,5},{8,10},{9,11},{10,... | collective-permute-start | bytes 3538952 | tf_op jit(solution)/shard_map/ppermute | solution.py:504
  284.1 46.6 %collective-permute-start.32 = (bf16[768,768]{1,0:T(8,128)(2,1)S(1)}, bf16[768,768]{1,0:T(8,128)(2,1)}, u32[]{:S(2)}, u32[]{:S(2)}) collective-permute-start(bf16[768,768]{1,0:T(8,128)(2,1)S(1)} %add_convert_fusion.4), channel_id=1, source_target_pairs={{0,2},{1,3},{2,0},{3,1},{4,6},{5,7},{6,4},{7,5},{8,10},{9,11},{10,... | collective-permute-start | bytes 3538952 | tf_op jit(solution)/shard_map/ppermute | solution.py:504
  293.3 37.4 %collective-permute-start.33 = (bf16[96,1536]{1,0:T(8,128)(2,1)}, bf16[96,1536]{1,0:T(8,128)(2,1)}, u32[]{:S(2)}, u32[]{:S(2)}) collective-permute-start(bf16[96,1536]{1,0:T(8,128)(2,1)} %get-tuple-element.346), channel_id=1, source_target_pairs={{0,8},{4,12},{8,0},{12,4},{16,24},{20,28},{24,16},{28,20},{1,9},{5... | collective-permute-start | bytes 884744 | tf_op jit(solution)/shard_map/ppermute | solution.py:504
  300.5 30.2 %collective-permute-start.34 = (bf16[96,1536]{1,0:T(8,128)(2,1)S(1)}, bf16[96,1536]{1,0:T(8,128)(2,1)}, u32[]{:S(2)}, u32[]{:S(2)}) collective-permute-start(bf16[96,1536]{1,0:T(8,128)(2,1)S(1)} %get-tuple-element.347), channel_id=1, source_target_pairs={{0,16},{4,20},{8,24},{12,28},{16,0},{20,4},{24,8},{28,12},{1,17},{... | collective-permute-start | bytes 884744 | tf_op jit(solution)/shard_map/ppermute | solution.py:504
  300.5 30.2 %collective-permute-start.35 = (bf16[96,1536]{1,0:T(8,128)(2,1)S(1)}, bf16[96,1536]{1,0:T(8,128)(2,1)}, u32[]{:S(2)}, u32[]{:S(2)}) collective-permute-start(bf16[96,1536]{1,0:T(8,128)(2,1)S(1)} %get-tuple-element.348), channel_id=1, source_target_pairs={{0,24},{4,28},{8,16},{12,20},{16,8},{20,12},{24,0},{28,4},{1,25},{... | collective-permute-start | bytes 884744 | tf_op jit(solution)/shard_map/ppermute | solution.py:504
  327.9 32.0 %collective-permute-start.39 = (bf16[768,768]{1,0:T(8,128)(2,1)}, bf16[768,768]{1,0:T(8,128)(2,1)}, u32[]{:S(2)}, u32[]{:S(2)}) collective-permute-start(bf16[768,768]{1,0:T(8,128)(2,1)} %get-tuple-element.361), channel_id=1, source_target_pairs={{0,1},{1,0},{2,3},{3,2},{4,5},{5,4},{6,7},{7,6},{8,9},{9,8},{10,11... | collective-permute-start | bytes 3538952 | tf_op jit(solution)/shard_map/ppermute | solution.py:504
  332.1 32.4 %collective-permute-start.36 = (bf16[96,1536]{1,0:T(8,128)(2,1)S(1)}, bf16[96,1536]{1,0:T(8,128)(2,1)S(1)}, u32[]{:S(2)}, u32[]{:S(2)}) collective-permute-start(bf16[96,1536]{1,0:T(8,128)(2,1)S(1)} %add_convert_fusion.8), channel_id=1, source_target_pairs={{0,8},{4,12},{8,0},{12,4},{16,24},{20,28},{24,16},{28,20},{1,9},{5... | collective-permute-start | bytes 884744 | tf_op jit(solution)/shard_map/ppermute | solution.py:504
  333.2 31.2 %collective-permute-start.37 = (bf16[96,1536]{1,0:T(8,128)(2,1)S(1)}, bf16[96,1536]{1,0:T(8,128)(2,1)S(1)}, u32[]{:S(2)}, u32[]{:S(2)}) collective-permute-start(bf16[96,1536]{1,0:T(8,128)(2,1)S(1)} %add_convert_fusion.8), channel_id=1, source_target_pairs={{0,16},{4,20},{8,24},{12,28},{16,0},{20,4},{24,8},{28,12},{1,17},{... | collective-permute-start | bytes 884744 | tf_op jit(solution)/shard_map/ppermute | solution.py:504
  334.1 30.3 %collective-permute-start.38 = (bf16[96,1536]{1,0:T(8,128)(2,1)S(1)}, bf16[96,1536]{1,0:T(8,128)(2,1)}, u32[]{:S(2)}, u32[]{:S(2)}) collective-permute-start(bf16[96,1536]{1,0:T(8,128)(2,1)S(1)} %add_convert_fusion.8), channel_id=1, source_target_pairs={{0,24},{4,28},{8,16},{12,20},{16,8},{20,12},{24,0},{28,4},{1,25},{... | collective-permute-start | bytes 884744 | tf_op jit(solution)/shard_map/ppermute | solution.py:504
  364.5 15.1 %collective-permute-start.42 = (bf16[384,768]{1,0:T(8,128)(2,1)S(1)}, bf16[384,768]{1,0:T(8,128)(2,1)S(1)}, u32[]{:S(2)}, u32[]{:S(2)}) collective-permute-start(bf16[384,768]{1,0:T(8,128)(2,1)S(1)} %get-tuple-element.383), channel_id=1, source_target_pairs={{0,4},{4,0},{8,12},{12,8},{16,20},{20,16},{24,28},{28,24},{1,5},{5... | collective-permute-start | bytes 1769480 | tf_op jit(solution)/shard_map/ppermute | solution.py:504
  366.0 19.4 %collective-permute-start.40 = (bf16[3,208,768]{2,1,0:T(8,128)(2,1)}, bf16[3,208,768]{2,1,0:T(8,128)(2,1)}, u32[]{:S(2)}, u32[]{:S(2)}) collective-permute-start(bf16[3,208,768]{2,1,0:T(8,128)(2,1)} %get-tuple-element.376), channel_id=1, source_target_pairs={{0,1},{1,2},{2,3},{4,5},{5,6},{6,7},{8,9},{9,10},{10,11},{12,13},{... | collective-permute-start | bytes 2875400 | tf_op jit(solution)/shard_map/ppermute | solution.py:510
  368.4 17.0 %collective-permute-start.41 = (bf16[3,208,768]{2,1,0:T(8,128)(2,1)S(1)}, bf16[3,208,768]{2,1,0:T(8,128)(2,1)}, u32[]{:S(2)}, u32[]{:S(2)}) collective-permute-start(bf16[3,208,768]{2,1,0:T(8,128)(2,1)S(1)} %copy-done.30), channel_id=1, source_target_pairs={{1,0},{2,1},{3,2},{5,4},{6,5},{7,6},{9,8},{10,9},{11,10},{13,12},{... | collective-permute-start | bytes 2875400 | tf_op jit(solution)/shard_map/ppermute | solution.py:510
  379.6 26.8 %collective-permute-start.43 = (bf16[384,1536]{1,0:T(8,128)(2,1)S(1)}, bf16[384,1536]{1,0:T(8,128)(2,1)S(1)}, u32[]{:S(2)}, u32[]{:S(2)}) collective-permute-start(bf16[384,1536]{1,0:T(8,128)(2,1)S(1)} %bitcast.158), channel_id=1, source_target_pairs={{0,4},{4,0},{8,12},{12,8},{16,20},{20,16},{24,28},{28,24},{1,5},{5... | collective-permute-start | bytes 3538952 | tf_op jit(solution)/shard_map/ppermute | solution.py:504
  385.4 14.2 %collective-permute-start.44 = (bf16[96,768]{1,0:T(8,128)(2,1)S(1)}, bf16[96,768]{1,0:T(8,128)(2,1)S(1)}, u32[]{:S(2)}, u32[]{:S(2)}) collective-permute-start(bf16[96,768]{1,0:T(8,128)(2,1)S(1)} %get-tuple-element.401), channel_id=1, source_target_pairs={{0,8},{4,12},{8,0},{12,4},{16,24},{20,28},{24,16},{28,20},{1,9},{5... | collective-permute-start | bytes 442376 | tf_op jit(solution)/shard_map/ppermute | solution.py:504
  385.7 14.0 %collective-permute-start.45 = (bf16[96,768]{1,0:T(8,128)(2,1)S(1)}, bf16[96,768]{1,0:T(8,128)(2,1)S(1)}, u32[]{:S(2)}, u32[]{:S(2)}) collective-permute-start(bf16[96,768]{1,0:T(8,128)(2,1)S(1)} %get-tuple-element.402), channel_id=1, source_target_pairs={{0,16},{4,20},{8,24},{12,28},{16,0},{20,4},{24,8},{28,12},{1,17},{... | collective-permute-start | bytes 442376 | tf_op jit(solution)/shard_map/ppermute | solution.py:504
  387.5 12.2 %collective-permute-start.46 = (bf16[96,768]{1,0:T(8,128)(2,1)S(1)}, bf16[96,768]{1,0:T(8,128)(2,1)S(1)}, u32[]{:S(2)}, u32[]{:S(2)}) collective-permute-start(bf16[96,768]{1,0:T(8,128)(2,1)S(1)} %get-tuple-element.403), channel_id=1, source_target_pairs={{0,24},{4,28},{8,16},{12,20},{16,8},{20,12},{24,0},{28,4},{1,25},{... | collective-permute-start | bytes 442376 | tf_op jit(solution)/shard_map/ppermute | solution.py:504
  409.3 14.3 %collective-permute-start.51 = (bf16[96,768]{1,0:T(8,128)(2,1)}, bf16[96,768]{1,0:T(8,128)(2,1)}, u32[]{:S(2)}, u32[]{:S(2)}) collective-permute-start(bf16[96,768]{1,0:T(8,128)(2,1)} %add_convert_fusion.9), channel_id=1, source_target_pairs={{0,16},{4,20},{8,24},{12,28},{16,0},{20,4},{24,8},{28,12},{1,17},{... | collective-permute-start | bytes 442376 | tf_op jit(solution)/shard_map/ppermute | solution.py:504
  412.3 11.3 %collective-permute-start.52 = (bf16[96,768]{1,0:T(8,128)(2,1)}, bf16[96,768]{1,0:T(8,128)(2,1)S(1)}, u32[]{:S(2)}, u32[]{:S(2)}) collective-permute-start(bf16[96,768]{1,0:T(8,128)(2,1)} %add_convert_fusion.9), channel_id=1, source_target_pairs={{0,24},{4,28},{8,16},{12,20},{16,8},{20,12},{24,0},{28,4},{1,25},{... | collective-permute-start | bytes 442376 | tf_op jit(solution)/shard_map/ppermute | solution.py:504
  430.7 17.8 %collective-permute-start.53 = (bf16[384,768]{1,0:T(8,128)(2,1)S(1)}, bf16[384,768]{1,0:T(8,128)(2,1)S(1)}, u32[]{:S(2)}, u32[]{:S(2)}) collective-permute-start(bf16[384,768]{1,0:T(8,128)(2,1)S(1)} %bitcast.161), channel_id=1, source_target_pairs={{0,4},{4,0},{8,12},{12,8},{16,20},{20,16},{24,28},{28,24},{1,5},{5... | collective-permute-start | bytes 1769480 | tf_op jit(solution)/shard_map/ppermute | solution.py:504
  432.9 12.8 %collective-permute-start.57 = (f32[84,128]{1,0:T(8,128)}, f32[84,128]{1,0:T(8,128)}, u32[]{:S(2)}, u32[]{:S(2)}) collective-permute-start(f32[84,128]{1,0:T(8,128)} %add_add_fusion), channel_id=1, source_target_pairs={{0,4},{4,0},{8,12},{12,8},{16,20},{20,16},{24,28},{28,24},{1,5},{5... | collective-permute-start | bytes 129032 | tf_op jit(solution)/shard_map/ppermute | solution.py:504
  (41 other events, 311.2 us)

commit v2 on v1

--- a/solution.py
+++ b/solution.py
@@ -654,7 +654,8 @@
     for bits in groups:
         heads_blocks = arrange_blocks(exchange(heads_blocks, bits), bits)
     feed_blocks = jnp.concatenate([up_weight, down_weight.T], axis=1)[None]
-    heads_blocks, feed_blocks = tie(heads_blocks, feed_blocks)
+    heads_blocks, feed_blocks, *biases = tie(heads_blocks, feed_blocks, *qv_biases, *up_biases)
+    qv_biases, up_biases = biases[:narrow_size], biases[narrow_size:]
     for bits in groups[:-1]:
         feed_blocks = arrange_blocks(exchange(feed_blocks, bits), bits)
     feed_parts = exchange(feed_blocks, groups[-1])
@@ -697,8 +698,7 @@
         return attend(offset, window_normed, [piece], qv_biases[at], bounds, own, before)
 
     heads_low, heads_high = halves(heads_all)
-    window_normed, heads_low, *biases = tie(window_normed, heads_low, *qv_biases, *up_biases)
-    qv_biases, up_biases = biases[:narrow_size], biases[narrow_size:]
+    window_normed, heads_low = tie(window_normed, heads_low)
     heads_near = swap(heads_own, "narrow", 1)
     far_low = swap(heads_low, "narrow", 2)
     mixed, saved0 = attend_on(heads_own, 0, None)

time: 458 us -> 454 us (level)
  transfers between devices with their start and end apart: 58 -> 58, of which waited for: 18 -> 17; matrix products, arithmetic and copies ran while one was open for 14% -> 14% of each run, Pallas kernels for 51% -> 51%
where the time goes in v2:
time: 454 us; the launch traced here: 448 us
  Pallas kernels  229 us (50%)
  starting transfers between devices  67.2 us (15%)
  waiting for transfers between devices  64.8 us (14%)
  other arithmetic  49 us (11%)
  local copies, waits for them, and re-layouts  36 us (8%)
    pallas_call x4, Pallas kernels, attend_back(): pl.pallas_call(partial(attend_back_kernel, own, heads, count, first, halo...  87.9 us
    ppermute x56, waiting for transfers between devices, swap(): return lax.ppermute(values_in, axis, [(i, i ^ bit) for i in range(size)])  64.8 us
    ppermute x56, starting transfers between devices, swap(): return lax.ppermute(values_in, axis, [(i, i ^ bit) for i in range(size)])  63.5 us
    pallas_call x4, Pallas kernels, attend(): pl.pallas_call(partial(attend_kernel, own, heads, count, first), grid_spe...  57.1 us
    pallas_call x4, Pallas kernels, feed_part(): pl.pallas_call(partial(feed_kernel, FEED_CHUNKS, count, first), in_specs=...  51.3 us
    pallas_call x4, Pallas kernels, rows_call(): pl.pallas_call(kernel, grid_spec=pltpu.PrefetchScalarGridSpec(num_scalar_...  33 us
    convert_element_type x10, other arithmetic, add_low(): return total.astype(bf16)  15.9 us
  transfers between devices with their start and end apart: 58, of which 17 were waited for; matrix products, arithmetic and copies ran while one was open for 14% of the time, Pallas kernels for 51%

profile of v2, /device:TPU:0, one launch (start us, length us, event | category | flops | bytes accessed | tf_op | source)
XLA Modules:
  0.0 448.0 jit_solution(16020559324112337689)
XLA Ops:
  2.5 5.1 %collective-permute-start = (bf16[1,96,768]{2,1,0:T(8,128)(2,1)S(1)}, bf16[1,96,768]{2,1,0:T(8,128)(2,1)S(1)}, u32[]{:S(2)}, u32[]{:S(2)}) collective-permute-start(bf16[1,96,768]{2,1,0:T(8,128)(2,1)S(1)} %maximum_bitcast_fusion.2), channel_id=1, source_target_pairs={{0,24},{4,28},{8,16},{12,20},{16,8},{20,12},{24,0},{28,4},{1,25},{... | collective-permute-start | bytes 442376 | tf_op jit(solution)/shard_map/ppermute | solution.py:504
  9.8 1.7 collective-permute-start.4
  17.4 2.7 collective-permute-done.1
  23.5 8.1 %first_norm.1 = (bf16[3,768,768]{2,1,0:T(8,128)(2,1)}, bf16[3,320,768]{2,1,0:T(8,128)(2,1)}) custom-call(s32[3]{0:T(128)} %pad_add_fusion.place_ref, bf16[3,1280,768]{2,1,0:T(8,128)(2,1)} %x_ref.5, bf16[3,1280,768]{2,1,0:T(8,128)(2,1)} %c_ref.3, f32[8,768]{1,0:T(8,128)} %stack.117.vec_ref), custom_call_target="tpu_custom_call" | custom-call | flops 1024 | bytes 1024 | tf_op jit(solution)/shard_map/first_norm/pallas_call | solution.py:426
  31.9 3.2 collective-permute-done.6
  38.6 1.7 collective-permute-start.11
  43.5 11.3 %attend.4 = (f32[3,320,768]{2,1,0:T(8,128)}, bf16[3,320,192]{2,1,0:T(8,128)(2,1)}, bf16[3,768,192]{2,1,0:T(8,128)(2,1)}, bf16[3,768,192]{2,1,0:T(8,128)(2,1)}, b...) custom-call(s32[1]{0:T(128)} %bitcast.off_ref, bf16[3,768,768]{2,1,0:T(8,128)(2,1)} %get-tuple-element.219.refs_0_, ...), custom_call_target="tpu_custom_call" | custom-call | flops 1024 | bytes 1024 | tf_op jit(solution)/shard_map/attend/pallas_call | solution.py:150
  54.8 3.2 collective-permute-done.10
  65.6 11.7 %attend.5 = (f32[3,320,768]{2,1,0:T(8,128)}, bf16[3,320,192]{2,1,0:T(8,128)(2,1)}, bf16[3,768,192]{2,1,0:T(8,128)(2,1)}, bf16[3,768,192]{2,1,0:T(8,128)(2,1)}, b...) custom-call(s32[1]{0:T(128)} %bitcast.off_ref, bf16[3,768,768]{2,1,0:T(8,128)(2,1)} %get-tuple-element.219.refs_0_, ...), custom_call_target="tpu_custom_call" | custom-call | flops 1024 | bytes 1024 | tf_op jit(solution)/shard_map/attend/pallas_call | solution.py:150
  81.1 11.7 %attend.6 = (f32[3,320,768]{2,1,0:T(8,128)}, bf16[3,320,192]{2,1,0:T(8,128)(2,1)}, bf16[3,768,192]{2,1,0:T(8,128)(2,1)}, bf16[3,768,192]{2,1,0:T(8,128)(2,1)}, b...) custom-call(s32[1]{0:T(128)} %bitcast.off_ref, bf16[3,768,768]{2,1,0:T(8,128)(2,1)} %get-tuple-element.219.refs_0_, ...), custom_call_target="tpu_custom_call" | custom-call | flops 1024 | bytes 1024 | tf_op jit(solution)/shard_map/attend/pallas_call | solution.py:150
  95.8 22.4 %attend.7 = (f32[3,320,768]{2,1,0:T(8,128)}, bf16[3,320,192]{2,1,0:T(8,128)(2,1)}, bf16[3,768,192]{2,1,0:T(8,128)(2,1)}, bf16[3,768,192]{2,1,0:T(8,128)(2,1)}, b...) custom-call(s32[1]{0:T(128)} %bitcast.off_ref, bf16[3,768,768]{2,1,0:T(8,128)(2,1)} %get-tuple-element.219.refs_0_, ...), custom_call_target="tpu_custom_call" | custom-call | flops 1024 | bytes 1024 | tf_op jit(solution)/shard_map/attend/pallas_call | solution.py:150
  118.2 6.0 %second_norm.1 = (f32[3,320,768]{2,1,0:T(8,128)}, bf16[3,320,768]{2,1,0:T(8,128)(2,1)}) custom-call(s32[3]{0:T(128)} %pad_add_fusion.place_ref, f32[3,320,768]{2,1,0:T(8,128)} %get-tuple-element.251.mixed_ref, bf16[3,1280,768]{2,1,0:T(8,128)(2,1)} %x_ref.5, f32[8,768]{1,0:T(8,128)} %stack.117.vec_ref), custom_call_target="tpu_custom_call" | custom-call | flops 1024 | bytes 1024 | tf_op jit(solution)/shard_map/second_norm/pallas_call | solution.py:426
  125.7 11.5 %feed_part.4 = (f32[960,768]{1,0:T(8,128)}, f32[960,768]{1,0:T(8,128)}, bf16[768,1536]{1,0:T(8,128)(2,1)}, f32[1,768]{1,0:T(1,128)}) custom-call(bf16[960,768]{1,0:T(8,128)(2,1)} %bitcast.141, bf16[960,768]{1,0:T(8,128)(2,1)} %bitcast.137, bf16[768,1536]{1,0:T(8,128)(2,1)} %bitcast.152, f32[1,768]{1,0:T(1,128)} %reshape.808.refs_3_), custom_call_target="tpu_custom_call" | custom-call | flops 1024 | bytes 1024 | tf_op jit(solution)/shard_map/feed_part/pallas_call | solution.py:370
  137.2 2.5 collective-permute-done.19
  141.1 13.2 %feed_part.5 = (f32[960,768]{1,0:T(8,128)}, f32[960,768]{1,0:T(8,128)}, bf16[768,1536]{1,0:T(8,128)(2,1)}, f32[1,768]{1,0:T(1,128)}) custom-call(bf16[960,768]{1,0:T(8,128)(2,1)} %bitcast.142, bf16[960,768]{1,0:T(8,128)(2,1)} %bitcast.138, bf16[768,1536]{1,0:T(8,128)(2,1)} %collective-permute-done.18.refs_2_, ...), custom_call_target="tpu_custom_call", output_to_operand_aliasing={{0}: (4, {}), {1}: (5, {})} | custom-call | flops 1024 | bytes 1024 | tf_op jit(solution)/shard_map/feed_part/pallas_call | solution.py:370
  158.2 13.2 %feed_part.6 = (f32[960,768]{1,0:T(8,128)}, f32[960,768]{1,0:T(8,128)}, bf16[768,1536]{1,0:T(8,128)(2,1)}, f32[1,768]{1,0:T(1,128)}) custom-call(bf16[960,768]{1,0:T(8,128)(2,1)} %bitcast.143, bf16[960,768]{1,0:T(8,128)(2,1)} %bitcast.139, bf16[768,1536]{1,0:T(8,128)(2,1)} %bitcast.155, ...), custom_call_target="tpu_custom_call", output_to_operand_aliasing={{0}: (4, {}), {1}: (5, {})} | custom-call | flops 1024 | bytes 1024 | tf_op jit(solution)/shard_map/feed_part/pallas_call | solution.py:370
  171.3 3.0 add_convert_fusion.1
  177.0 13.4 %feed_part.7 = (f32[960,768]{1,0:T(8,128)}, f32[960,768]{1,0:T(8,128)}, bf16[768,1536]{1,0:T(8,128)(2,1)}, f32[1,768]{1,0:T(1,128)}) custom-call(bf16[960,768]{1,0:T(8,128)(2,1)} %bitcast.144, bf16[960,768]{1,0:T(8,128)(2,1)} %bitcast.140, bf16[768,1536]{1,0:T(8,128)(2,1)} %collective-permute-done.21.refs_2_, ...), custom_call_target="tpu_custom_call", output_to_operand_aliasing={{0}: (4, {}), {1}: (5, {})} | custom-call | flops 1024 | bytes 1024 | tf_op jit(solution)/shard_map/feed_part/pallas_call | solution.py:370
  191.9 10.6 %second_back.1 = (bf16[3,320,768]{2,1,0:T(8,128)(2,1)}, f32[3,320,768]{2,1,0:T(8,128)}, bf16[3,320,768]{2,1,0:T(8,128)(2,1)}, f32[8,768]{1,0:T(8,128)}) custom-call(s32[3]{0:T(128)} %pad_add_fusion.place_ref, f32[3,320,768]{2,1,0:T(8,128)} %bitcast.135, f32[3,320,768]{2,1,0:T(8,128)} %bitcast.136, f32[3,320,768]{2,1,0:T(8,128)} %get-tuple-element.294.m_ref, ...), custom_call_target="tpu_custom_call" | custom-call | flops 1024 | bytes 1024 | tf_op jit(solution)/shard_map/second_back/pallas_call | solution.py:426
  202.5 4.1 collective-permute-done.24
  206.5 2.3 add_convert_fusion
  213.5 21.2 %attend_back.4 = (f32[3,768,768]{2,1,0:T(8,128)}, bf16[768,768]{1,0:T(8,128)(2,1)}, f32[1,768]{1,0:T(1,128)}) custom-call(s32[1]{0:T(128)} %bitcast.off_ref, bf16[3,768,768]{2,1,0:T(8,128)(2,1)} %get-tuple-element.219.refs_0_, bf16[3,320,768]{2,1,0:T(8,128)(2,1)} %get-tuple-element.305.refs_1_, s32[3,2,2,480]{3,2,1,0:T(2,128)} %tile.10.refs_2_, ...), custom_call_target="tpu_custom_call" | custom-call | flops 1024 | bytes 1024 | tf_op jit(solution)/shard_map/attend_back/pallas_call | solution.py:285
  234.6 5.0 %collective-permute-done.27 = bf16[384,1536]{1,0:T(8,128)(2,1)S(1)} collective-permute-done((bf16[384,1536]{1,0:T(8,128)(2,1)}, bf16[384,1536]{1,0:T(8,128)(2,1)S(1)}, u32[]{:S(2)}, u32[]{:S(2)}) %collective-permute-start.27) | collective-permute-done | bytes 1179680 | tf_op jit(solution)/shard_map/ppermute | solution.py:504
  239.7 6.0 %collective-permute-done.26 = bf16[3,320,768]{2,1,0:T(8,128)(2,1)} collective-permute-done((bf16[3,320,768]{2,1,0:T(8,128)(2,1)}, bf16[3,320,768]{2,1,0:T(8,128)(2,1)}, u32[]{:S(2)}, u32[]{:S(2)}) %collective-permute-start.26) | collective-permute-done | bytes 1474592 | tf_op jit(solution)/shard_map/ppermute | solution.py:504
  248.2 22.0 %attend_back.5 = (f32[3,768,768]{2,1,0:T(8,128)}, bf16[768,768]{1,0:T(8,128)(2,1)}, f32[1,768]{1,0:T(1,128)}) custom-call(s32[1]{0:T(128)} %bitcast.off_ref, bf16[3,768,768]{2,1,0:T(8,128)(2,1)} %get-tuple-element.219.refs_0_, bf16[3,320,768]{2,1,0:T(8,128)(2,1)} %get-tuple-element.305.refs_1_, s32[3,2,2,480]{3,2,1,0:T(2,128)} %tile.10.refs_2_, ...), custom_call_target="tpu_custom_call" | custom-call | flops 1024 | bytes 1024 | tf_op jit(solution)/shard_map/attend_back/pallas_call | solution.py:285
  270.2 5.5 %collective-permute-done.28 = bf16[384,1536]{1,0:T(8,128)(2,1)} collective-permute-done((bf16[384,1536]{1,0:T(8,128)(2,1)}, bf16[384,1536]{1,0:T(8,128)(2,1)}, u32[]{:S(2)}, u32[]{:S(2)}) %collective-permute-start.28) | collective-permute-done | bytes 1179680 | tf_op jit(solution)/shard_map/ppermute | solution.py:504
  288.2 8.1 %collective-permute-start.33 = (bf16[96,1536]{1,0:T(8,128)(2,1)}, bf16[96,1536]{1,0:T(8,128)(2,1)}, u32[]{:S(2)}, u32[]{:S(2)}) collective-permute-start(bf16[96,1536]{1,0:T(8,128)(2,1)} %get-tuple-element.346), channel_id=1, source_target_pairs={{0,8},{4,12},{8,0},{12,4},{16,24},{20,28},{24,16},{28,20},{1,9},{5... | collective-permute-start | bytes 884744 | tf_op jit(solution)/shard_map/ppermute | solution.py:504
  296.4 2.4 collective-permute-start.35
  301.5 22.3 %attend_back.6 = (f32[3,768,768]{2,1,0:T(8,128)}, bf16[768,768]{1,0:T(8,128)(2,1)}, f32[1,768]{1,0:T(1,128)}) custom-call(s32[1]{0:T(128)} %bitcast.off_ref, bf16[3,768,768]{2,1,0:T(8,128)(2,1)} %get-tuple-element.219.refs_0_, bf16[3,320,768]{2,1,0:T(8,128)(2,1)} %get-tuple-element.305.refs_1_, s32[3,2,2,480]{3,2,1,0:T(2,128)} %tile.10.refs_2_, ...), custom_call_target="tpu_custom_call" | custom-call | flops 1024 | bytes 1024 | tf_op jit(solution)/shard_map/attend_back/pallas_call | solution.py:285
  330.0 2.4 collective-permute-start.38
  332.4 22.4 %attend_back.7 = (f32[3,768,768]{2,1,0:T(8,128)}, bf16[768,768]{1,0:T(8,128)(2,1)}, f32[1,768]{1,0:T(1,128)}, bf16[3,208,768]{2,1,0:T(8,128)(2,1)}, bf16[3,208,768]{2,1,0:T(8,128)(2,1)}) custom-call(s32[1]{0:T(128)} %bitcast.off_ref, bf16[3,768,768]{2,1,0:T(8,128)(2,1)} %get-tuple-element.219.refs_0_, bf16[3,320,768]{2,1,0:T(8,128)(2,1)} %get-tuple-element.305.refs_1_, ...), custom_call_target="tpu_custom_call" | custom-call | flops 1024 | bytes 1024 | tf_op jit(solution)/shard_map/attend_back/pallas_call | solution.py:285
  355.8 2.4 add_convert_fusion.2
  360.9 2.4 collective-permute-start.40
  367.5 2.0 select_bitcast_fusion.1
  369.5 5.9 %collective-permute-done.42 = bf16[384,768]{1,0:T(8,128)(2,1)S(1)} collective-permute-done((bf16[384,768]{1,0:T(8,128)(2,1)S(1)}, bf16[384,768]{1,0:T(8,128)(2,1)S(1)}, u32[]{:S(2)}, u32[]{:S(2)}) %collective-permute-start.42) | collective-permute-done | bytes 589856 | tf_op jit(solution)/shard_map/ppermute | solution.py:504
  377.1 3.0 copy.60
  380.6 1.8 collective-permute-start.45
  382.4 2.4 collective-permute-start.46
  384.8 8.3 %first_back.1 = (bf16[3,320,768]{2,1,0:T(8,128)(2,1)}, f32[8,768]{1,0:T(8,128)}) custom-call(s32[3]{0:T(128)} %pad_add_fusion.place_ref, f32[3,768,768]{2,1,0:T(8,128)} %get-tuple-element.385.win_ref, bf16[3,208,768]{2,1,0:T(8,128)(2,1)} %collective-permute-done.40.left_ref, bf16[3,208,768]{2,1,0:T(8,128)(2,1)} %collective-permute-done.41.right_ref, ...), custom_call_target="tpu_custom_call" | custom-call | flops 1024 | bytes 1024 | tf_op jit(solution)/shard_map/first_back/pallas_call | solution.py:426
  394.6 7.7 %collective-permute-done.43 = bf16[384,1536]{1,0:T(8,128)(2,1)S(1)} collective-permute-done((bf16[384,1536]{1,0:T(8,128)(2,1)S(1)}, bf16[384,1536]{1,0:T(8,128)(2,1)S(1)}, u32[]{:S(2)}, u32[]{:S(2)}) %collective-permute-start.43) | collective-permute-done | bytes 1179680 | tf_op jit(solution)/shard_map/ppermute | solution.py:504
  405.1 1.8 collective-permute-start.51
  408.1 2.4 collective-permute-start.52
  411.4 1.9 collective-permute-done.50
  413.2 6.1 %collective-permute-done.51 = bf16[96,768]{1,0:T(8,128)(2,1)} collective-permute-done((bf16[96,768]{1,0:T(8,128)(2,1)}, bf16[96,768]{1,0:T(8,128)(2,1)}, u32[]{:S(2)}, u32[]{:S(2)}) %collective-permute-start.51) | collective-permute-done | bytes 147488 | tf_op jit(solution)/shard_map/ppermute | solution.py:504
  419.4 2.7 collective-permute-start.54
  422.1 2.3 collective-permute-start.56
  431.5 1.8 copy.63
  433.3 8.2 %collective-permute-done.57 = f32[84,128]{1,0:T(8,128)} collective-permute-done((f32[84,128]{1,0:T(8,128)}, f32[84,128]{1,0:T(8,128)}, u32[]{:S(2)}, u32[]{:S(2)}) %collective-permute-start.57) | collective-permute-done | bytes 43040 | tf_op jit(solution)/shard_map/ppermute | solution.py:504
  (282 shorter events, 103.6 us)
Async XLA Ops:
  2.5 14.9 %collective-permute-start = (bf16[1,96,768]{2,1,0:T(8,128)(2,1)S(1)}, bf16[1,96,768]{2,1,0:T(8,128)(2,1)S(1)}, u32[]{:S(2)}, u32[]{:S(2)}) collective-permute-start(bf16[1,96,768]{2,1,0:T(8,128)(2,1)S(1)} %maximum_bitcast_fusion.2), channel_id=1, source_target_pairs={{0,24},{4,28},{8,16},{12,20},{16,8},{20,12},{24,0},{28,4},{1,25},{... | collective-permute-start | bytes 442376 | tf_op jit(solution)/shard_map/ppermute | solution.py:504
  7.7 12.5 %collective-permute-start.1 = (bf16[1,96,768]{2,1,0:T(8,128)(2,1)S(1)}, bf16[1,96,768]{2,1,0:T(8,128)(2,1)S(1)}, u32[]{:S(2)}, u32[]{:S(2)}) collective-permute-start(bf16[1,96,768]{2,1,0:T(8,128)(2,1)S(1)} %maximum_bitcast_fusion.2), channel_id=1, source_target_pairs={{0,16},{4,20},{8,24},{12,28},{16,0},{20,4},{24,8},{28,12},{1,17},{... | collective-permute-start | bytes 442376 | tf_op jit(solution)/shard_map/ppermute | solution.py:504
  7.7 12.5 %collective-permute-start.2 = (bf16[1,96,768]{2,1,0:T(8,128)(2,1)S(1)}, bf16[1,96,768]{2,1,0:T(8,128)(2,1)S(1)}, u32[]{:S(2)}, u32[]{:S(2)}) collective-permute-start(bf16[1,96,768]{2,1,0:T(8,128)(2,1)S(1)} %maximum_bitcast_fusion.2), channel_id=1, source_target_pairs={{0,8},{4,12},{8,0},{12,4},{16,24},{20,28},{24,16},{28,20},{1,9},{5... | collective-permute-start | bytes 442376 | tf_op jit(solution)/shard_map/ppermute | solution.py:504
  20.6 14.5 %collective-permute-start.6 = (bf16[4,96,768]{2,1,0:T(8,128)(2,1)S(1)}, bf16[4,96,768]{2,1,0:T(8,128)(2,1)S(1)}, u32[]{:S(2)}, u32[]{:S(2)}) collective-permute-start(bf16[4,96,768]{2,1,0:T(8,128)(2,1)S(1)} %maximum_bitcast_fusion), channel_id=1, source_target_pairs={{0,4},{4,0},{8,12},{12,8},{16,20},{20,16},{24,28},{28,24},{1,5},{5... | collective-permute-start | bytes 1769480 | tf_op jit(solution)/shard_map/ppermute | solution.py:504
  36.2 23.2 %collective-permute-start.8 = (bf16[4,96,768]{2,1,0:T(8,128)(2,1)}, bf16[4,96,768]{2,1,0:T(8,128)(2,1)S(1)}, u32[]{:S(2)}, u32[]{:S(2)}) collective-permute-start(bf16[4,96,768]{2,1,0:T(8,128)(2,1)} %bitcast.23), channel_id=1, source_target_pairs={{0,2},{1,3},{2,0},{3,1},{4,6},{5,7},{6,4},{7,5},{8,10},{9,11},{10,... | collective-permute-start | bytes 1769480 | tf_op jit(solution)/shard_map/ppermute | solution.py:504
  37.9 20.2 %collective-permute-start.10 = (bf16[1,96,1536]{2,1,0:T(8,128)(2,1)S(1)}, bf16[1,96,1536]{2,1,0:T(8,128)(2,1)S(1)}, u32[]{:S(2)}, u32[]{:S(2)}) collective-permute-start(bf16[1,96,1536]{2,1,0:T(8,128)(2,1)S(1)} %maximum_bitcast_fusion.1), channel_id=1, source_target_pairs={{0,16},{4,20},{8,24},{12,28},{16,0},{20,4},{24,8},{28,12},{1,17},{... | collective-permute-start | bytes 884744 | tf_op jit(solution)/shard_map/ppermute | solution.py:504
  38.6 19.4 %collective-permute-start.11 = (bf16[1,96,1536]{2,1,0:T(8,128)(2,1)S(1)}, bf16[1,96,1536]{2,1,0:T(8,128)(2,1)}, u32[]{:S(2)}, u32[]{:S(2)}) collective-permute-start(bf16[1,96,1536]{2,1,0:T(8,128)(2,1)S(1)} %maximum_bitcast_fusion.1), channel_id=1, source_target_pairs={{0,24},{4,28},{8,16},{12,20},{16,8},{20,12},{24,0},{28,4},{1,25},{... | collective-permute-start | bytes 884744 | tf_op jit(solution)/shard_map/ppermute | solution.py:504
  40.3 19.1 %collective-permute-start.9 = (bf16[1,96,1536]{2,1,0:T(8,128)(2,1)S(1)}, bf16[1,96,1536]{2,1,0:T(8,128)(2,1)}, u32[]{:S(2)}, u32[]{:S(2)}) collective-permute-start(bf16[1,96,1536]{2,1,0:T(8,128)(2,1)S(1)} %maximum_bitcast_fusion.1), channel_id=1, source_target_pairs={{0,8},{4,12},{8,0},{12,4},{16,24},{20,28},{24,16},{28,20},{1,9},{5... | collective-permute-start | bytes 884744 | tf_op jit(solution)/shard_map/ppermute | solution.py:504
  42.5 22.1 %collective-permute-start.7 = (bf16[768,768]{1,0:T(8,128)(2,1)S(1)}, bf16[768,768]{1,0:T(8,128)(2,1)S(1)}, u32[]{:S(2)}, u32[]{:S(2)}) collective-permute-start(bf16[768,768]{1,0:T(8,128)(2,1)S(1)} %bitcast.145), channel_id=1, source_target_pairs={{0,1},{1,0},{2,3},{3,2},{4,5},{5,4},{6,7},{7,6},{8,9},{9,8},{10,11... | collective-permute-start | bytes 3538952 | tf_op jit(solution)/shard_map/ppermute | solution.py:504
  62.6 14.7 %collective-permute-start.12 = (bf16[4,96,768]{2,1,0:T(8,128)(2,1)}, bf16[4,96,768]{2,1,0:T(8,128)(2,1)}, u32[]{:S(2)}, u32[]{:S(2)}) collective-permute-start(bf16[4,96,768]{2,1,0:T(8,128)(2,1)} %bitcast.26), channel_id=1, source_target_pairs={{0,2},{1,3},{2,0},{3,1},{4,6},{5,7},{6,4},{7,5},{8,10},{9,11},{10,... | collective-permute-start | bytes 1769480 | tf_op jit(solution)/shard_map/ppermute | solution.py:504
  63.1 14.2 %collective-permute-start.13 = (bf16[2,96,1536]{2,1,0:T(8,128)(2,1)S(1)}, bf16[2,96,1536]{2,1,0:T(8,128)(2,1)S(1)}, u32[]{:S(2)}, u32[]{:S(2)}) collective-permute-start(bf16[2,96,1536]{2,1,0:T(8,128)(2,1)S(1)} %get-tuple-element.244), channel_id=1, source_target_pairs={{0,4},{4,0},{8,12},{12,8},{16,20},{20,16},{24,28},{28,24},{1,5},{5... | collective-permute-start | bytes 1769480 | tf_op jit(solution)/shard_map/ppermute | solution.py:504
  78.7 14.0 %collective-permute-start.15 = (bf16[2,96,1536]{2,1,0:T(8,128)(2,1)}, bf16[2,96,1536]{2,1,0:T(8,128)(2,1)S(1)}, u32[]{:S(2)}, u32[]{:S(2)}) collective-permute-start(bf16[2,96,1536]{2,1,0:T(8,128)(2,1)} %get-tuple-element.250), channel_id=1, source_target_pairs={{0,4},{4,0},{8,12},{12,8},{16,20},{20,16},{24,28},{28,24},{1,5},{5... | collective-permute-start | bytes 1769480 | tf_op jit(solution)/shard_map/ppermute | solution.py:504
  79.6 13.1 %collective-permute-start.16 = (bf16[2,96,1536]{2,1,0:T(8,128)(2,1)S(1)}, bf16[2,96,1536]{2,1,0:T(8,128)(2,1)S(1)}, u32[]{:S(2)}, u32[]{:S(2)}) collective-permute-start(bf16[2,96,1536]{2,1,0:T(8,128)(2,1)S(1)} %get-tuple-element.244), channel_id=1, source_target_pairs={{0,2},{1,3},{2,0},{3,1},{4,6},{5,7},{6,4},{7,5},{8,10},{9,11},{10,... | collective-permute-start | bytes 1769480 | tf_op jit(solution)/shard_map/ppermute | solution.py:504
  81.0 14.8 %collective-permute-start.14 = (bf16[768,768]{1,0:T(8,128)(2,1)S(1)}, bf16[768,768]{1,0:T(8,128)(2,1)}, u32[]{:S(2)}, u32[]{:S(2)}) collective-permute-start(bf16[768,768]{1,0:T(8,128)(2,1)S(1)} %bitcast.148), channel_id=1, source_target_pairs={{0,1},{1,0},{2,3},{3,2},{4,5},{5,4},{6,7},{7,6},{8,9},{9,8},{10,11... | collective-permute-start | bytes 3538952 | tf_op jit(solution)/shard_map/ppermute | solution.py:504
  94.7 46.4 %collective-permute-start.18 = (bf16[768,1536]{1,0:T(8,128)(2,1)S(1)}, bf16[768,1536]{1,0:T(8,128)(2,1)}, u32[]{:S(2)}, u32[]{:S(2)}) collective-permute-start(bf16[768,1536]{1,0:T(8,128)(2,1)S(1)} %bitcast.151), channel_id=1, source_target_pairs={{0,1},{1,0},{2,3},{3,2},{4,5},{5,4},{6,7},{7,6},{8,9},{9,8},{10,11... | collective-permute-start | bytes 7077896 | tf_op jit(solution)/shard_map/ppermute | solution.py:504
  95.3 23.0 %collective-permute-start.17 = (bf16[2,96,1536]{2,1,0:T(8,128)(2,1)}, bf16[2,96,1536]{2,1,0:T(8,128)(2,1)}, u32[]{:S(2)}, u32[]{:S(2)}) collective-permute-start(bf16[2,96,1536]{2,1,0:T(8,128)(2,1)} %get-tuple-element.250), channel_id=1, source_target_pairs={{0,2},{1,3},{2,0},{3,1},{4,6},{5,7},{6,4},{7,5},{8,10},{9,11},{10,... | collective-permute-start | bytes 1769480 | tf_op jit(solution)/shard_map/ppermute | solution.py:504
  124.2 15.4 %collective-permute-start.19 = (bf16[2,96,1536]{2,1,0:T(8,128)(2,1)S(1)}, bf16[2,96,1536]{2,1,0:T(8,128)(2,1)S(1)}, u32[]{:S(2)}, u32[]{:S(2)}) collective-permute-start(bf16[2,96,1536]{2,1,0:T(8,128)(2,1)S(1)} %copy-done.8), channel_id=1, source_target_pairs={{0,4},{4,0},{8,12},{12,8},{16,20},{20,16},{24,28},{28,24},{1,5},{5... | collective-permute-start | bytes 1769480 | tf_op jit(solution)/shard_map/ppermute | solution.py:504
  139.6 14.9 %collective-permute-start.20 = (bf16[2,96,1536]{2,1,0:T(8,128)(2,1)}, bf16[2,96,1536]{2,1,0:T(8,128)(2,1)}, u32[]{:S(2)}, u32[]{:S(2)}) collective-permute-start(bf16[2,96,1536]{2,1,0:T(8,128)(2,1)} %collective-permute-done.17), channel_id=1, source_target_pairs={{0,4},{4,0},{8,12},{12,8},{16,20},{20,16},{24,28},{28,24},{1,5},{5... | collective-permute-start | bytes 1769480 | tf_op jit(solution)/shard_map/ppermute | solution.py:504
  156.8 14.6 %collective-permute-start.22 = (bf16[768,1536]{1,0:T(8,128)(2,1)}, bf16[768,1536]{1,0:T(8,128)(2,1)}, u32[]{:S(2)}, u32[]{:S(2)}) collective-permute-start(bf16[768,1536]{1,0:T(8,128)(2,1)} %get-tuple-element.280), channel_id=1, source_target_pairs={{0,1},{1,0},{2,3},{3,2},{4,5},{5,4},{6,7},{7,6},{8,9},{9,8},{10,11... | collective-permute-start | bytes 7077896 | tf_op jit(solution)/shard_map/ppermute | solution.py:504
  156.8 20.2 %collective-permute-start.21 = (bf16[768,1536]{1,0:T(8,128)(2,1)S(1)}, bf16[768,1536]{1,0:T(8,128)(2,1)}, u32[]{:S(2)}, u32[]{:S(2)}) collective-permute-start(bf16[768,1536]{1,0:T(8,128)(2,1)S(1)} %bitcast.154), channel_id=1, source_target_pairs={{0,1},{1,0},{2,3},{3,2},{4,5},{5,4},{6,7},{7,6},{8,9},{9,8},{10,11... | collective-permute-start | bytes 7077896 | tf_op jit(solution)/shard_map/ppermute | solution.py:504
  175.5 14.9 %collective-permute-start.23 = (bf16[384,768]{1,0:T(8,128)(2,1)}, bf16[384,768]{1,0:T(8,128)(2,1)}, u32[]{:S(2)}, u32[]{:S(2)}) collective-permute-start(bf16[384,768]{1,0:T(8,128)(2,1)} %get-tuple-element.289), channel_id=1, source_target_pairs={{0,4},{4,0},{8,12},{12,8},{16,20},{20,16},{24,28},{28,24},{1,5},{5... | collective-permute-start | bytes 1769480 | tf_op jit(solution)/shard_map/ppermute | solution.py:504
  190.4 16.1 %collective-permute-start.25 = (bf16[768,1536]{1,0:T(8,128)(2,1)}, bf16[768,1536]{1,0:T(8,128)(2,1)}, u32[]{:S(2)}, u32[]{:S(2)}) collective-permute-start(bf16[768,1536]{1,0:T(8,128)(2,1)} %get-tuple-element.297), channel_id=1, source_target_pairs={{0,1},{1,0},{2,3},{3,2},{4,5},{5,4},{6,7},{7,6},{8,9},{9,8},{10,11... | collective-permute-start | bytes 7077896 | tf_op jit(solution)/shard_map/ppermute | solution.py:504
  190.5 16.0 %collective-permute-start.24 = (bf16[384,768]{1,0:T(8,128)(2,1)}, bf16[384,768]{1,0:T(8,128)(2,1)}, u32[]{:S(2)}, u32[]{:S(2)}) collective-permute-start(bf16[384,768]{1,0:T(8,128)(2,1)} %get-tuple-element.296), channel_id=1, source_target_pairs={{0,4},{4,0},{8,12},{12,8},{16,20},{20,16},{24,28},{28,24},{1,5},{5... | collective-permute-start | bytes 1769480 | tf_op jit(solution)/shard_map/ppermute | solution.py:504
  211.5 34.2 %collective-permute-start.26 = (bf16[3,320,768]{2,1,0:T(8,128)(2,1)}, bf16[3,320,768]{2,1,0:T(8,128)(2,1)}, u32[]{:S(2)}, u32[]{:S(2)}) collective-permute-start(bf16[3,320,768]{2,1,0:T(8,128)(2,1)} %get-tuple-element.374), channel_id=1, source_target_pairs={{0,2},{1,3},{2,0},{3,1},{4,6},{5,7},{6,4},{7,5},{8,10},{9,11},{10,... | collective-permute-start | bytes 4423688 | tf_op jit(solution)/shard_map/ppermute | solution.py:504
  212.2 27.5 %collective-permute-start.27 = (bf16[384,1536]{1,0:T(8,128)(2,1)}, bf16[384,1536]{1,0:T(8,128)(2,1)S(1)}, u32[]{:S(2)}, u32[]{:S(2)}) collective-permute-start(bf16[384,1536]{1,0:T(8,128)(2,1)} %get-tuple-element.328), channel_id=1, source_target_pairs={{0,4},{4,0},{8,12},{12,8},{16,20},{20,16},{24,28},{28,24},{1,5},{5... | collective-permute-start | bytes 3538952 | tf_op jit(solution)/shard_map/ppermute | solution.py:504
  213.5 56.7 %collective-permute-start.30 = (bf16[3,320,768]{2,1,0:T(8,128)(2,1)}, bf16[3,320,768]{2,1,0:T(8,128)(2,1)}, u32[]{:S(2)}, u32[]{:S(2)}) collective-permute-start(bf16[3,320,768]{2,1,0:T(8,128)(2,1)} %get-tuple-element.374), channel_id=1, source_target_pairs={{0,1},{1,0},{2,3},{3,2},{4,5},{5,4},{6,7},{7,6},{8,9},{9,8},{10,11... | collective-permute-start | bytes 4423688 | tf_op jit(solution)/shard_map/ppermute | solution.py:504
  246.9 28.7 %collective-permute-start.31 = (bf16[3,320,768]{2,1,0:T(8,128)(2,1)}, bf16[3,320,768]{2,1,0:T(8,128)(2,1)S(1)}, u32[]{:S(2)}, u32[]{:S(2)}) collective-permute-start(bf16[3,320,768]{2,1,0:T(8,128)(2,1)} %collective-permute-done.26), channel_id=1, source_target_pairs={{0,1},{1,0},{2,3},{3,2},{4,5},{5,4},{6,7},{7,6},{8,9},{9,8},{10,11... | collective-permute-start | bytes 4423688 | tf_op jit(solution)/shard_map/ppermute | solution.py:504
  246.9 23.2 %collective-permute-start.29 = (bf16[768,768]{1,0:T(8,128)(2,1)}, bf16[768,768]{1,0:T(8,128)(2,1)}, u32[]{:S(2)}, u32[]{:S(2)}) collective-permute-start(bf16[768,768]{1,0:T(8,128)(2,1)} %get-tuple-element.336), channel_id=1, source_target_pairs={{0,1},{1,0},{2,3},{3,2},{4,5},{5,4},{6,7},{7,6},{8,9},{9,8},{10,11... | collective-permute-start | bytes 3538952 | tf_op jit(solution)/shard_map/ppermute | solution.py:504
  247.5 28.2 %collective-permute-start.28 = (bf16[384,1536]{1,0:T(8,128)(2,1)}, bf16[384,1536]{1,0:T(8,128)(2,1)}, u32[]{:S(2)}, u32[]{:S(2)}) collective-permute-start(bf16[384,1536]{1,0:T(8,128)(2,1)} %add_convert_fusion.5), channel_id=1, source_target_pairs={{0,2},{1,3},{2,0},{3,1},{4,6},{5,7},{6,4},{7,5},{8,10},{9,11},{10,... | collective-permute-start | bytes 3538952 | tf_op jit(solution)/shard_map/ppermute | solution.py:504
  279.7 46.8 %collective-permute-start.32 = (bf16[768,768]{1,0:T(8,128)(2,1)S(1)}, bf16[768,768]{1,0:T(8,128)(2,1)}, u32[]{:S(2)}, u32[]{:S(2)}) collective-permute-start(bf16[768,768]{1,0:T(8,128)(2,1)S(1)} %add_convert_fusion.4), channel_id=1, source_target_pairs={{0,2},{1,3},{2,0},{3,1},{4,6},{5,7},{6,4},{7,5},{8,10},{9,11},{10,... | collective-permute-start | bytes 3538952 | tf_op jit(solution)/shard_map/ppermute | solution.py:504
  288.2 38.3 %collective-permute-start.33 = (bf16[96,1536]{1,0:T(8,128)(2,1)}, bf16[96,1536]{1,0:T(8,128)(2,1)}, u32[]{:S(2)}, u32[]{:S(2)}) collective-permute-start(bf16[96,1536]{1,0:T(8,128)(2,1)} %get-tuple-element.346), channel_id=1, source_target_pairs={{0,8},{4,12},{8,0},{12,4},{16,24},{20,28},{24,16},{28,20},{1,9},{5... | collective-permute-start | bytes 884744 | tf_op jit(solution)/shard_map/ppermute | solution.py:504
  296.3 30.2 %collective-permute-start.34 = (bf16[96,1536]{1,0:T(8,128)(2,1)S(1)}, bf16[96,1536]{1,0:T(8,128)(2,1)}, u32[]{:S(2)}, u32[]{:S(2)}) collective-permute-start(bf16[96,1536]{1,0:T(8,128)(2,1)S(1)} %get-tuple-element.347), channel_id=1, source_target_pairs={{0,16},{4,20},{8,24},{12,28},{16,0},{20,4},{24,8},{28,12},{1,17},{... | collective-permute-start | bytes 884744 | tf_op jit(solution)/shard_map/ppermute | solution.py:504
  296.4 30.2 %collective-permute-start.35 = (bf16[96,1536]{1,0:T(8,128)(2,1)S(1)}, bf16[96,1536]{1,0:T(8,128)(2,1)}, u32[]{:S(2)}, u32[]{:S(2)}) collective-permute-start(bf16[96,1536]{1,0:T(8,128)(2,1)S(1)} %get-tuple-element.348), channel_id=1, source_target_pairs={{0,24},{4,28},{8,16},{12,20},{16,8},{20,12},{24,0},{28,4},{1,25},{... | collective-permute-start | bytes 884744 | tf_op jit(solution)/shard_map/ppermute | solution.py:504
  323.8 32.0 %collective-permute-start.39 = (bf16[768,768]{1,0:T(8,128)(2,1)}, bf16[768,768]{1,0:T(8,128)(2,1)}, u32[]{:S(2)}, u32[]{:S(2)}) collective-permute-start(bf16[768,768]{1,0:T(8,128)(2,1)} %get-tuple-element.361), channel_id=1, source_target_pairs={{0,1},{1,0},{2,3},{3,2},{4,5},{5,4},{6,7},{7,6},{8,9},{9,8},{10,11... | collective-permute-start | bytes 3538952 | tf_op jit(solution)/shard_map/ppermute | solution.py:504
  327.9 32.4 %collective-permute-start.36 = (bf16[96,1536]{1,0:T(8,128)(2,1)S(1)}, bf16[96,1536]{1,0:T(8,128)(2,1)S(1)}, u32[]{:S(2)}, u32[]{:S(2)}) collective-permute-start(bf16[96,1536]{1,0:T(8,128)(2,1)S(1)} %add_convert_fusion.8), channel_id=1, source_target_pairs={{0,8},{4,12},{8,0},{12,4},{16,24},{20,28},{24,16},{28,20},{1,9},{5... | collective-permute-start | bytes 884744 | tf_op jit(solution)/shard_map/ppermute | solution.py:504
  329.1 31.2 %collective-permute-start.37 = (bf16[96,1536]{1,0:T(8,128)(2,1)S(1)}, bf16[96,1536]{1,0:T(8,128)(2,1)S(1)}, u32[]{:S(2)}, u32[]{:S(2)}) collective-permute-start(bf16[96,1536]{1,0:T(8,128)(2,1)S(1)} %add_convert_fusion.8), channel_id=1, source_target_pairs={{0,16},{4,20},{8,24},{12,28},{16,0},{20,4},{24,8},{28,12},{1,17},{... | collective-permute-start | bytes 884744 | tf_op jit(solution)/shard_map/ppermute | solution.py:504
  330.0 30.3 %collective-permute-start.38 = (bf16[96,1536]{1,0:T(8,128)(2,1)S(1)}, bf16[96,1536]{1,0:T(8,128)(2,1)}, u32[]{:S(2)}, u32[]{:S(2)}) collective-permute-start(bf16[96,1536]{1,0:T(8,128)(2,1)S(1)} %add_convert_fusion.8), channel_id=1, source_target_pairs={{0,24},{4,28},{8,16},{12,20},{16,8},{20,12},{24,0},{28,4},{1,25},{... | collective-permute-start | bytes 884744 | tf_op jit(solution)/shard_map/ppermute | solution.py:504
  360.3 15.1 %collective-permute-start.42 = (bf16[384,768]{1,0:T(8,128)(2,1)S(1)}, bf16[384,768]{1,0:T(8,128)(2,1)S(1)}, u32[]{:S(2)}, u32[]{:S(2)}) collective-permute-start(bf16[384,768]{1,0:T(8,128)(2,1)S(1)} %get-tuple-element.383), channel_id=1, source_target_pairs={{0,4},{4,0},{8,12},{12,8},{16,20},{20,16},{24,28},{28,24},{1,5},{5... | collective-permute-start | bytes 1769480 | tf_op jit(solution)/shard_map/ppermute | solution.py:504
  360.9 19.4 %collective-permute-start.40 = (bf16[3,208,768]{2,1,0:T(8,128)(2,1)}, bf16[3,208,768]{2,1,0:T(8,128)(2,1)}, u32[]{:S(2)}, u32[]{:S(2)}) collective-permute-start(bf16[3,208,768]{2,1,0:T(8,128)(2,1)} %get-tuple-element.376), channel_id=1, source_target_pairs={{0,1},{1,2},{2,3},{4,5},{5,6},{6,7},{8,9},{9,10},{10,11},{12,13},{... | collective-permute-start | bytes 2875400 | tf_op jit(solution)/shard_map/ppermute | solution.py:510
  363.3 17.0 %collective-permute-start.41 = (bf16[3,208,768]{2,1,0:T(8,128)(2,1)S(1)}, bf16[3,208,768]{2,1,0:T(8,128)(2,1)}, u32[]{:S(2)}, u32[]{:S(2)}) collective-permute-start(bf16[3,208,768]{2,1,0:T(8,128)(2,1)S(1)} %copy-done.30), channel_id=1, source_target_pairs={{1,0},{2,1},{3,2},{5,4},{6,5},{7,6},{9,8},{10,9},{11,10},{13,12},{... | collective-permute-start | bytes 2875400 | tf_op jit(solution)/shard_map/ppermute | solution.py:510
  375.4 26.8 %collective-permute-start.43 = (bf16[384,1536]{1,0:T(8,128)(2,1)S(1)}, bf16[384,1536]{1,0:T(8,128)(2,1)S(1)}, u32[]{:S(2)}, u32[]{:S(2)}) collective-permute-start(bf16[384,1536]{1,0:T(8,128)(2,1)S(1)} %bitcast.158), channel_id=1, source_target_pairs={{0,4},{4,0},{8,12},{12,8},{16,20},{20,16},{24,28},{28,24},{1,5},{5... | collective-permute-start | bytes 3538952 | tf_op jit(solution)/shard_map/ppermute | solution.py:504
  380.3 14.2 %collective-permute-start.44 = (bf16[96,768]{1,0:T(8,128)(2,1)S(1)}, bf16[96,768]{1,0:T(8,128)(2,1)S(1)}, u32[]{:S(2)}, u32[]{:S(2)}) collective-permute-start(bf16[96,768]{1,0:T(8,128)(2,1)S(1)} %get-tuple-element.401), channel_id=1, source_target_pairs={{0,8},{4,12},{8,0},{12,4},{16,24},{20,28},{24,16},{28,20},{1,9},{5... | collective-permute-start | bytes 442376 | tf_op jit(solution)/shard_map/ppermute | solution.py:504
  380.6 14.0 %collective-permute-start.45 = (bf16[96,768]{1,0:T(8,128)(2,1)S(1)}, bf16[96,768]{1,0:T(8,128)(2,1)S(1)}, u32[]{:S(2)}, u32[]{:S(2)}) collective-permute-start(bf16[96,768]{1,0:T(8,128)(2,1)S(1)} %get-tuple-element.402), channel_id=1, source_target_pairs={{0,16},{4,20},{8,24},{12,28},{16,0},{20,4},{24,8},{28,12},{1,17},{... | collective-permute-start | bytes 442376 | tf_op jit(solution)/shard_map/ppermute | solution.py:504
  382.4 12.2 %collective-permute-start.46 = (bf16[96,768]{1,0:T(8,128)(2,1)S(1)}, bf16[96,768]{1,0:T(8,128)(2,1)S(1)}, u32[]{:S(2)}, u32[]{:S(2)}) collective-permute-start(bf16[96,768]{1,0:T(8,128)(2,1)S(1)} %get-tuple-element.403), channel_id=1, source_target_pairs={{0,24},{4,28},{8,16},{12,20},{16,8},{20,12},{24,0},{28,4},{1,25},{... | collective-permute-start | bytes 442376 | tf_op jit(solution)/shard_map/ppermute | solution.py:504
  405.1 14.3 %collective-permute-start.51 = (bf16[96,768]{1,0:T(8,128)(2,1)}, bf16[96,768]{1,0:T(8,128)(2,1)}, u32[]{:S(2)}, u32[]{:S(2)}) collective-permute-start(bf16[96,768]{1,0:T(8,128)(2,1)} %add_convert_fusion.9), channel_id=1, source_target_pairs={{0,16},{4,20},{8,24},{12,28},{16,0},{20,4},{24,8},{28,12},{1,17},{... | collective-permute-start | bytes 442376 | tf_op jit(solution)/shard_map/ppermute | solution.py:504
  408.1 11.3 %collective-permute-start.52 = (bf16[96,768]{1,0:T(8,128)(2,1)}, bf16[96,768]{1,0:T(8,128)(2,1)S(1)}, u32[]{:S(2)}, u32[]{:S(2)}) collective-permute-start(bf16[96,768]{1,0:T(8,128)(2,1)} %add_convert_fusion.9), channel_id=1, source_target_pairs={{0,24},{4,28},{8,16},{12,20},{16,8},{20,12},{24,0},{28,4},{1,25},{... | collective-permute-start | bytes 442376 | tf_op jit(solution)/shard_map/ppermute | solution.py:504
  426.5 17.8 %collective-permute-start.53 = (bf16[384,768]{1,0:T(8,128)(2,1)S(1)}, bf16[384,768]{1,0:T(8,128)(2,1)S(1)}, u32[]{:S(2)}, u32[]{:S(2)}) collective-permute-start(bf16[384,768]{1,0:T(8,128)(2,1)S(1)} %bitcast.161), channel_id=1, source_target_pairs={{0,4},{4,0},{8,12},{12,8},{16,20},{20,16},{24,28},{28,24},{1,5},{5... | collective-permute-start | bytes 1769480 | tf_op jit(solution)/shard_map/ppermute | solution.py:504
  428.7 12.8 %collective-permute-start.57 = (f32[84,128]{1,0:T(8,128)}, f32[84,128]{1,0:T(8,128)}, u32[]{:S(2)}, u32[]{:S(2)}) collective-permute-start(f32[84,128]{1,0:T(8,128)} %add_add_fusion), channel_id=1, source_target_pairs={{0,4},{4,0},{8,12},{12,8},{16,20},{20,16},{24,28},{28,24},{1,5},{5... | collective-permute-start | bytes 129032 | tf_op jit(solution)/shard_map/ppermute | solution.py:504
  (41 other events, 282.5 us)

commit v3 on v2

--- a/solution.py
+++ b/solution.py
@@ -777,7 +777,7 @@
     near = add_low(near_keep, jnp.concatenate([up_sent, down_sent], axis=1))
     far_cut = cut(add_low(part2, given), "wide", last)
     mixed_grad, near, layer_own, *far_cut = tie(mixed_grad, near, layer_own, *far_cut)
-    layer_far = swap(layer_own, "narrow", 2)
+    layer_far, layer_last = swap(layer_own[:-1], "narrow", 2), layer_own[-1:]
     far_sent = send_cut(far_cut, last)
     window_grad, (heads3,), sums3, _ = back_on([heads_cross], saved3, None, 0)
     given3 = swap(heads3, "narrow", 1)
@@ -805,10 +805,12 @@
     given1 = swap(heads1, "narrow", 1)
     window_grad, heads_given, *mine_sent = tie(window_grad, heads_given, *mine_sent)
     mine = add_low(mine_cut[0], *mine_sent)
-    window_grad, mine = tie(window_grad, mine)
+    window_grad, mine, layer_last = tie(window_grad, mine, layer_last)
     mine_all = exchange(mine, groups[-1])
+    layer_last = swap(layer_last, "narrow", 2)
     window_grad, (heads0,), sums0, halos = back_on([heads_own], saved0, window_grad, halo)
-    window_grad, *mine_all = tie(window_grad, *mine_all)
+    window_grad, layer_last, *mine_all = tie(window_grad, layer_last, *mine_all)
+    layer_last = [layer_last, swap(layer_last, "narrow", 1)]
     heads_cut = cut(add_low(heads0, given1, heads_given), "wide", last)
     tied = tie(window_grad, *halos, *heads_cut, *mine_all, *layer_parts)
     window_grad, *halos = tied[:3]
@@ -832,7 +834,10 @@
     heads_sent = send_cut(heads_cut, groups[-1])
     y_high, core_high = bit_of("narrow", 2), bit_of("narrow", 1)
     layer_near = join(layer_parts[0], layer_parts[1], core_high, 1)
-    layer_far = join(layer_parts[2], layer_parts[3], core_high, 1)
+    layer_far = [
+        jnp.concatenate(pair, axis=0) for pair in zip(layer_parts[2:], layer_last)
+    ]
+    layer_far = join(*layer_far, core_high, 1)
     layer_out = join(layer_near, layer_far, y_high, 1).reshape(micro, row_count, width)
     head_bias_parts = [
         jnp.concatenate([s[0, 2 * cols : 3 * cols], s[0, cols : 2 * cols]])

time: 454 us -> 447 us (0.985)
  waiting for transfers between devices: 64.8 us -> 53.5 us
    ppermute x56 -> x58, waiting for transfers between devices: 64.8 us -> 53.5 us  [swap(): return lax.ppermute(values_in, axis, [(i, i ^ bit) for i in range(size)])]
    ppermute x56 -> x58, starting transfers between devices: 63.5 us -> 66.5 us  [swap(): return lax.ppermute(values_in, axis, [(i, i ^ bit) for i in range(size)])]
  transfers between devices with their start and end apart: 58 -> 60, of which waited for: 17 -> 16; matrix products, arithmetic and copies ran while one was open for 14% -> 14% of each run, Pallas kernels for 51% -> 52%
where the time goes in v3:
time: 447 us; the launch traced here: 441 us
  Pallas kernels  229 us (51%)
  starting transfers between devices  70 us (16%)
  waiting for transfers between devices  53.5 us (12%)
  other arithmetic  47.8 us (11%)
  local copies, waits for them, and re-layouts  38.1 us (9%)
    pallas_call x4, Pallas kernels, attend_back(): pl.pallas_call(partial(attend_back_kernel, own, heads, count, first, halo...  88 us
    ppermute x58, starting transfers between devices, swap(): return lax.ppermute(values_in, axis, [(i, i ^ bit) for i in range(size)])  66.5 us
    pallas_call x4, Pallas kernels, attend(): pl.pallas_call(partial(attend_kernel, own, heads, count, first), grid_spe...  57.1 us
    ppermute x58, waiting for transfers between devices, swap(): return lax.ppermute(values_in, axis, [(i, i ^ bit) for i in range(size)])  53.5 us
    pallas_call x4, Pallas kernels, feed_part(): pl.pallas_call(partial(feed_kernel, FEED_CHUNKS, count, first), in_specs=...  51.3 us
    pallas_call x4, Pallas kernels, rows_call(): pl.pallas_call(kernel, grid_spec=pltpu.PrefetchScalarGridSpec(num_scalar_...  33.1 us
    convert_element_type x10, other arithmetic, add_low(): return total.astype(bf16)  17.7 us
  transfers between devices with their start and end apart: 60, of which 16 were waited for; matrix products, arithmetic and copies ran while one was open for 14% of the time, Pallas kernels for 52%

profile of v3, /device:TPU:0, one launch (start us, length us, event | category | flops | bytes accessed | tf_op | source)
XLA Modules:
  0.0 440.8 jit_solution(10946135180205600312)
XLA Ops:
  2.5 5.1 %collective-permute-start = (bf16[1,96,768]{2,1,0:T(8,128)(2,1)S(1)}, bf16[1,96,768]{2,1,0:T(8,128)(2,1)S(1)}, u32[]{:S(2)}, u32[]{:S(2)}) collective-permute-start(bf16[1,96,768]{2,1,0:T(8,128)(2,1)S(1)} %maximum_bitcast_fusion.2), channel_id=1, source_target_pairs={{0,24},{4,28},{8,16},{12,20},{16,8},{20,12},{24,0},{28,4},{1,25},{... | collective-permute-start | bytes 442376 | tf_op jit(solution)/shard_map/ppermute | solution.py:504
  9.8 1.7 collective-permute-start.4
  17.4 2.7 collective-permute-done.1
  23.6 8.1 %first_norm.1 = (bf16[3,768,768]{2,1,0:T(8,128)(2,1)}, bf16[3,320,768]{2,1,0:T(8,128)(2,1)}) custom-call(s32[3]{0:T(128)} %pad_add_fusion.place_ref, bf16[3,1280,768]{2,1,0:T(8,128)(2,1)} %x_ref.5, bf16[3,1280,768]{2,1,0:T(8,128)(2,1)} %c_ref.3, f32[8,768]{1,0:T(8,128)} %stack.117.vec_ref), custom_call_target="tpu_custom_call" | custom-call | flops 1024 | bytes 1024 | tf_op jit(solution)/shard_map/first_norm/pallas_call | solution.py:426
  32.0 3.1 collective-permute-done.6
  43.5 11.4 %attend.4 = (f32[3,320,768]{2,1,0:T(8,128)}, bf16[3,320,192]{2,1,0:T(8,128)(2,1)}, bf16[3,768,192]{2,1,0:T(8,128)(2,1)}, bf16[3,768,192]{2,1,0:T(8,128)(2,1)}, b...) custom-call(s32[1]{0:T(128)} %bitcast.off_ref, bf16[3,768,768]{2,1,0:T(8,128)(2,1)} %get-tuple-element.221.refs_0_, ...), custom_call_target="tpu_custom_call" | custom-call | flops 1024 | bytes 1024 | tf_op jit(solution)/shard_map/attend/pallas_call | solution.py:150
  54.9 3.2 collective-permute-done.10
  64.9 11.7 %attend.5 = (f32[3,320,768]{2,1,0:T(8,128)}, bf16[3,320,192]{2,1,0:T(8,128)(2,1)}, bf16[3,768,192]{2,1,0:T(8,128)(2,1)}, bf16[3,768,192]{2,1,0:T(8,128)(2,1)}, b...) custom-call(s32[1]{0:T(128)} %bitcast.off_ref, bf16[3,768,768]{2,1,0:T(8,128)(2,1)} %get-tuple-element.221.refs_0_, ...), custom_call_target="tpu_custom_call" | custom-call | flops 1024 | bytes 1024 | tf_op jit(solution)/shard_map/attend/pallas_call | solution.py:150
  80.4 11.7 %attend.6 = (f32[3,320,768]{2,1,0:T(8,128)}, bf16[3,320,192]{2,1,0:T(8,128)(2,1)}, bf16[3,768,192]{2,1,0:T(8,128)(2,1)}, bf16[3,768,192]{2,1,0:T(8,128)(2,1)}, b...) custom-call(s32[1]{0:T(128)} %bitcast.off_ref, bf16[3,768,768]{2,1,0:T(8,128)(2,1)} %get-tuple-element.221.refs_0_, ...), custom_call_target="tpu_custom_call" | custom-call | flops 1024 | bytes 1024 | tf_op jit(solution)/shard_map/attend/pallas_call | solution.py:150
  95.1 22.4 %attend.7 = (f32[3,320,768]{2,1,0:T(8,128)}, bf16[3,320,192]{2,1,0:T(8,128)(2,1)}, bf16[3,768,192]{2,1,0:T(8,128)(2,1)}, bf16[3,768,192]{2,1,0:T(8,128)(2,1)}, b...) custom-call(s32[1]{0:T(128)} %bitcast.off_ref, bf16[3,768,768]{2,1,0:T(8,128)(2,1)} %get-tuple-element.221.refs_0_, ...), custom_call_target="tpu_custom_call" | custom-call | flops 1024 | bytes 1024 | tf_op jit(solution)/shard_map/attend/pallas_call | solution.py:150
  117.6 6.0 %second_norm.1 = (f32[3,320,768]{2,1,0:T(8,128)}, bf16[3,320,768]{2,1,0:T(8,128)(2,1)}) custom-call(s32[3]{0:T(128)} %pad_add_fusion.place_ref, f32[3,320,768]{2,1,0:T(8,128)} %get-tuple-element.253.mixed_ref, bf16[3,1280,768]{2,1,0:T(8,128)(2,1)} %x_ref.5, f32[8,768]{1,0:T(8,128)} %stack.117.vec_ref), custom_call_target="tpu_custom_call" | custom-call | flops 1024 | bytes 1024 | tf_op jit(solution)/shard_map/second_norm/pallas_call | solution.py:426
  125.0 11.5 %feed_part.4 = (f32[960,768]{1,0:T(8,128)}, f32[960,768]{1,0:T(8,128)}, bf16[768,1536]{1,0:T(8,128)(2,1)}, f32[1,768]{1,0:T(1,128)}) custom-call(bf16[960,768]{1,0:T(8,128)(2,1)} %bitcast.147, bf16[960,768]{1,0:T(8,128)(2,1)} %bitcast.143, bf16[768,1536]{1,0:T(8,128)(2,1)} %bitcast.158, f32[1,768]{1,0:T(1,128)} %reshape.1034.refs_3_), custom_call_target="tpu_custom_call" | custom-call | flops 1024 | bytes 1024 | tf_op jit(solution)/shard_map/feed_part/pallas_call | solution.py:370
  136.4 2.5 collective-permute-done.19
  140.4 13.2 %feed_part.5 = (f32[960,768]{1,0:T(8,128)}, f32[960,768]{1,0:T(8,128)}, bf16[768,1536]{1,0:T(8,128)(2,1)}, f32[1,768]{1,0:T(1,128)}) custom-call(bf16[960,768]{1,0:T(8,128)(2,1)} %bitcast.148, bf16[960,768]{1,0:T(8,128)(2,1)} %bitcast.144, bf16[768,1536]{1,0:T(8,128)(2,1)} %collective-permute-done.18.refs_2_, ...), custom_call_target="tpu_custom_call", output_to_operand_aliasing={{0}: (4, {}), {1}: (5, {})} | custom-call | flops 1024 | bytes 1024 | tf_op jit(solution)/shard_map/feed_part/pallas_call | solution.py:370
  157.1 13.2 %feed_part.6 = (f32[960,768]{1,0:T(8,128)}, f32[960,768]{1,0:T(8,128)}, bf16[768,1536]{1,0:T(8,128)(2,1)}, f32[1,768]{1,0:T(1,128)}) custom-call(bf16[960,768]{1,0:T(8,128)(2,1)} %bitcast.149, bf16[960,768]{1,0:T(8,128)(2,1)} %bitcast.145, bf16[768,1536]{1,0:T(8,128)(2,1)} %bitcast.161, ...), custom_call_target="tpu_custom_call", output_to_operand_aliasing={{0}: (4, {}), {1}: (5, {})} | custom-call | flops 1024 | bytes 1024 | tf_op jit(solution)/shard_map/feed_part/pallas_call | solution.py:370
  170.3 3.0 add_convert_fusion.1
  177.0 13.4 %feed_part.7 = (f32[960,768]{1,0:T(8,128)}, f32[960,768]{1,0:T(8,128)}, bf16[768,1536]{1,0:T(8,128)(2,1)}, f32[1,768]{1,0:T(1,128)}) custom-call(bf16[960,768]{1,0:T(8,128)(2,1)} %bitcast.150, bf16[960,768]{1,0:T(8,128)(2,1)} %bitcast.146, bf16[768,1536]{1,0:T(8,128)(2,1)} %collective-permute-done.21.refs_2_, ...), custom_call_target="tpu_custom_call", output_to_operand_aliasing={{0}: (4, {}), {1}: (5, {})} | custom-call | flops 1024 | bytes 1024 | tf_op jit(solution)/shard_map/feed_part/pallas_call | solution.py:370
  191.8 10.7 %second_back.1 = (bf16[3,320,768]{2,1,0:T(8,128)(2,1)}, f32[3,320,768]{2,1,0:T(8,128)}, bf16[3,320,768]{2,1,0:T(8,128)(2,1)}, f32[8,768]{1,0:T(8,128)}) custom-call(s32[3]{0:T(128)} %pad_add_fusion.place_ref, f32[3,320,768]{2,1,0:T(8,128)} %bitcast.141, f32[3,320,768]{2,1,0:T(8,128)} %bitcast.142, f32[3,320,768]{2,1,0:T(8,128)} %get-tuple-element.296.m_ref, ...), custom_call_target="tpu_custom_call" | custom-call | flops 1024 | bytes 1024 | tf_op jit(solution)/shard_map/second_back/pallas_call | solution.py:426
  202.4 4.0 collective-permute-done.24
  206.4 2.5 add_convert_fusion
  215.0 21.3 %attend_back.4 = (f32[3,768,768]{2,1,0:T(8,128)}, bf16[768,768]{1,0:T(8,128)(2,1)}, f32[1,768]{1,0:T(1,128)}) custom-call(s32[1]{0:T(128)} %bitcast.off_ref, bf16[3,768,768]{2,1,0:T(8,128)(2,1)} %get-tuple-element.221.refs_0_, bf16[3,320,768]{2,1,0:T(8,128)(2,1)} %get-tuple-element.307.refs_1_, s32[3,2,2,480]{3,2,1,0:T(2,128)} %tile.10.refs_2_, ...), custom_call_target="tpu_custom_call" | custom-call | flops 1024 | bytes 1024 | tf_op jit(solution)/shard_map/attend_back/pallas_call | solution.py:285
  237.9 2.1 collective-permute-done.27
  239.9 2.9 add_convert_fusion.5
  243.5 21.9 %attend_back.5 = (f32[3,768,768]{2,1,0:T(8,128)}, bf16[768,768]{1,0:T(8,128)(2,1)}, f32[1,768]{1,0:T(1,128)}) custom-call(s32[1]{0:T(128)} %bitcast.off_ref, bf16[3,768,768]{2,1,0:T(8,128)(2,1)} %get-tuple-element.221.refs_0_, bf16[3,320,768]{2,1,0:T(8,128)(2,1)} %get-tuple-element.307.refs_1_, s32[3,2,2,480]{3,2,1,0:T(2,128)} %tile.10.refs_2_, ...), custom_call_target="tpu_custom_call" | custom-call | flops 1024 | bytes 1024 | tf_op jit(solution)/shard_map/attend_back/pallas_call | solution.py:285
  265.5 4.3 collective-permute-done.28
  280.6 8.0 %collective-permute-start.33 = (bf16[96,1536]{1,0:T(8,128)(2,1)}, bf16[96,1536]{1,0:T(8,128)(2,1)}, u32[]{:S(2)}, u32[]{:S(2)}) collective-permute-start(bf16[96,1536]{1,0:T(8,128)(2,1)} %get-tuple-element.348), channel_id=1, source_target_pairs={{0,8},{4,12},{8,0},{12,4},{16,24},{20,28},{24,16},{28,20},{1,9},{5... | collective-permute-start | bytes 884744 | tf_op jit(solution)/shard_map/ppermute | solution.py:504
  288.7 2.4 collective-permute-start.35
  291.1 22.4 %attend_back.6 = (f32[3,768,768]{2,1,0:T(8,128)}, bf16[768,768]{1,0:T(8,128)(2,1)}, f32[1,768]{1,0:T(1,128)}) custom-call(s32[1]{0:T(128)} %bitcast.off_ref, bf16[3,768,768]{2,1,0:T(8,128)(2,1)} %get-tuple-element.221.refs_0_, bf16[3,320,768]{2,1,0:T(8,128)(2,1)} %get-tuple-element.307.refs_1_, s32[3,2,2,480]{3,2,1,0:T(2,128)} %tile.10.refs_2_, ...), custom_call_target="tpu_custom_call" | custom-call | flops 1024 | bytes 1024 | tf_op jit(solution)/shard_map/attend_back/pallas_call | solution.py:285
  321.6 2.4 collective-permute-start.39
  325.6 22.4 %attend_back.7 = (f32[3,768,768]{2,1,0:T(8,128)}, bf16[768,768]{1,0:T(8,128)(2,1)}, f32[1,768]{1,0:T(1,128)}, bf16[3,208,768]{2,1,0:T(8,128)(2,1)}, bf16[3,208,768]{2,1,0:T(8,128)(2,1)}) custom-call(s32[1]{0:T(128)} %bitcast.off_ref, bf16[3,768,768]{2,1,0:T(8,128)(2,1)} %get-tuple-element.221.refs_0_, bf16[3,320,768]{2,1,0:T(8,128)(2,1)} %get-tuple-element.307.refs_1_, ...), custom_call_target="tpu_custom_call" | custom-call | flops 1024 | bytes 1024 | tf_op jit(solution)/shard_map/attend_back/pallas_call | solution.py:285
  349.0 2.4 add_convert_fusion.2
  354.2 2.2 collective-permute-start.42
  361.8 1.9 select_bitcast_fusion.3
  363.7 4.7 %collective-permute-done.44 = bf16[384,768]{1,0:T(8,128)(2,1)S(1)} collective-permute-done((bf16[384,768]{1,0:T(8,128)(2,1)S(1)}, bf16[384,768]{1,0:T(8,128)(2,1)S(1)}, u32[]{:S(2)}, u32[]{:S(2)}) %collective-permute-start.44) | collective-permute-done | bytes 589856 | tf_op jit(solution)/shard_map/ppermute | solution.py:504
  370.1 3.0 copy.63
  373.5 2.1 collective-permute-start.47
  375.6 2.2 collective-permute-start.48
  377.8 8.3 %first_back.1 = (bf16[3,320,768]{2,1,0:T(8,128)(2,1)}, f32[8,768]{1,0:T(8,128)}) custom-call(s32[3]{0:T(128)} %pad_add_fusion.place_ref, f32[3,768,768]{2,1,0:T(8,128)} %get-tuple-element.389.win_ref, bf16[3,208,768]{2,1,0:T(8,128)(2,1)} %collective-permute-done.42.left_ref, bf16[3,208,768]{2,1,0:T(8,128)(2,1)} %collective-permute-done.43.right_ref, ...), custom_call_target="tpu_custom_call" | custom-call | flops 1024 | bytes 1024 | tf_op jit(solution)/shard_map/first_back/pallas_call | solution.py:426
  387.6 7.3 %collective-permute-done.45 = bf16[384,1536]{1,0:T(8,128)(2,1)S(1)} collective-permute-done((bf16[384,1536]{1,0:T(8,128)(2,1)S(1)}, bf16[384,1536]{1,0:T(8,128)(2,1)S(1)}, u32[]{:S(2)}, u32[]{:S(2)}) %collective-permute-start.45) | collective-permute-done | bytes 1179680 | tf_op jit(solution)/shard_map/ppermute | solution.py:504
  395.7 1.8 collective-permute-start.51
  397.7 1.8 collective-permute-start.53
  400.7 2.5 collective-permute-start.54
  404.1 1.8 collective-permute-done.52
  405.8 6.1 %collective-permute-done.53 = bf16[96,768]{1,0:T(8,128)(2,1)} collective-permute-done((bf16[96,768]{1,0:T(8,128)(2,1)}, bf16[96,768]{1,0:T(8,128)(2,1)}, u32[]{:S(2)}, u32[]{:S(2)}) %collective-permute-start.53) | collective-permute-done | bytes 147488 | tf_op jit(solution)/shard_map/ppermute | solution.py:504
  412.0 2.8 collective-permute-start.56
  414.8 2.3 collective-permute-start.58
  424.3 1.8 copy.66
  426.1 8.2 %collective-permute-done.59 = f32[84,128]{1,0:T(8,128)} collective-permute-done((f32[84,128]{1,0:T(8,128)}, f32[84,128]{1,0:T(8,128)}, u32[]{:S(2)}, u32[]{:S(2)}) %collective-permute-start.59) | collective-permute-done | bytes 43040 | tf_op jit(solution)/shard_map/ppermute | solution.py:504
  (306 shorter events, 104.7 us)
Async XLA Ops:
  2.5 14.9 %collective-permute-start = (bf16[1,96,768]{2,1,0:T(8,128)(2,1)S(1)}, bf16[1,96,768]{2,1,0:T(8,128)(2,1)S(1)}, u32[]{:S(2)}, u32[]{:S(2)}) collective-permute-start(bf16[1,96,768]{2,1,0:T(8,128)(2,1)S(1)} %maximum_bitcast_fusion.2), channel_id=1, source_target_pairs={{0,24},{4,28},{8,16},{12,20},{16,8},{20,12},{24,0},{28,4},{1,25},{... | collective-permute-start | bytes 442376 | tf_op jit(solution)/shard_map/ppermute | solution.py:504
  7.7 12.5 %collective-permute-start.1 = (bf16[1,96,768]{2,1,0:T(8,128)(2,1)S(1)}, bf16[1,96,768]{2,1,0:T(8,128)(2,1)S(1)}, u32[]{:S(2)}, u32[]{:S(2)}) collective-permute-start(bf16[1,96,768]{2,1,0:T(8,128)(2,1)S(1)} %maximum_bitcast_fusion.2), channel_id=1, source_target_pairs={{0,16},{4,20},{8,24},{12,28},{16,0},{20,4},{24,8},{28,12},{1,17},{... | collective-permute-start | bytes 442376 | tf_op jit(solution)/shard_map/ppermute | solution.py:504
  7.7 12.5 %collective-permute-start.2 = (bf16[1,96,768]{2,1,0:T(8,128)(2,1)S(1)}, bf16[1,96,768]{2,1,0:T(8,128)(2,1)S(1)}, u32[]{:S(2)}, u32[]{:S(2)}) collective-permute-start(bf16[1,96,768]{2,1,0:T(8,128)(2,1)S(1)} %maximum_bitcast_fusion.2), channel_id=1, source_target_pairs={{0,8},{4,12},{8,0},{12,4},{16,24},{20,28},{24,16},{28,20},{1,9},{5... | collective-permute-start | bytes 442376 | tf_op jit(solution)/shard_map/ppermute | solution.py:504
  20.6 14.5 %collective-permute-start.6 = (bf16[4,96,768]{2,1,0:T(8,128)(2,1)S(1)}, bf16[4,96,768]{2,1,0:T(8,128)(2,1)S(1)}, u32[]{:S(2)}, u32[]{:S(2)}) collective-permute-start(bf16[4,96,768]{2,1,0:T(8,128)(2,1)S(1)} %maximum_bitcast_fusion), channel_id=1, source_target_pairs={{0,4},{4,0},{8,12},{12,8},{16,20},{20,16},{24,28},{28,24},{1,5},{5... | collective-permute-start | bytes 1769480 | tf_op jit(solution)/shard_map/ppermute | solution.py:504
  36.2 23.2 %collective-permute-start.8 = (bf16[4,96,768]{2,1,0:T(8,128)(2,1)}, bf16[4,96,768]{2,1,0:T(8,128)(2,1)S(1)}, u32[]{:S(2)}, u32[]{:S(2)}) collective-permute-start(bf16[4,96,768]{2,1,0:T(8,128)(2,1)} %bitcast.23), channel_id=1, source_target_pairs={{0,2},{1,3},{2,0},{3,1},{4,6},{5,7},{6,4},{7,5},{8,10},{9,11},{10,... | collective-permute-start | bytes 1769480 | tf_op jit(solution)/shard_map/ppermute | solution.py:504
  37.9 20.2 %collective-permute-start.10 = (bf16[1,96,1536]{2,1,0:T(8,128)(2,1)S(1)}, bf16[1,96,1536]{2,1,0:T(8,128)(2,1)S(1)}, u32[]{:S(2)}, u32[]{:S(2)}) collective-permute-start(bf16[1,96,1536]{2,1,0:T(8,128)(2,1)S(1)} %maximum_bitcast_fusion.1), channel_id=1, source_target_pairs={{0,16},{4,20},{8,24},{12,28},{16,0},{20,4},{24,8},{28,12},{1,17},{... | collective-permute-start | bytes 884744 | tf_op jit(solution)/shard_map/ppermute | solution.py:504
  38.6 19.4 %collective-permute-start.11 = (bf16[1,96,1536]{2,1,0:T(8,128)(2,1)S(1)}, bf16[1,96,1536]{2,1,0:T(8,128)(2,1)}, u32[]{:S(2)}, u32[]{:S(2)}) collective-permute-start(bf16[1,96,1536]{2,1,0:T(8,128)(2,1)S(1)} %maximum_bitcast_fusion.1), channel_id=1, source_target_pairs={{0,24},{4,28},{8,16},{12,20},{16,8},{20,12},{24,0},{28,4},{1,25},{... | collective-permute-start | bytes 884744 | tf_op jit(solution)/shard_map/ppermute | solution.py:504
  40.3 19.1 %collective-permute-start.9 = (bf16[1,96,1536]{2,1,0:T(8,128)(2,1)S(1)}, bf16[1,96,1536]{2,1,0:T(8,128)(2,1)}, u32[]{:S(2)}, u32[]{:S(2)}) collective-permute-start(bf16[1,96,1536]{2,1,0:T(8,128)(2,1)S(1)} %maximum_bitcast_fusion.1), channel_id=1, source_target_pairs={{0,8},{4,12},{8,0},{12,4},{16,24},{20,28},{24,16},{28,20},{1,9},{5... | collective-permute-start | bytes 884744 | tf_op jit(solution)/shard_map/ppermute | solution.py:504
  42.5 21.4 %collective-permute-start.7 = (bf16[768,768]{1,0:T(8,128)(2,1)S(1)}, bf16[768,768]{1,0:T(8,128)(2,1)S(1)}, u32[]{:S(2)}, u32[]{:S(2)}) collective-permute-start(bf16[768,768]{1,0:T(8,128)(2,1)S(1)} %bitcast.151), channel_id=1, source_target_pairs={{0,1},{1,0},{2,3},{3,2},{4,5},{5,4},{6,7},{7,6},{8,9},{9,8},{10,11... | collective-permute-start | bytes 3538952 | tf_op jit(solution)/shard_map/ppermute | solution.py:504
  61.8 14.8 %collective-permute-start.12 = (bf16[4,96,768]{2,1,0:T(8,128)(2,1)}, bf16[4,96,768]{2,1,0:T(8,128)(2,1)}, u32[]{:S(2)}, u32[]{:S(2)}) collective-permute-start(bf16[4,96,768]{2,1,0:T(8,128)(2,1)} %bitcast.26), channel_id=1, source_target_pairs={{0,2},{1,3},{2,0},{3,1},{4,6},{5,7},{6,4},{7,5},{8,10},{9,11},{10,... | collective-permute-start | bytes 1769480 | tf_op jit(solution)/shard_map/ppermute | solution.py:504
  62.4 14.2 %collective-permute-start.13 = (bf16[2,96,1536]{2,1,0:T(8,128)(2,1)S(1)}, bf16[2,96,1536]{2,1,0:T(8,128)(2,1)}, u32[]{:S(2)}, u32[]{:S(2)}) collective-permute-start(bf16[2,96,1536]{2,1,0:T(8,128)(2,1)S(1)} %get-tuple-element.246), channel_id=1, source_target_pairs={{0,4},{4,0},{8,12},{12,8},{16,20},{20,16},{24,28},{28,24},{1,5},{5... | collective-permute-start | bytes 1769480 | tf_op jit(solution)/shard_map/ppermute | solution.py:504
  77.9 14.2 %collective-permute-start.15 = (bf16[2,96,1536]{2,1,0:T(8,128)(2,1)S(1)}, bf16[2,96,1536]{2,1,0:T(8,128)(2,1)S(1)}, u32[]{:S(2)}, u32[]{:S(2)}) collective-permute-start(bf16[2,96,1536]{2,1,0:T(8,128)(2,1)S(1)} %get-tuple-element.252), channel_id=1, source_target_pairs={{0,4},{4,0},{8,12},{12,8},{16,20},{20,16},{24,28},{28,24},{1,5},{5... | collective-permute-start | bytes 1769480 | tf_op jit(solution)/shard_map/ppermute | solution.py:504
  78.9 13.2 %collective-permute-start.16 = (bf16[2,96,1536]{2,1,0:T(8,128)(2,1)S(1)}, bf16[2,96,1536]{2,1,0:T(8,128)(2,1)S(1)}, u32[]{:S(2)}, u32[]{:S(2)}) collective-permute-start(bf16[2,96,1536]{2,1,0:T(8,128)(2,1)S(1)} %get-tuple-element.246), channel_id=1, source_target_pairs={{0,2},{1,3},{2,0},{3,1},{4,6},{5,7},{6,4},{7,5},{8,10},{9,11},{10,... | collective-permute-start | bytes 1769480 | tf_op jit(solution)/shard_map/ppermute | solution.py:504
  80.4 14.7 %collective-permute-start.14 = (bf16[768,768]{1,0:T(8,128)(2,1)S(1)}, bf16[768,768]{1,0:T(8,128)(2,1)}, u32[]{:S(2)}, u32[]{:S(2)}) collective-permute-start(bf16[768,768]{1,0:T(8,128)(2,1)S(1)} %bitcast.154), channel_id=1, source_target_pairs={{0,1},{1,0},{2,3},{3,2},{4,5},{5,4},{6,7},{7,6},{8,9},{9,8},{10,11... | collective-permute-start | bytes 3538952 | tf_op jit(solution)/shard_map/ppermute | solution.py:504
  94.0 46.3 %collective-permute-start.18 = (bf16[768,1536]{1,0:T(8,128)(2,1)S(1)}, bf16[768,1536]{1,0:T(8,128)(2,1)}, u32[]{:S(2)}, u32[]{:S(2)}) collective-permute-start(bf16[768,1536]{1,0:T(8,128)(2,1)S(1)} %bitcast.157), channel_id=1, source_target_pairs={{0,1},{1,0},{2,3},{3,2},{4,5},{5,4},{6,7},{7,6},{8,9},{9,8},{10,11... | collective-permute-start | bytes 7077896 | tf_op jit(solution)/shard_map/ppermute | solution.py:504
  94.6 22.9 %collective-permute-start.17 = (bf16[2,96,1536]{2,1,0:T(8,128)(2,1)S(1)}, bf16[2,96,1536]{2,1,0:T(8,128)(2,1)}, u32[]{:S(2)}, u32[]{:S(2)}) collective-permute-start(bf16[2,96,1536]{2,1,0:T(8,128)(2,1)S(1)} %get-tuple-element.252), channel_id=1, source_target_pairs={{0,2},{1,3},{2,0},{3,1},{4,6},{5,7},{6,4},{7,5},{8,10},{9,11},{10,... | collective-permute-start | bytes 1769480 | tf_op jit(solution)/shard_map/ppermute | solution.py:504
  123.5 15.4 %collective-permute-start.19 = (bf16[2,96,1536]{2,1,0:T(8,128)(2,1)S(1)}, bf16[2,96,1536]{2,1,0:T(8,128)(2,1)S(1)}, u32[]{:S(2)}, u32[]{:S(2)}) collective-permute-start(bf16[2,96,1536]{2,1,0:T(8,128)(2,1)S(1)} %copy-done.10), channel_id=1, source_target_pairs={{0,4},{4,0},{8,12},{12,8},{16,20},{20,16},{24,28},{28,24},{1,5},{5... | collective-permute-start | bytes 1769480 | tf_op jit(solution)/shard_map/ppermute | solution.py:504
  138.9 14.7 %collective-permute-start.20 = (bf16[2,96,1536]{2,1,0:T(8,128)(2,1)}, bf16[2,96,1536]{2,1,0:T(8,128)(2,1)S(1)}, u32[]{:S(2)}, u32[]{:S(2)}) collective-permute-start(bf16[2,96,1536]{2,1,0:T(8,128)(2,1)} %collective-permute-done.17), channel_id=1, source_target_pairs={{0,4},{4,0},{8,12},{12,8},{16,20},{20,16},{24,28},{28,24},{1,5},{5... | collective-permute-start | bytes 1769480 | tf_op jit(solution)/shard_map/ppermute | solution.py:504
  155.7 14.6 %collective-permute-start.22 = (bf16[768,1536]{1,0:T(8,128)(2,1)}, bf16[768,1536]{1,0:T(8,128)(2,1)}, u32[]{:S(2)}, u32[]{:S(2)}) collective-permute-start(bf16[768,1536]{1,0:T(8,128)(2,1)} %get-tuple-element.282), channel_id=1, source_target_pairs={{0,1},{1,0},{2,3},{3,2},{4,5},{5,4},{6,7},{7,6},{8,9},{9,8},{10,11... | collective-permute-start | bytes 7077896 | tf_op jit(solution)/shard_map/ppermute | solution.py:504
  155.8 21.3 %collective-permute-start.21 = (bf16[768,1536]{1,0:T(8,128)(2,1)S(1)}, bf16[768,1536]{1,0:T(8,128)(2,1)}, u32[]{:S(2)}, u32[]{:S(2)}) collective-permute-start(bf16[768,1536]{1,0:T(8,128)(2,1)S(1)} %bitcast.160), channel_id=1, source_target_pairs={{0,1},{1,0},{2,3},{3,2},{4,5},{5,4},{6,7},{7,6},{8,9},{9,8},{10,11... | collective-permute-start | bytes 7077896 | tf_op jit(solution)/shard_map/ppermute | solution.py:504
  175.5 14.9 %collective-permute-start.23 = (bf16[384,768]{1,0:T(8,128)(2,1)}, bf16[384,768]{1,0:T(8,128)(2,1)S(1)}, u32[]{:S(2)}, u32[]{:S(2)}) collective-permute-start(bf16[384,768]{1,0:T(8,128)(2,1)} %get-tuple-element.291), channel_id=1, source_target_pairs={{0,4},{4,0},{8,12},{12,8},{16,20},{20,16},{24,28},{28,24},{1,5},{5... | collective-permute-start | bytes 1769480 | tf_op jit(solution)/shard_map/ppermute | solution.py:504
  190.5 16.0 %collective-permute-start.25 = (bf16[768,1536]{1,0:T(8,128)(2,1)}, bf16[768,1536]{1,0:T(8,128)(2,1)}, u32[]{:S(2)}, u32[]{:S(2)}) collective-permute-start(bf16[768,1536]{1,0:T(8,128)(2,1)} %get-tuple-element.299), channel_id=1, source_target_pairs={{0,1},{1,0},{2,3},{3,2},{4,5},{5,4},{6,7},{7,6},{8,9},{9,8},{10,11... | collective-permute-start | bytes 7077896 | tf_op jit(solution)/shard_map/ppermute | solution.py:504
  190.5 15.9 %collective-permute-start.24 = (bf16[384,768]{1,0:T(8,128)(2,1)}, bf16[384,768]{1,0:T(8,128)(2,1)S(1)}, u32[]{:S(2)}, u32[]{:S(2)}) collective-permute-start(bf16[384,768]{1,0:T(8,128)(2,1)} %get-tuple-element.298), channel_id=1, source_target_pairs={{0,4},{4,0},{8,12},{12,8},{16,20},{20,16},{24,28},{28,24},{1,5},{5... | collective-permute-start | bytes 1769480 | tf_op jit(solution)/shard_map/ppermute | solution.py:504
  212.1 27.8 %collective-permute-start.27 = (bf16[384,1536]{1,0:T(8,128)(2,1)}, bf16[384,1536]{1,0:T(8,128)(2,1)}, u32[]{:S(2)}, u32[]{:S(2)}) collective-permute-start(bf16[384,1536]{1,0:T(8,128)(2,1)} %get-tuple-element.330), channel_id=1, source_target_pairs={{0,4},{4,0},{8,12},{12,8},{16,20},{20,16},{24,28},{28,24},{1,5},{5... | collective-permute-start | bytes 3538952 | tf_op jit(solution)/shard_map/ppermute | solution.py:504
  214.5 23.3 %collective-permute-start.26 = (bf16[2,320,768]{2,1,0:T(8,128)(2,1)}, bf16[2,320,768]{2,1,0:T(8,128)(2,1)}, u32[]{:S(2)}, u32[]{:S(2)}) collective-permute-start(bf16[2,320,768]{2,1,0:T(8,128)(2,1)} %slice.168), channel_id=1, source_target_pairs={{0,2},{1,3},{2,0},{3,1},{4,6},{5,7},{6,4},{7,5},{8,10},{9,11},{10,... | collective-permute-start | bytes 2949128 | tf_op jit(solution)/shard_map/ppermute | solution.py:504
  215.0 50.5 %collective-permute-start.30 = (bf16[3,320,768]{2,1,0:T(8,128)(2,1)S(1)}, bf16[3,320,768]{2,1,0:T(8,128)(2,1)}, u32[]{:S(2)}, u32[]{:S(2)}) collective-permute-start(bf16[3,320,768]{2,1,0:T(8,128)(2,1)S(1)} %copy-done.4), channel_id=1, source_target_pairs={{0,1},{1,0},{2,3},{3,2},{4,5},{5,4},{6,7},{7,6},{8,9},{9,8},{10,11... | collective-permute-start | bytes 4423688 | tf_op jit(solution)/shard_map/ppermute | solution.py:504
  236.3 29.2 %collective-permute-start.29 = (bf16[768,768]{1,0:T(8,128)(2,1)}, bf16[768,768]{1,0:T(8,128)(2,1)}, u32[]{:S(2)}, u32[]{:S(2)}) collective-permute-start(bf16[768,768]{1,0:T(8,128)(2,1)} %get-tuple-element.338), channel_id=1, source_target_pairs={{0,1},{1,0},{2,3},{3,2},{4,5},{5,4},{6,7},{7,6},{8,9},{9,8},{10,11... | collective-permute-start | bytes 3538952 | tf_op jit(solution)/shard_map/ppermute | solution.py:504
  242.8 26.9 %collective-permute-start.28 = (bf16[384,1536]{1,0:T(8,128)(2,1)}, bf16[384,1536]{1,0:T(8,128)(2,1)}, u32[]{:S(2)}, u32[]{:S(2)}) collective-permute-start(bf16[384,1536]{1,0:T(8,128)(2,1)} %add_convert_fusion.5), channel_id=1, source_target_pairs={{0,2},{1,3},{2,0},{3,1},{4,6},{5,7},{6,4},{7,5},{8,10},{9,11},{10,... | collective-permute-start | bytes 3538952 | tf_op jit(solution)/shard_map/ppermute | solution.py:504
  243.5 21.9 %collective-permute-start.31 = (bf16[2,320,768]{2,1,0:T(8,128)(2,1)}, bf16[2,320,768]{2,1,0:T(8,128)(2,1)}, u32[]{:S(2)}, u32[]{:S(2)}) collective-permute-start(bf16[2,320,768]{2,1,0:T(8,128)(2,1)} %collective-permute-done.26), channel_id=1, source_target_pairs={{0,1},{1,0},{2,3},{3,2},{4,5},{5,4},{6,7},{7,6},{8,9},{9,8},{10,11... | collective-permute-start | bytes 2949128 | tf_op jit(solution)/shard_map/ppermute | solution.py:504
  273.9 44.4 %collective-permute-start.32 = (bf16[768,768]{1,0:T(8,128)(2,1)S(1)}, bf16[768,768]{1,0:T(8,128)(2,1)}, u32[]{:S(2)}, u32[]{:S(2)}) collective-permute-start(bf16[768,768]{1,0:T(8,128)(2,1)S(1)} %add_convert_fusion.4), channel_id=1, source_target_pairs={{0,2},{1,3},{2,0},{3,1},{4,6},{5,7},{6,4},{7,5},{8,10},{9,11},{10,... | collective-permute-start | bytes 3538952 | tf_op jit(solution)/shard_map/ppermute | solution.py:504
  280.6 37.7 %collective-permute-start.33 = (bf16[96,1536]{1,0:T(8,128)(2,1)}, bf16[96,1536]{1,0:T(8,128)(2,1)}, u32[]{:S(2)}, u32[]{:S(2)}) collective-permute-start(bf16[96,1536]{1,0:T(8,128)(2,1)} %get-tuple-element.348), channel_id=1, source_target_pairs={{0,8},{4,12},{8,0},{12,4},{16,24},{20,28},{24,16},{28,20},{1,9},{5... | collective-permute-start | bytes 884744 | tf_op jit(solution)/shard_map/ppermute | solution.py:504
  288.7 29.7 %collective-permute-start.34 = (bf16[96,1536]{1,0:T(8,128)(2,1)S(1)}, bf16[96,1536]{1,0:T(8,128)(2,1)}, u32[]{:S(2)}, u32[]{:S(2)}) collective-permute-start(bf16[96,1536]{1,0:T(8,128)(2,1)S(1)} %get-tuple-element.349), channel_id=1, source_target_pairs={{0,16},{4,20},{8,24},{12,28},{16,0},{20,4},{24,8},{28,12},{1,17},{... | collective-permute-start | bytes 884744 | tf_op jit(solution)/shard_map/ppermute | solution.py:504
  288.7 29.7 %collective-permute-start.35 = (bf16[96,1536]{1,0:T(8,128)(2,1)S(1)}, bf16[96,1536]{1,0:T(8,128)(2,1)}, u32[]{:S(2)}, u32[]{:S(2)}) collective-permute-start(bf16[96,1536]{1,0:T(8,128)(2,1)S(1)} %get-tuple-element.350), channel_id=1, source_target_pairs={{0,24},{4,28},{8,16},{12,20},{16,8},{20,12},{24,0},{28,4},{1,25},{... | collective-permute-start | bytes 884744 | tf_op jit(solution)/shard_map/ppermute | solution.py:504
  313.5 35.5 %collective-permute-start.40 = (bf16[768,768]{1,0:T(8,128)(2,1)}, bf16[768,768]{1,0:T(8,128)(2,1)}, u32[]{:S(2)}, u32[]{:S(2)}) collective-permute-start(bf16[768,768]{1,0:T(8,128)(2,1)} %get-tuple-element.364), channel_id=1, source_target_pairs={{0,1},{1,0},{2,3},{3,2},{4,5},{5,4},{6,7},{7,6},{8,9},{9,8},{10,11... | collective-permute-start | bytes 3538952 | tf_op jit(solution)/shard_map/ppermute | solution.py:504
  319.6 33.9 %collective-permute-start.37 = (bf16[96,1536]{1,0:T(8,128)(2,1)S(1)}, bf16[96,1536]{1,0:T(8,128)(2,1)S(1)}, u32[]{:S(2)}, u32[]{:S(2)}) collective-permute-start(bf16[96,1536]{1,0:T(8,128)(2,1)S(1)} %add_convert_fusion.8), channel_id=1, source_target_pairs={{0,8},{4,12},{8,0},{12,4},{16,24},{20,28},{24,16},{28,20},{1,9},{5... | collective-permute-start | bytes 884744 | tf_op jit(solution)/shard_map/ppermute | solution.py:504
  320.7 32.8 %collective-permute-start.38 = (bf16[96,1536]{1,0:T(8,128)(2,1)S(1)}, bf16[96,1536]{1,0:T(8,128)(2,1)S(1)}, u32[]{:S(2)}, u32[]{:S(2)}) collective-permute-start(bf16[96,1536]{1,0:T(8,128)(2,1)S(1)} %add_convert_fusion.8), channel_id=1, source_target_pairs={{0,16},{4,20},{8,24},{12,28},{16,0},{20,4},{24,8},{28,12},{1,17},{... | collective-permute-start | bytes 884744 | tf_op jit(solution)/shard_map/ppermute | solution.py:504
  321.6 31.9 %collective-permute-start.39 = (bf16[96,1536]{1,0:T(8,128)(2,1)S(1)}, bf16[96,1536]{1,0:T(8,128)(2,1)}, u32[]{:S(2)}, u32[]{:S(2)}) collective-permute-start(bf16[96,1536]{1,0:T(8,128)(2,1)S(1)} %add_convert_fusion.8), channel_id=1, source_target_pairs={{0,24},{4,28},{8,16},{12,20},{16,8},{20,12},{24,0},{28,4},{1,25},{... | collective-permute-start | bytes 884744 | tf_op jit(solution)/shard_map/ppermute | solution.py:504
  324.1 29.4 %collective-permute-start.36 = (bf16[1,320,768]{2,1,0:T(8,128)(2,1)}, bf16[1,320,768]{2,1,0:T(8,128)(2,1)}, u32[]{:S(2)}, u32[]{:S(2)}) collective-permute-start(bf16[1,320,768]{2,1,0:T(8,128)(2,1)} %slice.169), channel_id=1, source_target_pairs={{0,2},{1,3},{2,0},{3,1},{4,6},{5,7},{6,4},{7,5},{8,10},{9,11},{10,... | collective-permute-start | bytes 1474568 | tf_op jit(solution)/shard_map/ppermute | solution.py:504
  353.5 14.8 %collective-permute-start.44 = (bf16[384,768]{1,0:T(8,128)(2,1)S(1)}, bf16[384,768]{1,0:T(8,128)(2,1)S(1)}, u32[]{:S(2)}, u32[]{:S(2)}) collective-permute-start(bf16[384,768]{1,0:T(8,128)(2,1)S(1)} %get-tuple-element.387), channel_id=1, source_target_pairs={{0,4},{4,0},{8,12},{12,8},{16,20},{20,16},{24,28},{28,24},{1,5},{5... | collective-permute-start | bytes 1769480 | tf_op jit(solution)/shard_map/ppermute | solution.py:504
  354.2 19.1 %collective-permute-start.42 = (bf16[3,208,768]{2,1,0:T(8,128)(2,1)}, bf16[3,208,768]{2,1,0:T(8,128)(2,1)}, u32[]{:S(2)}, u32[]{:S(2)}) collective-permute-start(bf16[3,208,768]{2,1,0:T(8,128)(2,1)} %get-tuple-element.380), channel_id=1, source_target_pairs={{0,1},{1,2},{2,3},{4,5},{5,6},{6,7},{8,9},{9,10},{10,11},{12,13},{... | collective-permute-start | bytes 2875400 | tf_op jit(solution)/shard_map/ppermute | solution.py:510
  356.4 16.9 %collective-permute-start.43 = (bf16[3,208,768]{2,1,0:T(8,128)(2,1)S(1)}, bf16[3,208,768]{2,1,0:T(8,128)(2,1)}, u32[]{:S(2)}, u32[]{:S(2)}) collective-permute-start(bf16[3,208,768]{2,1,0:T(8,128)(2,1)S(1)} %copy-done.39), channel_id=1, source_target_pairs={{1,0},{2,1},{3,2},{5,4},{6,5},{7,6},{9,8},{10,9},{11,10},{13,12},{... | collective-permute-start | bytes 2875400 | tf_op jit(solution)/shard_map/ppermute | solution.py:510
  368.4 26.6 %collective-permute-start.45 = (bf16[384,1536]{1,0:T(8,128)(2,1)S(1)}, bf16[384,1536]{1,0:T(8,128)(2,1)S(1)}, u32[]{:S(2)}, u32[]{:S(2)}) collective-permute-start(bf16[384,1536]{1,0:T(8,128)(2,1)S(1)} %bitcast.164), channel_id=1, source_target_pairs={{0,4},{4,0},{8,12},{12,8},{16,20},{20,16},{24,28},{28,24},{1,5},{5... | collective-permute-start | bytes 3538952 | tf_op jit(solution)/shard_map/ppermute | solution.py:504
  373.3 14.3 %collective-permute-start.46 = (bf16[96,768]{1,0:T(8,128)(2,1)S(1)}, bf16[96,768]{1,0:T(8,128)(2,1)S(1)}, u32[]{:S(2)}, u32[]{:S(2)}) collective-permute-start(bf16[96,768]{1,0:T(8,128)(2,1)S(1)} %get-tuple-element.405), channel_id=1, source_target_pairs={{0,8},{4,12},{8,0},{12,4},{16,24},{20,28},{24,16},{28,20},{1,9},{5... | collective-permute-start | bytes 442376 | tf_op jit(solution)/shard_map/ppermute | solution.py:504
  373.5 14.1 %collective-permute-start.47 = (bf16[96,768]{1,0:T(8,128)(2,1)S(1)}, bf16[96,768]{1,0:T(8,128)(2,1)S(1)}, u32[]{:S(2)}, u32[]{:S(2)}) collective-permute-start(bf16[96,768]{1,0:T(8,128)(2,1)S(1)} %get-tuple-element.406), channel_id=1, source_target_pairs={{0,16},{4,20},{8,24},{12,28},{16,0},{20,4},{24,8},{28,12},{1,17},{... | collective-permute-start | bytes 442376 | tf_op jit(solution)/shard_map/ppermute | solution.py:504
  375.6 12.1 %collective-permute-start.48 = (bf16[96,768]{1,0:T(8,128)(2,1)S(1)}, bf16[96,768]{1,0:T(8,128)(2,1)S(1)}, u32[]{:S(2)}, u32[]{:S(2)}) collective-permute-start(bf16[96,768]{1,0:T(8,128)(2,1)S(1)} %get-tuple-element.407), channel_id=1, source_target_pairs={{0,24},{4,28},{8,16},{12,20},{16,8},{20,12},{24,0},{28,4},{1,25},{... | collective-permute-start | bytes 442376 | tf_op jit(solution)/shard_map/ppermute | solution.py:504
  397.7 14.3 %collective-permute-start.53 = (bf16[96,768]{1,0:T(8,128)(2,1)}, bf16[96,768]{1,0:T(8,128)(2,1)}, u32[]{:S(2)}, u32[]{:S(2)}) collective-permute-start(bf16[96,768]{1,0:T(8,128)(2,1)} %add_convert_fusion.9), channel_id=1, source_target_pairs={{0,16},{4,20},{8,24},{12,28},{16,0},{20,4},{24,8},{28,12},{1,17},{... | collective-permute-start | bytes 442376 | tf_op jit(solution)/shard_map/ppermute | solution.py:504
  419.2 17.9 %collective-permute-start.55 = (bf16[384,768]{1,0:T(8,128)(2,1)S(1)}, bf16[384,768]{1,0:T(8,128)(2,1)S(1)}, u32[]{:S(2)}, u32[]{:S(2)}) collective-permute-start(bf16[384,768]{1,0:T(8,128)(2,1)S(1)} %bitcast.168), channel_id=1, source_target_pairs={{0,4},{4,0},{8,12},{12,8},{16,20},{20,16},{24,28},{28,24},{1,5},{5... | collective-permute-start | bytes 1769480 | tf_op jit(solution)/shard_map/ppermute | solution.py:504
  421.4 12.9 %collective-permute-start.59 = (f32[84,128]{1,0:T(8,128)}, f32[84,128]{1,0:T(8,128)}, u32[]{:S(2)}, u32[]{:S(2)}) collective-permute-start(f32[84,128]{1,0:T(8,128)} %add_add_fusion), channel_id=1, source_target_pairs={{0,4},{4,0},{8,12},{12,8},{16,20},{20,16},{24,28},{28,24},{1,5},{5... | collective-permute-start | bytes 129032 | tf_op jit(solution)/shard_map/ppermute | solution.py:504
  (52 other events, 350.1 us)
